TPU v7x, 256 devices: a whole 4x4x8 slice. The times are simulated.
256 devices in a mesh: dp: 64 (over y, z, core), grp: 4 (over x).
Axes of the slice: x: 4, y: 4, z: 8, core: 2. Of those that a mesh axis runs over, the one named last changes fastest.
Arguments:
- vectors: bfloat16 [262144, 1024], P('dp', 'grp'), may hold values from -6 to 6
- coarse_init: float32 [1024, 1024], P(None, 'grp'), may hold values from -4 to 4
- fine_init: float32 [1024, 64, 1024], P('dp', None, 'grp'), may hold values from -4 to 4
- owner_of: int32 [262144, 1], P('dp'), may hold values from 0 to 63; in each aligned block of 4096 rows (0 to 4095, 4096 to 8191, ...) at most 128 rows name the same one
- slot_in_owner: int32 [262144], P('dp'), may hold values from 0 to 15
- fine_in_cluster: int32 [262144], P('dp'), may hold values from 0 to 63
- slot_cluster: int32 [1024], replicated, may hold values from 0 to 1023, each once
Outputs:
- coarse_out: float32 [1024, 1024], P(None, 'grp')
- fine_out: float32 [1024, 64, 1024], P('dp', None, 'grp')
- distances: float32 [64, 262144], P(None, 'dp')
Inputs may be any that keep to these rules, and one draw needn't show every extreme that they name: Among the 4096 vectors of one dp index at most 128 have the same owner_of, a bound that some block reaches of them. `slot_cluster`: each coarse cluster stands in exactly one slot.
All inputs are finite; a program needn't handle non-finite values.
Results may differ from a plain program's by a relative error of at most 0.0003.
Values may be sent and summed in bfloat16 or wider, within the bound.
No kernel may reach another device: no remote copies, remote signals or barrier semaphores. Data moves between devices by JAX's collectives and lax.ppermute only.
A program may use at most 64 MiB of HBM per device.

v0:
```python
import jax
import jax.numpy as jnp
from jax import lax
from jax.sharding import PartitionSpec as P

D = 1024
PASSES = 2


prior_weight = 2.0


def from_everyone(array, axis):
    copies = jnp.broadcast_to(array, (lax.axis_size(axis), *array.shape))
    return lax.all_to_all(copies, axis, split_axis=0, concat_axis=0, tiled=True)


def joined_along(pieces, dim):
    pieces = jnp.moveaxis(pieces, 0, dim)
    dims = pieces.shape
    return pieces.reshape(*dims[:dim], dims[dim] * dims[dim + 1], *dims[dim + 2 :])


def gathered_copies(array, axis, dim):
    pieces = from_everyone(array, axis)
    return joined_along(pieces, dim)


def cut_along(array, dim, peers):
    before, after = (array.shape[:dim], array.shape[dim + 1 :])
    return jnp.moveaxis(array.reshape(*before, peers, -1, *after), dim, 0)


def sum_at_owner(array, axis, dim):
    pieces = cut_along(array, dim, lax.axis_size(axis))
    arrived = lax.all_to_all(pieces, axis, split_axis=0, concat_axis=0, tiled=True)
    return arrived.sum(axis=0)


def label_sums(rows, labels, columns, block):
    width = rows.shape[1]
    blocks = rows.shape[0] // block

    def add_block(index, carry):
        totals, counts = carry
        start = index * block
        piece = lax.dynamic_slice_in_dim(rows, start, block, 0)
        marks = lax.dynamic_slice_in_dim(labels, start, block, 0)
        onehot = (marks[:, None] == jnp.arange(columns, dtype=jnp.int32)[None, :]).astype(
            jnp.bfloat16
        )
        totals = totals + lax.dot_general(
            onehot, piece, (((0,), (0,)), ((), ())), preferred_element_type=jnp.float32
        )
        counts = counts + jnp.sum(onehot.astype(jnp.float32), axis=0)
        return (totals, counts)

    start_state = (jnp.zeros((columns, width), jnp.float32), jnp.zeros((columns,), jnp.float32))
    return lax.fori_loop(0, blocks, add_block, start_state)


def partial_distances(rows, labels, cand_flat, slots, per_cluster, block):
    norms = jnp.sum(jnp.square(cand_flat.astype(jnp.float32)), axis=1)
    blocks = rows.shape[0] // block

    def one_block(args):
        piece, marks = args
        squares = jnp.sum(jnp.square(piece.astype(jnp.float32)), axis=1)
        cross = lax.dot_general(
            piece, cand_flat, (((1,), (1,)), ((), ())), preferred_element_type=jnp.float32
        )
        partial_value = squares[:, None] - 2.0 * cross + norms[None, :]
        partial_value = partial_value.reshape(block, slots, per_cluster)
        holder = marks // per_cluster
        pick = (holder[:, None] == jnp.arange(slots, dtype=jnp.int32)[None, :]).astype(jnp.float32)
        return jnp.sum(partial_value * pick[:, :, None], axis=1)

    result = lax.map(
        one_block, (rows.reshape(blocks, block, rows.shape[1]), labels.reshape(blocks, block))
    )
    return result.reshape(-1, per_cluster)


def shards(vectors, coarse_init, fine_init, owner_of, slot_in_owner, fine_in_cluster, slot_cluster):
    owners = lax.axis_size("dp")
    tokens = vectors.shape[0]
    width = vectors.shape[1]
    slots = fine_init.shape[0]
    per_cluster = fine_init.shape[1]
    capacity = 2 * tokens // owners
    owner = owner_of[:, 0]
    label = slot_in_owner * per_cluster + fine_in_cluster
    owner_hot = (owner[:, None] == jnp.arange(owners, dtype=jnp.int32)[None, :]).astype(jnp.int32)
    before = jnp.cumsum(owner_hot, axis=0) - owner_hot
    place = jnp.sum(before * owner_hot, axis=1)
    target = owner * capacity + place
    send_rows = jnp.zeros((owners * capacity, width), jnp.bfloat16).at[target].set(vectors)
    send_labels = jnp.full((owners * capacity,), -1, jnp.int32).at[target].set(label)
    got_rows, got_labels = (
        lax.all_to_all(
            send_rows.reshape(owners, capacity, width),
            "dp",
            split_axis=0,
            concat_axis=0,
            tiled=True,
        ),
        lax.all_to_all(
            send_labels.reshape(owners, capacity), "dp", split_axis=0, concat_axis=0, tiled=True
        ),
    )
    rows = got_rows.reshape(-1, width)
    labels = got_labels.reshape(-1)
    block = min(rows.shape[0], 1024)
    sum_f, count_f = label_sums(rows, labels, slots * per_cluster, block)
    sum_f = sum_f.reshape(slots, per_cluster, width)
    count_f = count_f.reshape(slots, per_cluster)
    mine = lax.dynamic_slice_in_dim(slot_cluster, lax.axis_index("dp") * slots, slots, 0)
    fine = fine_init
    sum_c = jnp.sum(sum_f, axis=1)
    count_c = jnp.sum(count_f, axis=1)
    coarse_mine = coarse_init[mine]
    for step in range(PASSES):
        coarse_mine = (sum_c + prior_weight * coarse_mine) / (count_c[:, None] + prior_weight)
        fine = (sum_f - count_f[:, :, None] * coarse_mine[:, None, :] + prior_weight * fine) / (
            count_f[:, :, None] + prior_weight
        )
    gathered = gathered_copies(coarse_mine, "dp", 0)
    coarse_out = jnp.zeros_like(gathered).at[slot_cluster].set(gathered)
    cand = (coarse_mine[:, None, :] + fine).astype(jnp.bfloat16).reshape(slots * per_cluster, width)
    partial_value = partial_distances(rows, labels, cand, slots, per_cluster, block)
    share = sum_at_owner(partial_value.reshape(owners, capacity, per_cluster), "grp", 2)
    returned = lax.all_to_all(share, "dp", split_axis=0, concat_axis=0, tiled=True)
    quarter = returned.shape[2]
    mine_rows = returned.reshape(-1, quarter)[target]
    distances = gathered_copies((mine_rows / D).T, "grp", 0)
    return (coarse_out, fine, distances)


def solution(mesh):
    return jax.shard_map(
        shards,
        mesh=mesh,
        in_specs=(
            P("dp", "grp"),
            P(None, "grp"),
            P("dp", None, "grp"),
            P("dp", None),
            P("dp"),
            P("dp"),
            P(),
        ),
        out_specs=(P(None, "grp"), P("dp", None, "grp"), P(None, "dp")),
        check_vma=False,
    )
```

profile of v0, /device:TPU:1, one launch (start us, length us, event | category | flops | bytes accessed | tf_op | source)
XLA Modules:
  0.0 402.3 jit_solution(5893481735370911833)
XLA Ops:
  1.6 18.4 %reduce-window.6 = s32[64,32,128]{2,1,0:T(8,128)S(1)} reduce-window(s32[64,32,128]{2,1,0:T(8,128)S(1)} %fusion.22, s32[]{:T(128)} %constant.121.clone.1), window={size=1x1x128 pad=0_0x0_0x127_0}, to_apply=%region_0.0 | reduce-window | flops 33292288 | bytes 2097156 | tf_op jit(solution)/shard_map/reduce-window
  22.4 16.1 %scatter_custom_fusion = s32[8192]{0:T(1024)} fusion(s32[4096]{0:T(1024)S(1)} %bitcast.89, s32[4096]{0:T(1024)S(1)} %multiply_add_fusion, s32[]{:T(128)} %constant.126.clone.1), kind=kCustom, calls=%fused_computation.57 | custom fusion | bytes 32772 | tf_op jit(solution)/shard_map/scatter | solution.py:98
  38.5 13.1 %all-to-all-start = ((s32[64,1,128]{2,1,0:T(1,128)}), s32[64,1,128]{2,1,0:T(1,128)S(1)}, u32[]{:S(2)}, u32[]{:S(2)}) async-start(s32[64,1,128]{2,1,0:T(1,128)} %bitcast.11), calls=%async_computation | async-start | bytes 65536 | tf_op jit(solution)/shard_map/all_to_all | solution.py:107
  51.6 20.9 %scatter_custom_fusion.1 = bf16[8192,256]{1,0:T(8,128)(2,1)} fusion(s32[4096]{0:T(1024)S(1)} %bitcast.90, bf16[4096,256]{1,0:T(8,128)(2,1)} %param.11, bf16[]{:T(256)} %constant.123.clone.1), kind=kCustom, calls=%fused_computation.31 | custom fusion | bytes 4194816 | tf_op jit(solution)/shard_map/scatter | solution.py:97
  72.5 10.7 %all-to-all-start.1 = ((bf16[64,128,256]{2,1,0:T(8,128)(2,1)}), bf16[64,128,256]{2,1,0:T(8,128)(2,1)}, u32[]{:S(2)}, u32[]{:S(2)}) async-start(bf16[64,128,256]{2,1,0:T(8,128)(2,1)} %bitcast.77), calls=%async_computation.1 | async-start | bytes 8388608 | tf_op jit(solution)/shard_map/all_to_all | solution.py:100
  85.1 93.9 %all-to-all-done.1 = bf16[64,128,256]{2,1,0:T(8,128)(2,1)} async-done(((bf16[64,128,256]{2,1,0:T(8,128)(2,1)}), bf16[64,128,256]{2,1,0:T(8,128)(2,1)}, u32[]{:S(2)}, u32[]{:S(2)}) %all-to-all-start.1) | async-done | bytes 4194336 | tf_op jit(solution)/shard_map/all_to_all | solution.py:100
  179.0 27.5 %while.29 = (s32[]{:T(128)}, f32[1024,256]{1,0:T(8,128)S(1)}, f32[1024]{0:T(1024)S(1)}, s32[8192]{0:T(1024)S(1)}, bf16[8192,256]{1,0:T(8,128)(2,1)}, /*index=5*/s32[]{:T(128)}, s32[]{:T(128)}, s32[]{:T(128)}, s32[]{:T(128)}) while((s32[]{:T(128)}, f32[1024,256]{1,0:T(8,128)S(1)}, f32[1024]{0:T(1024)S(1)}, s32[8192]{0:T(1024)S(1)}, ...), condition=%wide.region_7.8_spmd.clone, body=%wide.region_5.0_spmd.clone.sunk | while | flops 542639104 | bytes 2654366 | solution.py:59
  179.0 3.0 fusion.37
  182.5 2.9 fusion.37
  185.9 2.9 fusion.37
  189.4 2.9 fusion.37
  192.8 2.9 fusion.37
  196.2 2.9 fusion.37
  199.7 2.9 fusion.37
  203.1 2.9 fusion.37
  208.6 79.8 %while.28 = (s32[]{:T(128)}, f32[8,1024,64]{1,0,2:T(8,128)}, bf16[8,1024,256]{2,1,0:T(8,128)(2,1)}, bf16[1024,256]{1,0:T(8,128)(2,1)S(1)}, f32[1024]{0:T(1024)S(...) while((s32[]{:T(128)}, f32[8,1024,64]{1,0,2:T(8,128)}, bf16[8,1024,256]{2,1,0:T(8,128)(2,1)}, ...), condition=%wide.region_15.16_spmd, body=%wide.region_12.15_spmd.sunk | while | flops 542881792 | bytes 11436641 | solution.py:78
  208.6 1.3 multiply_reduce_fusion.5
  209.8 1.8 subtract_add_fusion.2
  212.5 6.1 %dynamic_update_slice.8 = f32[8,1024,64]{1,0,2:T(8,128)} dynamic-update-slice(f32[8,1024,64]{1,0,2:T(8,128)} %get-tuple-element.329, f32[1,1024,64]{1,0,2:T(1,128)S(1)} %copy.37, s32[]{:T(128)} %get-tuple-element.328, s32[]{:T(128)} %constant.121.clone.1..sunk, s32[]{:T(128)} %constant.121.clone.1..sunk) | dynamic-update-slice | bytes 524292 | tf_op jit(solution)/shard_map/while/body/jit(dynamic_update_index_in_dim)/dynamic_update_slice | solution.py:78
  218.6 1.3 multiply_reduce_fusion.5
  219.8 1.8 subtract_add_fusion.2
  222.5 6.1 %dynamic_update_slice.8 = f32[8,1024,64]{1,0,2:T(8,128)} dynamic-update-slice(f32[8,1024,64]{1,0,2:T(8,128)} %get-tuple-element.329, f32[1,1024,64]{1,0,2:T(1,128)S(1)} %copy.37, s32[]{:T(128)} %get-tuple-element.328, s32[]{:T(128)} %constant.121.clone.1..sunk, s32[]{:T(128)} %constant.121.clone.1..sunk) | dynamic-update-slice | bytes 524292 | tf_op jit(solution)/shard_map/while/body/jit(dynamic_update_index_in_dim)/dynamic_update_slice | solution.py:78
  228.5 1.3 multiply_reduce_fusion.5
  229.8 1.8 subtract_add_fusion.2
  232.4 6.1 %dynamic_update_slice.8 = f32[8,1024,64]{1,0,2:T(8,128)} dynamic-update-slice(f32[8,1024,64]{1,0,2:T(8,128)} %get-tuple-element.329, f32[1,1024,64]{1,0,2:T(1,128)S(1)} %copy.37, s32[]{:T(128)} %get-tuple-element.328, s32[]{:T(128)} %constant.121.clone.1..sunk, s32[]{:T(128)} %constant.121.clone.1..sunk) | dynamic-update-slice | bytes 524292 | tf_op jit(solution)/shard_map/while/body/jit(dynamic_update_index_in_dim)/dynamic_update_slice | solution.py:78
  238.5 1.3 multiply_reduce_fusion.5
  239.8 1.8 subtract_add_fusion.2
  242.4 6.1 %dynamic_update_slice.8 = f32[8,1024,64]{1,0,2:T(8,128)} dynamic-update-slice(f32[8,1024,64]{1,0,2:T(8,128)} %get-tuple-element.329, f32[1,1024,64]{1,0,2:T(1,128)S(1)} %copy.37, s32[]{:T(128)} %get-tuple-element.328, s32[]{:T(128)} %constant.121.clone.1..sunk, s32[]{:T(128)} %constant.121.clone.1..sunk) | dynamic-update-slice | bytes 524292 | tf_op jit(solution)/shard_map/while/body/jit(dynamic_update_index_in_dim)/dynamic_update_slice | solution.py:78
  249.8 1.8 subtract_add_fusion.2
  252.4 6.1 %dynamic_update_slice.8 = f32[8,1024,64]{1,0,2:T(8,128)} dynamic-update-slice(f32[8,1024,64]{1,0,2:T(8,128)} %get-tuple-element.329, f32[1,1024,64]{1,0,2:T(1,128)S(1)} %copy.37, s32[]{:T(128)} %get-tuple-element.328, s32[]{:T(128)} %constant.121.clone.1..sunk, s32[]{:T(128)} %constant.121.clone.1..sunk) | dynamic-update-slice | bytes 524292 | tf_op jit(solution)/shard_map/while/body/jit(dynamic_update_index_in_dim)/dynamic_update_slice | solution.py:78
  259.7 1.8 subtract_add_fusion.2
  262.4 6.1 %dynamic_update_slice.8 = f32[8,1024,64]{1,0,2:T(8,128)} dynamic-update-slice(f32[8,1024,64]{1,0,2:T(8,128)} %get-tuple-element.329, f32[1,1024,64]{1,0,2:T(1,128)S(1)} %copy.37, s32[]{:T(128)} %get-tuple-element.328, s32[]{:T(128)} %constant.121.clone.1..sunk, s32[]{:T(128)} %constant.121.clone.1..sunk) | dynamic-update-slice | bytes 524292 | tf_op jit(solution)/shard_map/while/body/jit(dynamic_update_index_in_dim)/dynamic_update_slice | solution.py:78
  269.7 1.8 subtract_add_fusion.2
  272.4 6.1 %dynamic_update_slice.8 = f32[8,1024,64]{1,0,2:T(8,128)} dynamic-update-slice(f32[8,1024,64]{1,0,2:T(8,128)} %get-tuple-element.329, f32[1,1024,64]{1,0,2:T(1,128)S(1)} %copy.37, s32[]{:T(128)} %get-tuple-element.328, s32[]{:T(128)} %constant.121.clone.1..sunk, s32[]{:T(128)} %constant.121.clone.1..sunk) | dynamic-update-slice | bytes 524292 | tf_op jit(solution)/shard_map/while/body/jit(dynamic_update_index_in_dim)/dynamic_update_slice | solution.py:78
  279.7 1.8 subtract_add_fusion.2
  282.3 6.1 %dynamic_update_slice.8 = f32[8,1024,64]{1,0,2:T(8,128)} dynamic-update-slice(f32[8,1024,64]{1,0,2:T(8,128)} %get-tuple-element.329, f32[1,1024,64]{1,0,2:T(1,128)S(1)} %copy.37, s32[]{:T(128)} %get-tuple-element.328, s32[]{:T(128)} %constant.121.clone.1..sunk, s32[]{:T(128)} %constant.121.clone.1..sunk) | dynamic-update-slice | bytes 524292 | tf_op jit(solution)/shard_map/while/body/jit(dynamic_update_index_in_dim)/dynamic_update_slice | solution.py:78
  288.4 1.7 reshape_reshape_reshape.3
  290.1 29.8 %all_to_all.34 = f32[4,64,128,16]{2,1,3,0:T(8,128)} all-to-all(f32[4,64,128,16]{2,1,3,0:T(8,128)S(1)} %bitcast.78), channel_id=1, replica_groups=mesh['dp'=64,'grp'=4] {'grp'}, dimensions={0} | all-to-all | bytes 4194304 | tf_op jit(solution)/shard_map/all_to_all | solution.py:36
  320.0 1.8 reduce_sum.92
  322.1 23.6 %all_to_all.35 = f32[64,128,16]{1,2,0:T(8,128)S(1)} all-to-all(f32[64,128,16]{1,2,0:T(8,128)S(1)} %copy.24), channel_id=1, replica_groups=mesh['dp'=64,'grp'=4] {'dp'}, dimensions={0} | all-to-all | bytes 1048576 | tf_op jit(solution)/shard_map/all_to_all | solution.py:132
  346.8 6.5 %all-to-all-start.2 = ((f32[64,16,256]{2,1,0:T(8,128)}), f32[64,16,256]{2,1,0:T(8,128)}, u32[]{:S(2)}, u32[]{:S(2)}) async-start(f32[64,16,256]{2,1,0:T(8,128)} %broadcast_in_dim.56), calls=%async_computation.2 | async-start | bytes 2097152 | tf_op jit(solution)/shard_map/all_to_all | solution.py:15
  353.3 2.6 copy.25
  355.9 16.3 %gather_fusion.1 = f32[4096,16]{1,0:T(8,128)} fusion(f32[8192,16]{1,0:T(8,128)} %bitcast.75, s32[4096]{0:T(1024)S(1)} %broadcast_clamp_fusion), kind=kCustom, calls=%fused_computation.1 | custom fusion | bytes 540672 | tf_op jit(solution)/shard_map/gather | solution.py:134
  372.1 1.7 multiply_bitcast_fusion
  374.4 7.3 %all-to-all-done.2 = f32[64,16,256]{2,1,0:T(8,128)} async-done(((f32[64,16,256]{2,1,0:T(8,128)}), f32[64,16,256]{2,1,0:T(8,128)}, u32[]{:S(2)}, u32[]{:S(2)}) %all-to-all-start.2) | async-done | bytes 1048608 | tf_op jit(solution)/shard_map/all_to_all | solution.py:15
  382.7 3.5 all-to-all-start.5
  386.3 6.3 %scatter_custom_fusion.2 = f32[1024,256]{1,0:T(8,128)} fusion(s32[1024]{0:T(1024)S(1)} %compare_select_fusion.1, f32[1024,256]{1,0:T(8,128)} %bitcast.16, f32[]{:T(128)} %constant.120.clone.1), kind=kCustom, calls=%fused_computation.51 | custom fusion | bytes 1049088 | tf_op jit(solution)/shard_map/scatter | solution.py:128
  392.5 8.8 %all-to-all-done.5 = f32[4,16,4096]{2,1,0:T(8,128)S(1)} async-done(((f32[4,16,4096]{2,1,0:T(8,128)}), f32[4,16,4096]{2,1,0:T(8,128)S(1)}, u32[]{:S(2)}, u32[]{:S(2)}) %all-to-all-start.5) | async-done | bytes 1048608 | tf_op jit(solution)/shard_map/all_to_all | solution.py:15
  (115 shorter events, 26.6 us)
Async XLA Ops:
  0.6 82.7 %copy-start = (f32[1024,256]{1,0:T(8,128)S(1)}, f32[1024,256]{1,0:T(8,128)}, u32[]{:S(2)}) copy-start(f32[1024,256]{1,0:T(8,128)} %param.12) | copy-start | bytes 3145732
  0.6 20.7 %copy-start.3 = (s32[4096,1]{0,1:T(1,128)S(1)}, s32[4096,1]{0,1:T(1,128)}, u32[]{:S(2)}) copy-start(s32[4096,1]{0,1:T(1,128)} %param.14) | copy-start | bytes 49156
  1.6 20.7 %copy-start.4 = (s32[4096]{0:T(1024)S(1)}, s32[4096]{0:T(1024)}, u32[]{:S(2)}) copy-start(s32[4096]{0:T(1024)} %param.16) | copy-start | bytes 49156
  1.6 20.7 %copy-start.5 = (s32[4096]{0:T(1024)S(1)}, s32[4096]{0:T(1024)}, u32[]{:S(2)}) copy-start(s32[4096]{0:T(1024)} %param.15) | copy-start | bytes 49156
  38.5 34.0 %all-to-all-start = ((s32[64,1,128]{2,1,0:T(1,128)}), s32[64,1,128]{2,1,0:T(1,128)S(1)}, u32[]{:S(2)}, u32[]{:S(2)}) async-start(s32[64,1,128]{2,1,0:T(1,128)} %bitcast.11), calls=%async_computation | async-start | bytes 65536 | tf_op jit(solution)/shard_map/all_to_all | solution.py:107
  72.5 10.7 %copy-start.6 = (s32[1024]{0:T(1024)S(1)}, s32[1024]{0:T(1024)}, u32[]{:S(2)}) copy-start(s32[1024]{0:T(1024)} %param.17) | copy-start | bytes 12292
  72.5 106.5 %all-to-all-start.1 = ((bf16[64,128,256]{2,1,0:T(8,128)(2,1)}), bf16[64,128,256]{2,1,0:T(8,128)(2,1)}, u32[]{:S(2)}, u32[]{:S(2)}) async-start(bf16[64,128,256]{2,1,0:T(8,128)(2,1)} %bitcast.77), calls=%async_computation.1 | async-start | bytes 8388608 | tf_op jit(solution)/shard_map/all_to_all | solution.py:100
  179.0 27.8 %copy-start.2 = (f32[16,64,256]{2,1,0:T(8,128)S(1)}, f32[16,64,256]{2,1,0:T(8,128)}, u32[]{:S(2)}) copy-start(f32[16,64,256]{2,1,0:T(8,128)} %param.13) | copy-start | bytes 3145732
  207.3 1.0 copy-start.1
  346.8 34.9 %all-to-all-start.2 = ((f32[64,16,256]{2,1,0:T(8,128)}), f32[64,16,256]{2,1,0:T(8,128)}, u32[]{:S(2)}, u32[]{:S(2)}) async-start(f32[64,16,256]{2,1,0:T(8,128)} %broadcast_in_dim.56), calls=%async_computation.2 | async-start | bytes 2097152 | tf_op jit(solution)/shard_map/all_to_all | solution.py:15
  382.7 18.6 %all-to-all-start.5 = ((f32[4,16,4096]{2,1,0:T(8,128)}), f32[4,16,4096]{2,1,0:T(8,128)S(1)}, u32[]{:S(2)}, u32[]{:S(2)}) async-start(f32[4,16,4096]{2,1,0:T(8,128)} %broadcast_in_dim.58), calls=%async_computation.5 | async-start | bytes 2097152 | tf_op jit(solution)/shard_map/all_to_all | solution.py:15
where the time goes:
time: 405 us; the launch traced here: 402 us
  local copies, waits for them, and re-layouts  122 us (30%)
  waiting for transfers between devices  110 us (27%)
  blocking collectives  53.4 us (13%)
  other arithmetic  44.3 us (11%)
  matrix products  37.5 us (9%)
  starting transfers between devices  33.8 us (8%)
    all_to_all x1, waiting for transfers between devices, shards(): lax.all_to_all(send_rows.reshape(owners, capacity, width), 'dp', split_ax...  93.9 us
    dynamic_update_slice x16, local copies, waits for them, and re-layouts, partial_distances(): lax.map(one_block, (rows.reshape(blocks, block, rows.shape[1]), labels.re...  50.7 us
    all_to_all x1, blocking collectives, sum_at_owner(): lax.all_to_all(pieces, axis, split_axis=0, concat_axis=0, tiled=True)  29.8 us
    all_to_all x1, blocking collectives, shards(): lax.all_to_all(share, 'dp', split_axis=0, concat_axis=0, tiled=True)  23.6 us
    dot_general x8, matrix products, add_block(): lax.dot_general(onehot, piece, (((0,), (0,)), ((), ())), preferred_elemen...  23.1 us
    scatter x1, local copies, waits for them, and re-layouts, shards(): jnp.zeros((owners * capacity, width), jnp.bfloat16).at[target].set(vectors)  20.9 us
    another operation x3, other arithmetic  19 us
    gather x1, local copies, waits for them, and re-layouts, shards(): mine_rows = returned.reshape(-1, quarter)[target]  16.3 us
  transfers between devices with their start and end apart: 4, of which 3 were waited for; matrix products, arithmetic and copies ran while one was open for 12% of the time, Pallas kernels for 0%

commit v1 on v0

v1 whole, which is shorter than its diff:
```python
import jax
import jax.numpy as jnp
from jax import lax
from jax.experimental import pallas as pl
from jax.experimental.pallas import tpu as pltpu
from jax.sharding import PartitionSpec as P

D = 1024
PASSES = 2
LANES = 128


prior_weight = 2.0

VMEM = pl.BlockSpec(memory_space=pltpu.VMEM)
SMEM = pl.BlockSpec(memory_space=pltpu.SMEM)


def call(body, out_shape, ins, flops, scratch=(), mem=60 << 20):
    return pl.pallas_call(
        body,
        out_shape=out_shape,
        in_specs=ins,
        out_specs=jax.tree.map(lambda _: VMEM, out_shape),
        scratch_shapes=list(scratch),
        compiler_params=pltpu.CompilerParams(vmem_limit_bytes=mem),
        cost_estimate=pl.CostEstimate(flops=flops, bytes_accessed=4 << 20, transcendentals=0),
    )


def exchanged(array, axis):
    return lax.all_to_all(array, axis, split_axis=0, concat_axis=0, tiled=True)


def iota(shape, dim):
    return lax.broadcasted_iota(jnp.int32, shape, dim)


def rank_body(owners, capacity, stride, per_cluster):
    def body(owner_ref, label_ref, target_ref, labels_ref):
        tokens = owner_ref.shape[1]
        step = 256
        upper = (iota((step, step), 0) < iota((step, step), 1)).astype(jnp.bfloat16)
        carry = jnp.zeros((owners, 1), jnp.float32)
        table = jnp.zeros((2 * owners, capacity), jnp.float32)
        for start in range(0, tokens, step):
            owner = owner_ref[:, start : start + step]
            label = label_ref[:, start : start + step]
            hot = (iota((owners, step), 0) == owner).astype(jnp.float32)
            hot16 = hot.astype(jnp.bfloat16)
            before = jnp.dot(hot16, upper, preferred_element_type=jnp.float32) + carry
            place = jnp.sum(hot * before, axis=0, keepdims=True).astype(jnp.int32)
            carry = carry + jnp.sum(hot, axis=1, keepdims=True)
            target_ref[:, start : start + step] = owner * stride + place
            at_place = (iota((capacity, step), 0) == place).astype(jnp.bfloat16)
            slot = (label // per_cluster).astype(jnp.float32)
            fine = (label % per_cluster).astype(jnp.float32)
            parts = jnp.concatenate([hot * (slot + 1.0), hot * fine], axis=0).astype(jnp.bfloat16)
            table = table + lax.dot_general(
                parts, at_place, (((1,), (1,)), ((), ())), preferred_element_type=jnp.float32
            )
        labels_ref[0] = table[:owners]
        labels_ref[1] = table[owners:]

    return body


def pack_body(capacity, stride, unroll):
    def body(target_ref, rows_ref, labels_ref, packed_ref, source, wide):
        tokens = rows_ref.shape[0]
        total = packed_ref.shape[0]
        wide[...] = jnp.zeros_like(wide)
        for half in range(2):
            owners = labels_ref.shape[1]
            wide[pl.ds(2 * capacity + half, owners, stride=2 * stride), :] = labels_ref[half]
            source[pl.ds(half, tokens, stride=2), :] = rows_ref[
                :, half * LANES : (half + 1) * LANES
            ].astype(jnp.float32)

        def move(index, carry):
            for offset in range(unroll):
                token = index * unroll + offset
                target = target_ref[token]
                wide[pl.ds(2 * target, 2), :] = source[pl.ds(2 * token, 2), :]
            return carry

        lax.fori_loop(0, tokens // unroll, move, 0)
        for half in range(2):
            packed_ref[:, half * LANES : (half + 1) * LANES] = wide[
                pl.ds(half, total, stride=2), :
            ].astype(jnp.bfloat16)

    return body


def sums_body(slots, per_cluster):
    def body(rows_ref, labels_ref, coarse_ref, fine_ref, coarse_out, fine_out, cand_out, norm_out,
             totals, counts):
        columns = slots * per_cluster
        blocks = labels_ref.shape[0]
        group = 4
        totals[...] = jnp.zeros_like(totals)
        counts[...] = jnp.zeros_like(counts)

        def add(index, carry):
            hots = []
            count = counts[...]
            for offset in range(group):
                marks = labels_ref[pl.ds(index * group + offset, 1), :]
                hot = (iota((columns, LANES), 0) == marks).astype(jnp.float32)
                count = count + hot
                hots.append(hot.astype(jnp.bfloat16))
            counts[...] = count
            rows = jnp.concatenate(
                [rows_ref[index * group + offset, :LANES, :] for offset in range(group)], axis=0
            )
            totals[...] += jnp.dot(
                jnp.concatenate(hots, axis=1), rows, preferred_element_type=jnp.float32
            )
            return carry

        lax.fori_loop(0, blocks // group, add, 0)
        for slot in range(slots):
            part = pl.ds(slot * per_cluster, per_cluster)
            sum_f = totals[part, :]
            count_f = jnp.sum(counts[part, :], axis=1, keepdims=True)
            sum_c = jnp.sum(sum_f, axis=0, keepdims=True)
            count_c = jnp.sum(count_f, axis=0, keepdims=True)
            coarse = coarse_ref[slot : slot + 1, :]
            fine = fine_ref[part, :]
            over_c = 1.0 / (count_c + prior_weight)
            over_f = 1.0 / (count_f + prior_weight)
            for step in range(PASSES):
                coarse = (sum_c + prior_weight * coarse) * over_c
                fine = (sum_f - count_f * coarse + prior_weight * fine) * over_f
            coarse_out[slot : slot + 1, :] = coarse
            fine_out[part, :] = fine
            cand = (coarse + fine).astype(jnp.bfloat16)
            value = cand.astype(jnp.float32)
            cand_out[part, :] = (value * -2.0).astype(jnp.bfloat16)
            norm_out[part, :] = jnp.broadcast_to(
                jnp.sum(value * value, axis=1, keepdims=True), (per_cluster, LANES)
            )

    return body


def distance_body(slots, per_cluster):
    def body(rows_ref, labels_ref, cand_ref, norm_ref, out_ref):
        blocks = labels_ref.shape[0]
        pieces = out_ref.shape[0]
        quarter = per_cluster // pieces
        group = 2

        def one(index, carry):
            rows = jnp.concatenate(
                [rows_ref[index * group + offset, :LANES, :] for offset in range(group)], axis=0
            )
            cross = lax.dot_general(
                cand_ref[...], rows, (((1,), (1,)), ((), ())), preferred_element_type=jnp.float32
            )
            for offset in range(group):
                marks = labels_ref[pl.ds(index * group + offset, 1), :]
                held = marks // per_cluster
                value = jnp.zeros((per_cluster, LANES), jnp.float32)
                for slot in range(slots):
                    part = slice(slot * per_cluster, (slot + 1) * per_cluster)
                    term = cross[part, offset * LANES : (offset + 1) * LANES] + norm_ref[part, :]
                    value = jnp.where(held == slot, term, value)
                for piece in range(pieces):
                    out_ref[piece, pl.ds(pl.multiple_of((index * group + offset) * quarter, 8), quarter), :] = value[
                        piece * quarter : (piece + 1) * quarter
                    ]
            return carry

        lax.fori_loop(0, blocks // group, one, 0)

    return body


def pick_body(stride, features):
    def body(got_ref, owner_ref, target_ref, square_ref, out_ref):
        owners, quarter, _ = got_ref.shape
        copies = out_ref.shape[0]
        tokens = owner_ref.shape[1]

        def one(index, carry):
            here = pl.ds(pl.multiple_of(index * LANES, LANES), LANES)
            owner = owner_ref[:, here]
            place = target_ref[:, here] - owner * stride
            place = jnp.broadcast_to(place, (quarter, LANES))
            owner = jnp.broadcast_to(owner, (quarter, LANES))
            value = jnp.zeros((quarter, LANES), jnp.float32)
            for number in range(owners):
                found = jnp.take_along_axis(got_ref[number], place, axis=1)
                value = jnp.where(owner == number, found, value)
            value = (value + square_ref[:, here]) * (1.0 / features)
            for copy in range(copies):
                out_ref[copy, :, here] = value
            return carry

        lax.fori_loop(0, tokens // LANES, one, 0)

    return body


def arrange_body():
    def body(cluster_ref, rows_ref, out_ref):
        def move(index, carry):
            for offset in range(8):
                row = index * 8 + offset
                out_ref[pl.ds(cluster_ref[row], 1), :] = rows_ref[pl.ds(row, 1), :]
            return carry

        lax.fori_loop(0, rows_ref.shape[0] // 8, move, 0)

    return body


def shards(vectors, coarse_init, fine_init, owner_of, slot_in_owner, fine_in_cluster, slot_cluster):
    owners = lax.axis_size("dp")
    pieces = lax.axis_size("grp")
    tokens, width = vectors.shape
    slots, per_cluster, _ = fine_init.shape
    columns = slots * per_cluster
    features = width * pieces
    capacity = 2 * tokens // owners
    stride = capacity + 8
    quarter = per_cluster // pieces
    total = owners * capacity
    f32, bf16, i32 = jnp.float32, jnp.bfloat16, jnp.int32
    shape = jax.ShapeDtypeStruct

    owner = owner_of.reshape(1, tokens)
    label = (slot_in_owner * per_cluster + fine_in_cluster).reshape(1, tokens)
    target, send_labels = call(
        rank_body(owners, capacity, stride, per_cluster),
        (shape((1, tokens), i32), shape((2, owners, capacity), f32)),
        [VMEM] * 2,
        flops=200_000_000,
    )(owner, label)
    send_rows = call(
        pack_body(capacity, stride, 16),
        shape((owners * stride, width), bf16),
        [SMEM, VMEM, VMEM],
        flops=200_000_000,
        scratch=[
            pltpu.VMEM((2 * tokens, LANES), f32),
            pltpu.VMEM((2 * owners * stride, LANES), f32),
        ],
    )(target.reshape(tokens), vectors, send_labels)
    rows = exchanged(send_rows.reshape(owners, stride, width), "dp")
    marks = rows[:, capacity, :].astype(i32)
    labels = (marks[:, :capacity] - 1) * per_cluster + marks[:, capacity:]

    squares = lax.psum(jnp.sum(jnp.square(vectors.astype(f32)), axis=1), "grp").reshape(1, tokens)
    mine = lax.dynamic_slice_in_dim(slot_cluster, lax.axis_index("dp") * slots, slots, 0)
    coarse_mine, fine, cand, norms = call(
        sums_body(slots, per_cluster),
        (
            shape((slots, width), f32),
            shape((columns, width), f32),
            shape((columns, width), bf16),
            shape((columns, LANES), f32),
        ),
        [VMEM] * 4,
        flops=2 * total * columns * width,
        scratch=[pltpu.VMEM((columns, width), f32), pltpu.VMEM((columns, LANES), f32)],
    )(rows, labels, coarse_init[mine], fine_init.reshape(columns, width))

    gathered = exchanged(jnp.broadcast_to(coarse_mine, (owners, slots, width)), "dp")

    partial = call(
        distance_body(slots, per_cluster),
        shape((pieces, owners * quarter, capacity), f32),
        [VMEM] * 4,
        flops=2 * total * columns * width,
    )(rows, labels, cand, norms)
    share = jnp.sum(exchanged(partial, "grp"), axis=0)
    returned = exchanged(share.reshape(owners, quarter, capacity), "dp")
    spread = call(
        pick_body(stride, features),
        shape((pieces, quarter, tokens), f32),
        [VMEM] * 4,
        flops=100_000_000,
    )(returned, owner, target, squares)
    distances = exchanged(spread, "grp").reshape(per_cluster, tokens)
    coarse_out = call(
        arrange_body(),
        shape((owners * slots, width), f32),
        [SMEM, VMEM],
        flops=10_000_000,
    )(slot_cluster, gathered.reshape(owners * slots, width))
    return (coarse_out, fine.reshape(slots, per_cluster, width), distances)


def solution(mesh):
    return jax.shard_map(
        shards,
        mesh=mesh,
        in_specs=(
            P("dp", "grp"),
            P(None, "grp"),
            P("dp", None, "grp"),
            P("dp", None),
            P("dp"),
            P("dp"),
            P(),
        ),
        out_specs=(P(None, "grp"), P("dp", None, "grp"), P(None, "dp")),
        check_vma=False,
    )
```

time: 405 us -> 276 us (0.68)
  local copies, waits for them, and re-layouts: 122 us -> 4.24 us
  Pallas kernels: 0 us -> 58.6 us
  other arithmetic: 44.3 us -> 6.13 us
  matrix products: 37.5 us -> 0 us
  blocking collectives: 53.4 us -> 67.4 us
  starting transfers between devices: 33.8 us -> 23.3 us
    pallas_call x0 -> x6, Pallas kernels: none -> 58.6 us  [the longest x1 15.4 us: shards(): call(distance_body(slots, per_cluster), shape((pieces, owners * quarter,...]
    dynamic_update_slice x16 -> x0, local copies, waits for them, and re-layouts: 50.7 us -> none  [partial_distances(): lax.map(one_block, (rows.reshape(blocks, block, rows.shape[1]), labels.re...]
    scatter x3 -> x0, local copies, waits for them, and re-layouts: 43.3 us -> none  [the longest x1 20.9 us: shards(): jnp.zeros((owners * capacity, width), jnp.bfloat16).at[target].set(vectors)]
    dot_general x16 -> x0, matrix products: 37.5 us -> none  [the longest x8 23.1 us: add_block(): lax.dot_general(onehot, piece, (((0,), (0,)), ((), ())), preferred_elemen...]
    another operation x3 -> x0, other arithmetic: 19 us -> none
    reduce_sum x28 -> x2, other arithmetic: 20.9 us -> 3.31 us  [the longest x1 2.69 us: shards(): share = jnp.sum(exchanged(partial, 'grp'), axis=0)]
    gather x2 -> x1, local copies, waits for them, and re-layouts: 16.8 us -> 1.17 us  [shards(): coarse_init[mine]]
    psum x0 -> x1, blocking collectives: none -> 13.4 us  [shards(): lax.psum(jnp.sum(jnp.square(vectors.astype(f32)), axis=1), 'grp')]
  transfers between devices with their start and end apart: 4 -> 3, of which waited for: 3 -> 3; matrix products, arithmetic and copies ran while one was open for 12% -> 1% of each run, Pallas kernels for 0% -> 5%
where the time goes in v1:
time: 276 us; the launch traced here: 275 us
  waiting for transfers between devices  114 us (41%)
  blocking collectives  67.4 us (24%)
  Pallas kernels  58.6 us (21%)
  starting transfers between devices  23.3 us (8%)
  other arithmetic  6.13 us (2%)
  local copies, waits for them, and re-layouts  4.24 us (2%)
    all_to_all x3, waiting for transfers between devices, exchanged(): return lax.all_to_all(array, axis, split_axis=0, concat_axis=0, tiled=True)  114 us
    all_to_all x2, blocking collectives, exchanged(): return lax.all_to_all(array, axis, split_axis=0, concat_axis=0, tiled=True)  54 us
    all_to_all x3, starting transfers between devices, exchanged(): return lax.all_to_all(array, axis, split_axis=0, concat_axis=0, tiled=True)  23.3 us
    pallas_call x1, Pallas kernels, shards(): call(distance_body(slots, per_cluster), shape((pieces, owners * quarter,...  15.4 us
    pallas_call x1, Pallas kernels, shards(): call(sums_body(slots, per_cluster), (shape((slots, width), f32), shape((c...  15 us
    psum x1, blocking collectives, shards(): lax.psum(jnp.sum(jnp.square(vectors.astype(f32)), axis=1), 'grp')  13.4 us
    pallas_call x1, Pallas kernels, shards(): call(pack_body(capacity, stride, 16), shape((owners * stride, width), bf1...  10.9 us
    pallas_call x1, Pallas kernels, shards(): call(pick_body(stride, features), shape((pieces, quarter, tokens), f32),...  8.94 us
  transfers between devices with their start and end apart: 3, of which 3 were waited for; matrix products, arithmetic and copies ran while one was open for 1% of the time, Pallas kernels for 5%

profile of v1, /device:TPU:1, one launch (start us, length us, event | category | flops | bytes accessed | tf_op | source)
XLA Modules:
  0.0 274.6 jit_solution(9636016008337651738)
XLA Ops:
  0.6 0.0 copy-start
  0.6 1.4 multiply_add_fusion
  2.1 2.4 shard_map.94
  4.5 10.9 %shard_map.95 = bf16[8704,256]{1,0:T(8,128)(2,1)} custom-call(s32[4096]{0:T(1024)} %bitcast.18, bf16[4096,256]{1,0:T(8,128)(2,1)} %rows_ref.1, f32[2,64,128]{2,1,0:T(8,128)} %get-tuple-element.10.labels_ref), custom_call_target="tpu_custom_call" | custom-call | flops 200000000 | bytes 4194304 | tf_op jit(solution)/shard_map/pallas_call | solution.py:242
  15.4 13.3 %all-to-all-start = ((bf16[64,136,256]{2,1,0:T(8,128)(2,1)}), bf16[64,136,256]{2,1,0:T(8,128)(2,1)}, u32[]{:S(2)}, u32[]{:S(2)}) async-start(bf16[64,136,256]{2,1,0:T(8,128)(2,1)} %bitcast.15), calls=%async_computation | async-start | bytes 8912896 | tf_op jit(solution)/shard_map/all_to_all | solution.py:32
  28.7 0.8 compare_select_fusion
  29.5 0.0 copy-done
  29.5 1.2 gather_fusion
  30.6 99.5 %all-to-all-done.rows_ref = bf16[64,136,256]{2,1,0:T(8,128)(2,1)} async-done(((bf16[64,136,256]{2,1,0:T(8,128)(2,1)}), bf16[64,136,256]{2,1,0:T(8,128)(2,1)}, u32[]{:S(2)}, u32[]{:S(2)}) %all-to-all-start) | async-done | bytes 4456480 | tf_op jit(solution)/shard_map/all_to_all | solution.py:32
  130.2 1.0 slice.14
  131.2 0.6 slice_add_fusion.labels_ref
  131.8 15.0 %shard_map.96 = (f32[16,256]{1,0:T(8,128)}, f32[1024,256]{1,0:T(8,128)}, bf16[1024,256]{1,0:T(8,128)(2,1)}, f32[1024,128]{1,0:T(8,128)}) custom-call(bf16[64,136,256]{2,1,0:T(8,128)(2,1)} %all-to-all-done.rows_ref, s32[64,128]{1,0:T(8,128)} %slice_add_fusion.labels_ref, f32[16,256]{1,0:T(8,128)} %gather_fusion, f32[1024,256]{1,0:T(8,128)} %bitcast.23), custom_call_target="tpu_custom_call" | custom-call | flops 4294967296 | bytes 4194304 | tf_op jit(solution)/shard_map/pallas_call | solution.py:258
  146.9 15.4 %shard_map.98 = f32[4,1024,128]{2,1,0:T(8,128)} custom-call(bf16[64,136,256]{2,1,0:T(8,128)(2,1)} %all-to-all-done.rows_ref, s32[64,128]{1,0:T(8,128)} %slice_add_fusion.labels_ref, bf16[1024,256]{1,0:T(8,128)(2,1)} %get-tuple-element.13.cand_ref, f32[1024,128]{1,0:T(8,128)} %get-tuple-element.14.norm_ref), custom_call_target="tpu_custom_call" | custom-call | flops 4294967296 | bytes 4194304 | tf_op jit(solution)/shard_map/pallas_call | solution.py:273
  162.2 0.0 copy-start.2
  162.2 30.7 %all_to_all.25 = f32[4,1024,128]{2,1,0:T(8,128)} all-to-all(f32[4,1024,128]{2,1,0:T(8,128)} %shard_map.98), channel_id=1, replica_groups=mesh['dp'=64,'grp'=4] {'grp'}, dimensions={0} | all-to-all | bytes 4194304 | tf_op jit(solution)/shard_map/all_to_all | solution.py:32
  193.0 0.0 copy-start.1
  193.0 2.7 reduce_sum.18
  195.7 23.3 %all_to_all.26.got_ref = f32[64,16,128]{2,1,0:T(8,128)} all-to-all(f32[64,16,128]{2,1,0:T(8,128)} %bitcast.17), channel_id=1, replica_groups=mesh['dp'=64,'grp'=4] {'dp'}, dimensions={0} | all-to-all | bytes 1048576 | tf_op jit(solution)/shard_map/all_to_all | solution.py:32
  219.0 0.0 copy-done.2
  219.0 1.1 broadcast_in_dim.7
  220.1 6.5 %all-to-all-start.1 = ((f32[64,16,256]{2,1,0:T(8,128)}), f32[64,16,256]{2,1,0:T(8,128)}, u32[]{:S(2)}, u32[]{:S(2)}) async-start(f32[64,16,256]{2,1,0:T(8,128)} %broadcast_in_dim.7), calls=%async_computation.1 | async-start | bytes 2097152 | tf_op jit(solution)/shard_map/all_to_all | solution.py:32
  226.6 0.0 copy-done.1
  226.6 0.6 multiply_reduce_fusion
  227.2 13.4 %psum.7.square_ref = f32[1,4096]{1,0:T(1,128)} all-reduce(f32[1,4096]{1,0:T(1,128)S(1)} %bitcast.19), channel_id=1, replica_groups=mesh['dp'=64,'grp'=4] {'grp'}, use_global_device_ids=true, to_apply=%region_2.0 | all-reduce | flops 4096 | bytes 32768 | tf_op jit(solution)/shard_map/psum | solution.py:256
  240.6 8.9 %shard_map.99 = f32[4,16,4096]{2,1,0:T(8,128)} custom-call(f32[64,16,128]{2,1,0:T(8,128)} %all_to_all.26.got_ref, s32[1,4096]{1,0:T(1,128)} %bitcast.21, s32[1,4096]{1,0:T(1,128)} %get-tuple-element.9.target_ref, f32[1,4096]{1,0:T(1,128)} %psum.7.square_ref), custom_call_target="tpu_custom_call" | custom-call | flops 100000000 | bytes 4194304 | tf_op jit(solution)/shard_map/pallas_call | solution.py:281
  249.5 5.5 %all-to-all-done.1 = f32[64,16,256]{2,1,0:T(8,128)} async-done(((f32[64,16,256]{2,1,0:T(8,128)}), f32[64,16,256]{2,1,0:T(8,128)}, u32[]{:S(2)}, u32[]{:S(2)}) %all-to-all-start.1) | async-done | bytes 1048608 | tf_op jit(solution)/shard_map/all_to_all | solution.py:32
  255.0 3.5 %all-to-all-start.4 = ((f32[4,16,4096]{2,1,0:T(8,128)}), f32[4,16,4096]{2,1,0:T(8,128)S(1)}, u32[]{:S(2)}, u32[]{:S(2)}) async-start(f32[4,16,4096]{2,1,0:T(8,128)} %shard_map.99), calls=%async_computation.4 | async-start | bytes 2097152 | tf_op jit(solution)/shard_map/all_to_all | solution.py:32
  258.5 5.9 %shard_map.97 = f32[1024,256]{1,0:T(8,128)} custom-call(s32[1024]{0:T(1024)} %cluster_ref.1, f32[1024,256]{1,0:T(8,128)} %bitcast.7.rows_ref), custom_call_target="tpu_custom_call" | custom-call | flops 10000000 | bytes 4194304 | tf_op jit(solution)/shard_map/pallas_call | solution.py:288
  264.5 9.2 %all-to-all-done.4 = f32[4,16,4096]{2,1,0:T(8,128)S(1)} async-done(((f32[4,16,4096]{2,1,0:T(8,128)}), f32[4,16,4096]{2,1,0:T(8,128)S(1)}, u32[]{:S(2)}, u32[]{:S(2)}) %all-to-all-start.4) | async-done | bytes 1048608 | tf_op jit(solution)/shard_map/all_to_all | solution.py:32
  273.6 1.0 copy.21
  (2 shorter events, 0.0 us)
Async XLA Ops:
  0.6 28.8 %copy-start = (f32[1024,256]{1,0:T(8,128)S(1)}, f32[1024,256]{1,0:T(8,128)}, u32[]{:S(2)}) copy-start(f32[1024,256]{1,0:T(8,128)} %param.8) | copy-start | bytes 3145732
  15.4 114.8 %all-to-all-start = ((bf16[64,136,256]{2,1,0:T(8,128)(2,1)}), bf16[64,136,256]{2,1,0:T(8,128)(2,1)}, u32[]{:S(2)}, u32[]{:S(2)}) async-start(bf16[64,136,256]{2,1,0:T(8,128)(2,1)} %bitcast.15), calls=%async_computation | async-start | bytes 8912896 | tf_op jit(solution)/shard_map/all_to_all | solution.py:32
  162.2 56.7 %copy-start.2 = (f32[16,256]{1,0:T(8,128)S(1)}, f32[16,256]{1,0:T(8,128)}, u32[]{:S(2)}) copy-start(f32[16,256]{1,0:T(8,128)} %get-tuple-element.11) | copy-start | bytes 49156
  193.0 33.6 %copy-start.1 = (bf16[4096,256]{1,0:T(8,128)(2,1)S(1)}, bf16[4096,256]{1,0:T(8,128)(2,1)}, u32[]{:S(2)}) copy-start(bf16[4096,256]{1,0:T(8,128)(2,1)} %rows_ref.1) | copy-start | bytes 6291460
  220.1 35.0 %all-to-all-start.1 = ((f32[64,16,256]{2,1,0:T(8,128)}), f32[64,16,256]{2,1,0:T(8,128)}, u32[]{:S(2)}, u32[]{:S(2)}) async-start(f32[64,16,256]{2,1,0:T(8,128)} %broadcast_in_dim.7), calls=%async_computation.1 | async-start | bytes 2097152 | tf_op jit(solution)/shard_map/all_to_all | solution.py:32
  255.0 18.6 %all-to-all-start.4 = ((f32[4,16,4096]{2,1,0:T(8,128)}), f32[4,16,4096]{2,1,0:T(8,128)S(1)}, u32[]{:S(2)}, u32[]{:S(2)}) async-start(f32[4,16,4096]{2,1,0:T(8,128)} %shard_map.99), calls=%async_computation.4 | async-start | bytes 2097152 | tf_op jit(solution)/shard_map/all_to_all | solution.py:32

commit v2 on v1

--- a/solution.py
+++ b/solution.py
@@ -16,7 +16,7 @@
 SMEM = pl.BlockSpec(memory_space=pltpu.SMEM)
 
 
-def call(body, out_shape, ins, flops, scratch=(), mem=60 << 20):
+def call(body, out_shape, ins, flops, scratch=(), mem=16 << 20):
     return pl.pallas_call(
         body,
         out_shape=out_shape,
@@ -36,13 +36,35 @@
     return lax.broadcasted_iota(jnp.int32, shape, dim)
 
 
+def digits(value):
+    first = value.astype(jnp.bfloat16).astype(jnp.float32)
+    rest = value - first
+    second = rest.astype(jnp.bfloat16).astype(jnp.float32)
+    return first, second, rest - second
+
+
+def coded(value):
+    top = jnp.max(value, axis=0, keepdims=True)
+    power = jnp.ceil(jnp.log2(jnp.maximum(top, 1e-30)))
+    code = jnp.minimum(jnp.round(value * jnp.exp2(16.0 - power)), 65535.0) - 32768.0
+    return code.astype(jnp.int32).astype(jnp.int16), power
+
+
+def decoded(code, scale):
+    return (code.astype(jnp.int32).astype(jnp.float32) + 32768.0) * scale
+
+
+def scale_of(power):
+    return jnp.exp2(power.astype(jnp.int32).astype(jnp.float32) - 16.0)
+
+
 def rank_body(owners, capacity, stride, per_cluster):
-    def body(owner_ref, label_ref, target_ref, labels_ref):
+    def body(owner_ref, label_ref, square_ref, target_ref, meta_ref):
         tokens = owner_ref.shape[1]
         step = 256
         upper = (iota((step, step), 0) < iota((step, step), 1)).astype(jnp.bfloat16)
         carry = jnp.zeros((owners, 1), jnp.float32)
-        table = jnp.zeros((2 * owners, capacity), jnp.float32)
+        table = jnp.zeros((5 * owners, capacity), jnp.float32)
         for start in range(0, tokens, step):
             owner = owner_ref[:, start : start + step]
             label = label_ref[:, start : start + step]
@@ -55,24 +77,27 @@
             at_place = (iota((capacity, step), 0) == place).astype(jnp.bfloat16)
             slot = (label // per_cluster).astype(jnp.float32)
             fine = (label % per_cluster).astype(jnp.float32)
-            parts = jnp.concatenate([hot * (slot + 1.0), hot * fine], axis=0).astype(jnp.bfloat16)
+            first, second, third = digits(square_ref[:, start : start + step])
+            parts = jnp.concatenate(
+                [hot * value for value in (slot + 1.0, fine, first, second, third)], axis=0
+            ).astype(jnp.bfloat16)
             table = table + lax.dot_general(
                 parts, at_place, (((1,), (1,)), ((), ())), preferred_element_type=jnp.float32
             )
-        labels_ref[0] = table[:owners]
-        labels_ref[1] = table[owners:]
+        for part in range(5):
+            meta_ref[part] = table[part * owners : (part + 1) * owners]
 
     return body
 
 
 def pack_body(capacity, stride, unroll):
-    def body(target_ref, rows_ref, labels_ref, packed_ref, source, wide):
+    def body(target_ref, rows_ref, meta_ref, packed_ref, source, wide):
         tokens = rows_ref.shape[0]
         total = packed_ref.shape[0]
         wide[...] = jnp.zeros_like(wide)
+        for part in range(5):
+            wide[pl.ds(2 * capacity + part, meta_ref.shape[1], stride=2 * stride), :] = meta_ref[part]
         for half in range(2):
-            owners = labels_ref.shape[1]
-            wide[pl.ds(2 * capacity + half, owners, stride=2 * stride), :] = labels_ref[half]
             source[pl.ds(half, tokens, stride=2), :] = rows_ref[
                 :, half * LANES : (half + 1) * LANES
             ].astype(jnp.float32)
@@ -94,19 +119,30 @@
 
 
 def sums_body(slots, per_cluster):
-    def body(rows_ref, labels_ref, coarse_ref, fine_ref, coarse_out, fine_out, cand_out, norm_out,
-             totals, counts):
+    def body(rows_ref, coarse_ref, fine_ref, coarse_out, fine_out, cand_out, norm_out,
+             held_out, square_out, totals, counts, labels):
         columns = slots * per_cluster
-        blocks = labels_ref.shape[0]
+        blocks, stride, _ = rows_ref.shape
         group = 4
         totals[...] = jnp.zeros_like(totals)
         counts[...] = jnp.zeros_like(counts)
+
+        def read(block, carry):
+            meta = rows_ref[block, LANES:stride, :].astype(jnp.float32)
+            slot, fine = meta[0:1, :LANES], meta[0:1, LANES:]
+            here = pl.ds(block, 1)
+            labels[here, :] = ((slot - 1.0) * per_cluster + fine).astype(jnp.int32)
+            held_out[here, :] = slot.astype(jnp.int32) - 1
+            square_out[here, :] = (meta[1:2, :LANES] + meta[1:2, LANES:]) + meta[2:3, :LANES]
+            return carry
+
+        lax.fori_loop(0, blocks, read, 0, unroll=4)
 
         def add(index, carry):
             hots = []
             count = counts[...]
             for offset in range(group):
-                marks = labels_ref[pl.ds(index * group + offset, 1), :]
+                marks = labels[pl.ds(index * group + offset, 1), :]
                 hot = (iota((columns, LANES), 0) == marks).astype(jnp.float32)
                 count = count + hot
                 hots.append(hot.astype(jnp.bfloat16))
@@ -146,43 +182,71 @@
 
 
 def distance_body(slots, per_cluster):
-    def body(rows_ref, labels_ref, cand_ref, norm_ref, out_ref):
-        blocks = labels_ref.shape[0]
+    def body(rows_ref, held_ref, square_ref, cand_ref, norm_ref, out_ref, powers):
+        blocks = rows_ref.shape[0]
         pieces = out_ref.shape[0]
         quarter = per_cluster // pieces
-        group = 2
+        group, pair = 4, 2
 
         def one(index, carry):
-            rows = jnp.concatenate(
-                [rows_ref[index * group + offset, :LANES, :] for offset in range(group)], axis=0
-            )
-            cross = lax.dot_general(
-                cand_ref[...], rows, (((1,), (1,)), ((), ())), preferred_element_type=jnp.float32
-            )
-            for offset in range(group):
-                marks = labels_ref[pl.ds(index * group + offset, 1), :]
-                held = marks // per_cluster
-                value = jnp.zeros((per_cluster, LANES), jnp.float32)
-                for slot in range(slots):
-                    part = slice(slot * per_cluster, (slot + 1) * per_cluster)
-                    term = cross[part, offset * LANES : (offset + 1) * LANES] + norm_ref[part, :]
-                    value = jnp.where(held == slot, term, value)
-                for piece in range(pieces):
-                    out_ref[piece, pl.ds(pl.multiple_of((index * group + offset) * quarter, 8), quarter), :] = value[
-                        piece * quarter : (piece + 1) * quarter
-                    ]
+            for first in range(0, group, pair):
+                rows = jnp.concatenate(
+                    [rows_ref[index * group + first + offset, :LANES, :] for offset in range(pair)],
+                    axis=0,
+                )
+                cross = lax.dot_general(
+                    cand_ref[...], rows, (((1,), (1,)), ((), ())),
+                    preferred_element_type=jnp.float32,
+                )
+                for offset in range(pair):
+                    block = index * group + first + offset
+                    held = held_ref[pl.ds(block, 1), :]
+                    value = jnp.zeros((per_cluster, LANES), jnp.float32)
+                    for slot in range(slots):
+                        part = slice(slot * per_cluster, (slot + 1) * per_cluster)
+                        term = cross[part, offset * LANES : (offset + 1) * LANES] + norm_ref[part, :]
+                        value = jnp.where(held == slot, term, value)
+                    value = jnp.maximum(value + square_ref[pl.ds(block, 1), :], 0.0)
+                    code, power = coded(value)
+                    powers[pl.ds(block, 1), :] = power
+                    for piece in range(pieces):
+                        out_ref[piece, pl.ds(pl.multiple_of(block * quarter, quarter), quarter), :] = (
+                            code[piece * quarter : (piece + 1) * quarter]
+                        )
             return carry
 
         lax.fori_loop(0, blocks // group, one, 0)
+        for piece in range(pieces):
+            out_ref[piece, blocks * quarter :, :] = powers[...].astype(jnp.int32).astype(jnp.int16)
+
+    return body
+
+
+def total_body():
+    def body(got_ref, out_ref, scales):
+        blocks, quarter, _ = out_ref.shape
+        pieces = got_ref.shape[0]
+        for piece in range(pieces):
+            scales[piece] = scale_of(got_ref[piece, blocks * quarter :, :])
+
+        def one(block, carry):
+            here = pl.ds(pl.multiple_of(block * quarter, quarter), quarter)
+            value = decoded(got_ref[0, here, :], scales[0, pl.ds(block, 1), :])
+            for piece in range(1, pieces):
+                value = value + decoded(got_ref[piece, here, :], scales[piece, pl.ds(block, 1), :])
+            out_ref[block] = value
+            return carry
+
+        lax.fori_loop(0, blocks, one, 0, unroll=4)
 
     return body
 
 
 def pick_body(stride, features):
-    def body(got_ref, owner_ref, target_ref, square_ref, out_ref):
+    def body(got_ref, owner_ref, target_ref, out_ref, powers):
         owners, quarter, _ = got_ref.shape
         copies = out_ref.shape[0]
-        tokens = owner_ref.shape[1]
+        groups = owner_ref.shape[1] // LANES
 
         def one(index, carry):
             here = pl.ds(pl.multiple_of(index * LANES, LANES), LANES)
@@ -194,12 +258,31 @@
             for number in range(owners):
                 found = jnp.take_along_axis(got_ref[number], place, axis=1)
                 value = jnp.where(owner == number, found, value)
-            value = (value + square_ref[:, here]) * (1.0 / features)
+            code, power = coded(value * (1.0 / features))
+            powers[pl.ds(index, 1), :] = power
             for copy in range(copies):
-                out_ref[copy, :, here] = value
-            return carry
-
-        lax.fori_loop(0, tokens // LANES, one, 0)
+                out_ref[copy, pl.ds(pl.multiple_of(index * quarter, quarter), quarter), :] = code
+            return carry
+
+        lax.fori_loop(0, groups, one, 0)
+        for copy in range(copies):
+            out_ref[copy, groups * quarter :, :] = powers[...].astype(jnp.int32).astype(jnp.int16)
+
+    return body
+
+
+def spread_body(quarter):
+    def body(got_ref, out_ref):
+        groups = out_ref.shape[1] // LANES
+        for piece in range(got_ref.shape[0]):
+            scales = scale_of(got_ref[piece, groups * quarter :, :])
+            for group in range(groups):
+                out_ref[piece * quarter : (piece + 1) * quarter, group * LANES : (group + 1) * LANES] = (
+                    decoded(
+                        got_ref[piece, group * quarter : (group + 1) * quarter, :],
+                        scales[group : group + 1],
+                    )
+                )
 
     return body
 
@@ -231,14 +314,17 @@
     f32, bf16, i32 = jnp.float32, jnp.bfloat16, jnp.int32
     shape = jax.ShapeDtypeStruct
 
+    i16 = jnp.int16
+    groups = tokens // LANES
     owner = owner_of.reshape(1, tokens)
     label = (slot_in_owner * per_cluster + fine_in_cluster).reshape(1, tokens)
-    target, send_labels = call(
+    squares = jnp.sum(jnp.square(vectors.astype(f32)), axis=1).reshape(1, tokens)
+    target, meta = call(
         rank_body(owners, capacity, stride, per_cluster),
-        (shape((1, tokens), i32), shape((2, owners, capacity), f32)),
-        [VMEM] * 2,
-        flops=200_000_000,
-    )(owner, label)
+        (shape((1, tokens), i32), shape((5, owners, capacity), f32)),
+        [VMEM] * 3,
+        flops=400_000_000,
+    )(owner, label, squares)
     send_rows = call(
         pack_body(capacity, stride, 16),
         shape((owners * stride, width), bf16),
@@ -248,49 +334,75 @@
             pltpu.VMEM((2 * tokens, LANES), f32),
             pltpu.VMEM((2 * owners * stride, LANES), f32),
         ],
-    )(target.reshape(tokens), vectors, send_labels)
+        mem=32 << 20,
+    )(target.reshape(tokens), vectors, meta)
     rows = exchanged(send_rows.reshape(owners, stride, width), "dp")
-    marks = rows[:, capacity, :].astype(i32)
-    labels = (marks[:, :capacity] - 1) * per_cluster + marks[:, capacity:]
-
-    squares = lax.psum(jnp.sum(jnp.square(vectors.astype(f32)), axis=1), "grp").reshape(1, tokens)
+    bits = [bit for bit in (8, 4, 2, 32, 16, 1) if bit < owners]
+    masks = [
+        sum(bit for place, bit in enumerate(bits) if number >> place & 1) for number in range(owners)
+    ]
+    order = jnp.bitwise_xor(jnp.array(masks, i32), lax.axis_index("dp"))
+    cluster_at = slot_cluster.reshape(owners, slots)[order].reshape(owners * slots)
     mine = lax.dynamic_slice_in_dim(slot_cluster, lax.axis_index("dp") * slots, slots, 0)
-    coarse_mine, fine, cand, norms = call(
+    coarse_mine, fine, cand, norms, held, square = call(
         sums_body(slots, per_cluster),
         (
             shape((slots, width), f32),
             shape((columns, width), f32),
             shape((columns, width), bf16),
             shape((columns, LANES), f32),
+            shape((owners, LANES), i32),
+            shape((owners, LANES), f32),
         ),
-        [VMEM] * 4,
+        [VMEM] * 3,
         flops=2 * total * columns * width,
-        scratch=[pltpu.VMEM((columns, width), f32), pltpu.VMEM((columns, LANES), f32)],
-    )(rows, labels, coarse_init[mine], fine_init.reshape(columns, width))
-
-    gathered = exchanged(jnp.broadcast_to(coarse_mine, (owners, slots, width)), "dp")
-
-    partial = call(
-        distance_body(slots, per_cluster),
-        shape((pieces, owners * quarter, capacity), f32),
-        [VMEM] * 4,
-        flops=2 * total * columns * width,
-    )(rows, labels, cand, norms)
-    share = jnp.sum(exchanged(partial, "grp"), axis=0)
-    returned = exchanged(share.reshape(owners, quarter, capacity), "dp")
+        scratch=[
+            pltpu.VMEM((columns, width), f32),
+            pltpu.VMEM((columns, LANES), f32),
+            pltpu.VMEM((owners, LANES), i32),
+        ],
+        mem=32 << 20,
+    )(rows, coarse_init[mine], fine_init.reshape(columns, width))
+
+    with jax.named_scope("centres"):
+        gathered = coarse_mine
+        for bit in bits:
+            other = lax.ppermute(gathered, "dp", [(i, i ^ bit) for i in range(owners)])
+            gathered = jnp.concatenate([gathered, other], axis=0)
+
+    with jax.named_scope("measure"):
+        partial = call(
+            distance_body(slots, per_cluster),
+            shape((pieces, owners * quarter + owners, capacity), i16),
+            [VMEM] * 5,
+            flops=2 * total * columns * width,
+            scratch=[pltpu.VMEM((owners, LANES), f32)],
+            mem=32 << 20,
+        )(rows, held, square, cand, norms)
+    share = call(
+        total_body(),
+        shape((owners, quarter, capacity), f32),
+        [VMEM],
+        flops=10_000_000,
+        scratch=[pltpu.VMEM((pieces, owners, LANES), f32)],
+    )(exchanged(partial, "grp"))
+    returned = exchanged(share, "dp")
     spread = call(
         pick_body(stride, features),
-        shape((pieces, quarter, tokens), f32),
-        [VMEM] * 4,
+        shape((pieces, groups * quarter + groups, LANES), i16),
+        [VMEM] * 3,
         flops=100_000_000,
-    )(returned, owner, target, squares)
-    distances = exchanged(spread, "grp").reshape(per_cluster, tokens)
+        scratch=[pltpu.VMEM((groups, LANES), f32)],
+    )(returned, owner, target)
+    distances = call(
+        spread_body(quarter), shape((per_cluster, tokens), f32), [VMEM], flops=10_000_000
+    )(exchanged(spread, "grp"))
     coarse_out = call(
         arrange_body(),
         shape((owners * slots, width), f32),
         [SMEM, VMEM],
         flops=10_000_000,
-    )(slot_cluster, gathered.reshape(owners * slots, width))
+    )(cluster_at, gathered)
     return (coarse_out, fine.reshape(slots, per_cluster, width), distances)
 
 

time: 276 us -> 230 us (0.83)
  blocking collectives: 67.4 us -> 0 us
  waiting for transfers between devices: 114 us -> 128 us
  starting transfers between devices: 23.3 us -> 35.2 us
  Pallas kernels: 58.6 us -> 53.2 us
  local copies, waits for them, and re-layouts: 4.24 us -> 8.13 us
  other arithmetic: 6.13 us -> 3.22 us
    all_to_all x2 -> x0, blocking collectives: 54 us -> none  [exchanged(): return lax.all_to_all(array, axis, split_axis=0, concat_axis=0, tiled=True)]
    ppermute x0 -> x6, waiting for transfers between devices: none -> 19.8 us  [shards(): other = lax.ppermute(gathered, 'dp', [(i, i ^ bit) for i in range(owners)])]
    psum x1 -> x0, blocking collectives: 13.4 us -> none  [shards(): lax.psum(jnp.sum(jnp.square(vectors.astype(f32)), axis=1), 'grp')]
    ppermute x0 -> x6, starting transfers between devices: none -> 7.6 us  [shards(): other = lax.ppermute(gathered, 'dp', [(i, i ^ bit) for i in range(owners)])]
    all_to_all x3 -> x4, waiting for transfers between devices: 114 us -> 109 us  [exchanged(): return lax.all_to_all(array, axis, split_axis=0, concat_axis=0, tiled=True)]
    unnamed x7 -> x21, local copies, waits for them, and re-layouts: 0.99 us -> 6.03 us
    all_to_all x3 -> x4, starting transfers between devices: 23.3 us -> 27.6 us  [exchanged(): return lax.all_to_all(array, axis, split_axis=0, concat_axis=0, tiled=True)]
    pallas_call x1, Pallas kernels: 10.9 us -> 7.93 us  [shards(): call(pack_body(capacity, stride, 16), shape((owners * stride, width), bf1...]
  transfers between devices with their start and end apart: 3 -> 10, of which waited for: 3 -> 7; matrix products, arithmetic and copies ran while one was open for 1% -> 2% of each run, Pallas kernels for 5% -> 7%
where the time goes in v2:
time: 230 us; the launch traced here: 229 us
  waiting for transfers between devices  128 us (56%)
  Pallas kernels  53.2 us (23%)
  starting transfers between devices  35.2 us (15%)
  local copies, waits for them, and re-layouts  8.13 us (4%)
  other arithmetic  3.22 us (1%)
    all_to_all x4, waiting for transfers between devices, exchanged(): return lax.all_to_all(array, axis, split_axis=0, concat_axis=0, tiled=True)  109 us
    all_to_all x4, starting transfers between devices, exchanged(): return lax.all_to_all(array, axis, split_axis=0, concat_axis=0, tiled=True)  27.6 us
    ppermute x6, waiting for transfers between devices, shards(): other = lax.ppermute(gathered, 'dp', [(i, i ^ bit) for i in range(owners)])  19.8 us
    pallas_call x1, Pallas kernels, shards(): call(sums_body(slots, per_cluster), (shape((slots, width), f32), shape((c...  14.6 us
    pallas_call x1, Pallas kernels, shards(): call(distance_body(slots, per_cluster), shape((pieces, owners * quarter +...  11.9 us
    pallas_call x1, Pallas kernels, shards(): call(pick_body(stride, features), shape((pieces, groups * quarter + group...  8.58 us
    pallas_call x1, Pallas kernels, shards(): call(pack_body(capacity, stride, 16), shape((owners * stride, width), bf1...  7.93 us
    ppermute x6, starting transfers between devices, shards(): other = lax.ppermute(gathered, 'dp', [(i, i ^ bit) for i in range(owners)])  7.6 us
  transfers between devices with their start and end apart: 10, of which 7 were waited for; matrix products, arithmetic and copies ran while one was open for 2% of the time, Pallas kernels for 7%

profile of v2, /device:TPU:1, one launch (start us, length us, event | category | flops | bytes accessed | tf_op | source)
XLA Modules:
  0.0 228.9 jit_solution(8407783544472716229)
XLA Ops:
  0.6 0.0 copy-start
  0.6 0.0 copy-start.2
  0.7 2.4 %multiply_reduce_fusion = f32[4096]{0:T(1024)S(1)} fusion(bf16[4096,256]{1,0:T(8,128)(2,1)} %rows_ref.1), kind=kLoop, calls=%fused_computation.2 | loop fusion | flops 3141632 | bytes 2113536 | tf_op jit(solution)/shard_map/reduce_sum | solution.py:321
  3.0 0.7 multiply_add_fusion
  3.8 0.7 copy-done.3
  4.5 2.5 %shard_map.103 = (s32[1,4096]{1,0:T(1,128)S(1)}, f32[5,64,128]{2,1,0:T(8,128)S(1)}) custom-call(s32[1,4096]{1,0:T(1,128)S(1)} %bitcast.9, s32[1,4096]{1,0:T(1,128)S(1)} %bitcast.12, f32[1,4096]{1,0:T(1,128)S(1)} %bitcast.11), custom_call_target="tpu_custom_call" | custom-call | flops 400000000 | bytes 4194304 | tf_op jit(solution)/shard_map/pallas_call | solution.py:322
  7.0 0.0 copy-done.2
  7.0 7.9 %shard_map.104 = bf16[8704,256]{1,0:T(8,128)(2,1)S(1)} custom-call(s32[4096]{0:T(1024)S(1)} %bitcast.8, bf16[4096,256]{1,0:T(8,128)(2,1)S(1)} %copy-done.2, f32[5,64,128]{2,1,0:T(8,128)S(1)} %get-tuple-element.12.meta_ref), custom_call_target="tpu_custom_call" | custom-call | flops 200000000 | bytes 4194304 | tf_op jit(solution)/shard_map/pallas_call | solution.py:328
  14.9 0.0 copy-start.1
  14.9 2.1 copy-done.1
  17.0 13.4 %all-to-all-start = ((bf16[64,136,256]{2,1,0:T(8,128)(2,1)}), bf16[64,136,256]{2,1,0:T(8,128)(2,1)}, u32[]{:S(2)}, u32[]{:S(2)}) async-start(bf16[64,136,256]{2,1,0:T(8,128)(2,1)} %bitcast.7), calls=%async_computation | async-start | bytes 8912896 | tf_op jit(solution)/shard_map/all_to_all | solution.py:32
  30.5 0.1 compare_select_fusion
  30.6 0.6 gather_fusion.1
  31.1 100.8 %all-to-all-done.rows_ref = bf16[64,136,256]{2,1,0:T(8,128)(2,1)} async-done(((bf16[64,136,256]{2,1,0:T(8,128)(2,1)}), bf16[64,136,256]{2,1,0:T(8,128)(2,1)}, u32[]{:S(2)}, u32[]{:S(2)}) %all-to-all-start) | async-done | bytes 4456480 | tf_op jit(solution)/shard_map/all_to_all | solution.py:32
  132.0 14.6 %shard_map.105 = (f32[16,256]{1,0:T(8,128)S(1)}, f32[1024,256]{1,0:T(8,128)}, bf16[1024,256]{1,0:T(8,128)(2,1)S(1)}, f32[1024,128]{1,0:T(8,128)S(1)}, s32[64,128]{1,0:T(8,128)S(1)}, /*index=5*/f32[64,128]{1,0:T(8,128)S(1)}) custom-call(bf16[64,136,256]{2,1,0:T(8,128)(2,1)} %all-to-all-done.rows_ref, f32[16,256]{1,0:T(8,128)S(1)} %gather_fusion.1, ...), custom_call_target="tpu_custom_call" | custom-call | flops 4294967296 | bytes 4194304 | tf_op jit(solution)/shard_map/pallas_call | solution.py:347
  146.5 11.9 %measure.1 = s16[4,1088,128]{2,1,0:T(8,128)(2,1)} custom-call(bf16[64,136,256]{2,1,0:T(8,128)(2,1)} %all-to-all-done.rows_ref, s32[64,128]{1,0:T(8,128)S(1)} %get-tuple-element.15.held_ref, f32[64,128]{1,0:T(8,128)S(1)} %get-tuple-element.16.square_ref, bf16[1024,256]{1,0:T(8,128)(2,1)S(1)} %get-tuple-element.17.cand_ref, ...), custom_call_target="tpu_custom_call" | custom-call | flops 4294967296 | bytes 4194304 | tf_op jit(solution)/shard_map/measure/pallas_call | solution.py:374
  158.5 4.1 %all-to-all-start.1 = ((s16[4,1088,128]{2,1,0:T(8,128)(2,1)}), s16[4,1088,128]{2,1,0:T(8,128)(2,1)S(1)}, u32[]{:S(2)}, u32[]{:S(2)}) async-start(s16[4,1088,128]{2,1,0:T(8,128)(2,1)} %measure.1), calls=%async_computation.1 | async-start | bytes 2228224 | tf_op jit(solution)/shard_map/all_to_all | solution.py:32
  162.6 2.1 collective-permute-start
  164.7 4.4 %collective-permute-done = f32[16,256]{1,0:T(8,128)S(1)} collective-permute-done((f32[16,256]{1,0:T(8,128)S(1)}, f32[16,256]{1,0:T(8,128)S(1)}, u32[]{:S(2)}, u32[]{:S(2)}) %collective-permute-start) | collective-permute-done | bytes 16416 | tf_op jit(solution)/shard_map/centres/ppermute | solution.py:370
  169.1 0.0 collective-permute-start.1
  169.1 0.6 constant_dynamic-update-slice_fusion.10
  169.7 3.7 %collective-permute-done.1 = f32[32,256]{1,0:T(8,128)S(1)} collective-permute-done((f32[32,256]{1,0:T(8,128)S(1)}, f32[32,256]{1,0:T(8,128)S(1)}, u32[]{:S(2)}, u32[]{:S(2)}) %collective-permute-start.1) | collective-permute-done | bytes 32800 | tf_op jit(solution)/shard_map/centres/ppermute | solution.py:370
  173.4 0.0 collective-permute-start.2
  173.5 0.6 constant_dynamic-update-slice_fusion.9
  174.1 3.9 %all-to-all-done.1.got_ref = s16[4,1088,128]{2,1,0:T(8,128)(2,1)S(1)} async-done(((s16[4,1088,128]{2,1,0:T(8,128)(2,1)}), s16[4,1088,128]{2,1,0:T(8,128)(2,1)S(1)}, u32[]{:S(2)}, u32[]{:S(2)}) %all-to-all-start.1) | async-done | bytes 1114144 | tf_op jit(solution)/shard_map/all_to_all | solution.py:32
  177.9 1.3 shard_map.107
  179.2 6.6 %all-to-all-start.2 = ((f32[64,16,128]{2,1,0:T(8,128)}), f32[64,16,128]{2,1,0:T(8,128)S(1)}, u32[]{:S(2)}, u32[]{:S(2)}) async-start(f32[64,16,128]{2,1,0:T(8,128)} %shard_map.107), calls=%async_computation.2 | async-start | bytes 1048576 | tf_op jit(solution)/shard_map/all_to_all | solution.py:32
  185.8 0.0 collective-permute-done.2
  185.8 3.0 %collective-permute-start.3 = (f32[128,256]{1,0:T(8,128)S(1)}, f32[128,256]{1,0:T(8,128)S(1)}, u32[]{:S(2)}, u32[]{:S(2)}) collective-permute-start(f32[128,256]{1,0:T(8,128)S(1)} %pad_maximum_fusion), channel_id=1, source_target_pairs={{0,128},{4,132},{8,136},{12,140},{16,144},{20,148},{24,152},{28,15... | collective-permute-start | bytes 393224 | tf_op jit(solution)/shard_map/centres/ppermute | solution.py:370
  188.9 0.6 constant_dynamic-update-slice_fusion.8
  189.5 0.7 constant_dynamic-update-slice_fusion.7
  190.2 3.3 %collective-permute-done.3 = f32[128,256]{1,0:T(8,128)S(1)} collective-permute-done((f32[128,256]{1,0:T(8,128)S(1)}, f32[128,256]{1,0:T(8,128)S(1)}, u32[]{:S(2)}, u32[]{:S(2)}) %collective-permute-start.3) | collective-permute-done | bytes 131104 | tf_op jit(solution)/shard_map/centres/ppermute | solution.py:370
  193.4 0.7 constant_dynamic-update-slice_fusion.6
  194.2 0.8 collective-permute-start.4
  194.9 8.4 %collective-permute-done.4 = f32[256,256]{1,0:T(8,128)S(1)} collective-permute-done((f32[256,256]{1,0:T(8,128)}, f32[256,256]{1,0:T(8,128)S(1)}, u32[]{:S(2)}, u32[]{:S(2)}) %collective-permute-start.4) | collective-permute-done | bytes 262176 | tf_op jit(solution)/shard_map/centres/ppermute | solution.py:370
  203.4 0.7 constant_dynamic-update-slice_fusion.5
  204.1 1.7 collective-permute-start.5
  205.8 0.1 reshape.33
  205.9 0.0 all-to-all-done.2.got_ref
  205.9 0.0 copy-done.4
  205.9 8.6 %shard_map.108 = s16[4,544,128]{2,1,0:T(8,128)(2,1)} custom-call(f32[64,16,128]{2,1,0:T(8,128)S(1)} %all-to-all-done.2.got_ref, s32[1,4096]{1,0:T(1,128)S(1)} %bitcast.10, s32[1,4096]{1,0:T(1,128)S(1)} %get-tuple-element.11.target_ref), custom_call_target="tpu_custom_call" | custom-call | flops 100000000 | bytes 4194304 | tf_op jit(solution)/shard_map/pallas_call | solution.py:390
  214.4 3.5 %all-to-all-start.3 = ((s16[4,544,128]{2,1,0:T(8,128)(2,1)}), s16[4,544,128]{2,1,0:T(8,128)(2,1)S(1)}, u32[]{:S(2)}, u32[]{:S(2)}) async-start(s16[4,544,128]{2,1,0:T(8,128)(2,1)} %shard_map.108), calls=%async_computation.3 | async-start | bytes 1114112 | tf_op jit(solution)/shard_map/all_to_all | solution.py:32
  218.0 0.6 gather_fusion
  218.6 0.1 reshape.34.cluster_ref
  218.6 0.0 collective-permute-done.5
  218.7 5.3 %shard_map.106 = f32[1024,256]{1,0:T(8,128)} custom-call(s32[1024]{0:T(1024)S(1)} %reshape.34.cluster_ref, f32[1024,256]{1,0:T(8,128)S(1)} %constant_dynamic-update-slice_fusion.11.rows_ref), custom_call_target="tpu_custom_call" | custom-call | flops 10000000 | bytes 4194304 | tf_op jit(solution)/shard_map/pallas_call | solution.py:400
  224.0 3.9 %all-to-all-done.3.got_ref = s16[4,544,128]{2,1,0:T(8,128)(2,1)S(1)} async-done(((s16[4,544,128]{2,1,0:T(8,128)(2,1)}), s16[4,544,128]{2,1,0:T(8,128)(2,1)S(1)}, u32[]{:S(2)}, u32[]{:S(2)}) %all-to-all-start.3) | async-done | bytes 557088 | tf_op jit(solution)/shard_map/all_to_all | solution.py:32
  227.8 1.1 shard_map.109
  (16 shorter events, 0.1 us)
Async XLA Ops:
  0.6 29.9 %copy-start = (f32[1024,256]{1,0:T(8,128)S(1)}, f32[1024,256]{1,0:T(8,128)}, u32[]{:S(2)}) copy-start(f32[1024,256]{1,0:T(8,128)} %param.9) | copy-start | bytes 3145732
  0.6 6.3 %copy-start.2 = (bf16[4096,256]{1,0:T(8,128)(2,1)S(1)}, bf16[4096,256]{1,0:T(8,128)(2,1)}, u32[]{:S(2)}) copy-start(bf16[4096,256]{1,0:T(8,128)(2,1)} %rows_ref.1) | copy-start | bytes 6291460
  3.8 0.7 copy-start.3
  14.9 2.1 copy-start.1
  17.0 13.5 %copy-start.6 = (s32[1024]{0:T(1024)S(1)}, s32[1024]{0:T(1024)}, u32[]{:S(2)}) copy-start(s32[1024]{0:T(1024)} %param.14) | copy-start | bytes 12292
  17.0 114.9 %copy-start.5 = (f32[16,64,256]{2,1,0:T(8,128)S(1)}, f32[16,64,256]{2,1,0:T(8,128)}, u32[]{:S(2)}) copy-start(f32[16,64,256]{2,1,0:T(8,128)} %param.10) | copy-start | bytes 3145732
  17.0 114.9 %all-to-all-start = ((bf16[64,136,256]{2,1,0:T(8,128)(2,1)}), bf16[64,136,256]{2,1,0:T(8,128)(2,1)}, u32[]{:S(2)}, u32[]{:S(2)}) async-start(bf16[64,136,256]{2,1,0:T(8,128)(2,1)} %bitcast.7), calls=%async_computation | async-start | bytes 8912896 | tf_op jit(solution)/shard_map/all_to_all | solution.py:32
  158.5 47.4 %copy-start.4 = (s32[4096,1]{0,1:T(1,128)S(1)}, s32[4096,1]{0,1:T(1,128)}, u32[]{:S(2)}) copy-start(s32[4096,1]{0,1:T(1,128)} %param.11) | copy-start | bytes 49156
  158.5 19.5 %all-to-all-start.1 = ((s16[4,1088,128]{2,1,0:T(8,128)(2,1)}), s16[4,1088,128]{2,1,0:T(8,128)(2,1)S(1)}, u32[]{:S(2)}, u32[]{:S(2)}) async-start(s16[4,1088,128]{2,1,0:T(8,128)(2,1)} %measure.1), calls=%async_computation.1 | async-start | bytes 2228224 | tf_op jit(solution)/shard_map/all_to_all | solution.py:32
  162.6 55.3 %copy-start.7 = (s32[64]{0:T(128)S(1)}, s32[64]{0:T(128)}, u32[]{:S(2)}) copy-start(s32[64]{0:T(128)} %constant.6.clone) | copy-start | bytes 772
  162.6 6.5 %collective-permute-start = (f32[16,256]{1,0:T(8,128)S(1)}, f32[16,256]{1,0:T(8,128)S(1)}, u32[]{:S(2)}, u32[]{:S(2)}) collective-permute-start(f32[16,256]{1,0:T(8,128)S(1)} %get-tuple-element.13), channel_id=1, source_target_pairs={{0,32},{4,36},{8,40},{12,44},{16,48},{20,52},{24,56},{28,60},{32,0... | collective-permute-start | bytes 49160 | tf_op jit(solution)/shard_map/centres/ppermute | solution.py:370
  169.1 4.3 %collective-permute-start.1 = (f32[32,256]{1,0:T(8,128)S(1)}, f32[32,256]{1,0:T(8,128)S(1)}, u32[]{:S(2)}, u32[]{:S(2)}) collective-permute-start(f32[32,256]{1,0:T(8,128)S(1)} %pad_maximum_fusion.2), channel_id=1, source_target_pairs={{0,16},{4,20},{8,24},{12,28},{16,0},{20,4},{24,8},{28,12},{32,48},... | collective-permute-start | bytes 98312 | tf_op jit(solution)/shard_map/centres/ppermute | solution.py:370
  173.4 12.4 %collective-permute-start.2 = (f32[64,256]{1,0:T(8,128)S(1)}, f32[64,256]{1,0:T(8,128)S(1)}, u32[]{:S(2)}, u32[]{:S(2)}) collective-permute-start(f32[64,256]{1,0:T(8,128)S(1)} %pad_maximum_fusion.1), channel_id=1, source_target_pairs={{0,8},{4,12},{8,0},{12,4},{16,24},{20,28},{24,16},{28,20},{32,40},... | collective-permute-start | bytes 196616 | tf_op jit(solution)/shard_map/centres/ppermute | solution.py:370
  179.2 26.6 %all-to-all-start.2 = ((f32[64,16,128]{2,1,0:T(8,128)}), f32[64,16,128]{2,1,0:T(8,128)S(1)}, u32[]{:S(2)}, u32[]{:S(2)}) async-start(f32[64,16,128]{2,1,0:T(8,128)} %shard_map.107), calls=%async_computation.2 | async-start | bytes 1048576 | tf_op jit(solution)/shard_map/all_to_all | solution.py:32
  185.8 7.6 %collective-permute-start.3 = (f32[128,256]{1,0:T(8,128)S(1)}, f32[128,256]{1,0:T(8,128)S(1)}, u32[]{:S(2)}, u32[]{:S(2)}) collective-permute-start(f32[128,256]{1,0:T(8,128)S(1)} %pad_maximum_fusion), channel_id=1, source_target_pairs={{0,128},{4,132},{8,136},{12,140},{16,144},{20,148},{24,152},{28,15... | collective-permute-start | bytes 393224 | tf_op jit(solution)/shard_map/centres/ppermute | solution.py:370
  194.2 9.2 %collective-permute-start.4 = (f32[256,256]{1,0:T(8,128)}, f32[256,256]{1,0:T(8,128)S(1)}, u32[]{:S(2)}, u32[]{:S(2)}) collective-permute-start(f32[256,256]{1,0:T(8,128)} %get-tuple-element.23), channel_id=1, source_target_pairs={{0,64},{4,68},{8,72},{12,76},{16,80},{20,84},{24,88},{28,92},{32,9... | collective-permute-start | bytes 786440 | tf_op jit(solution)/shard_map/centres/ppermute | solution.py:370
  204.1 14.5 %collective-permute-start.5 = (f32[512,256]{1,0:T(8,128)}, f32[512,256]{1,0:T(8,128)S(1)}, u32[]{:S(2)}, u32[]{:S(2)}) collective-permute-start(f32[512,256]{1,0:T(8,128)} %get-tuple-element.19), channel_id=1, source_target_pairs={{0,4},{4,0},{8,12},{12,8},{16,20},{20,16},{24,28},{28,24},{32,36},... | collective-permute-start | bytes 1572872 | tf_op jit(solution)/shard_map/centres/ppermute | solution.py:370
  214.4 13.4 %all-to-all-start.3 = ((s16[4,544,128]{2,1,0:T(8,128)(2,1)}), s16[4,544,128]{2,1,0:T(8,128)(2,1)S(1)}, u32[]{:S(2)}, u32[]{:S(2)}) async-start(s16[4,544,128]{2,1,0:T(8,128)(2,1)} %shard_map.108), calls=%async_computation.3 | async-start | bytes 1114112 | tf_op jit(solution)/shard_map/all_to_all | solution.py:32

commit v3 on v2

--- a/solution.py
+++ b/solution.py
@@ -5,7 +5,7 @@
 from jax.experimental.pallas import tpu as pltpu
 from jax.sharding import PartitionSpec as P
 
-D = 1024
+
 PASSES = 2
 LANES = 128
 
@@ -58,8 +58,8 @@
     return jnp.exp2(power.astype(jnp.int32).astype(jnp.float32) - 16.0)
 
 
-def rank_body(owners, capacity, stride, per_cluster):
-    def body(owner_ref, label_ref, square_ref, target_ref, meta_ref):
+def rank_body(owners, capacity, stride):
+    def body(owner_ref, slot_ref, fine_ref, square_ref, target_ref, meta_ref):
         tokens = owner_ref.shape[1]
         step = 256
         upper = (iota((step, step), 0) < iota((step, step), 1)).astype(jnp.bfloat16)
@@ -67,7 +67,6 @@
         table = jnp.zeros((5 * owners, capacity), jnp.float32)
         for start in range(0, tokens, step):
             owner = owner_ref[:, start : start + step]
-            label = label_ref[:, start : start + step]
             hot = (iota((owners, step), 0) == owner).astype(jnp.float32)
             hot16 = hot.astype(jnp.bfloat16)
             before = jnp.dot(hot16, upper, preferred_element_type=jnp.float32) + carry
@@ -75,8 +74,8 @@
             carry = carry + jnp.sum(hot, axis=1, keepdims=True)
             target_ref[:, start : start + step] = owner * stride + place
             at_place = (iota((capacity, step), 0) == place).astype(jnp.bfloat16)
-            slot = (label // per_cluster).astype(jnp.float32)
-            fine = (label % per_cluster).astype(jnp.float32)
+            slot = slot_ref[:, start : start + step].astype(jnp.float32)
+            fine = fine_ref[:, start : start + step].astype(jnp.float32)
             first, second, third = digits(square_ref[:, start : start + step])
             parts = jnp.concatenate(
                 [hot * value for value in (slot + 1.0, fine, first, second, third)], axis=0
@@ -123,7 +122,7 @@
              held_out, square_out, totals, counts, labels):
         columns = slots * per_cluster
         blocks, stride, _ = rows_ref.shape
-        group = 4
+        group = 16
         totals[...] = jnp.zeros_like(totals)
         counts[...] = jnp.zeros_like(counts)
 
@@ -138,15 +137,18 @@
 
         lax.fori_loop(0, blocks, read, 0, unroll=4)
 
+        ids = iota((columns, LANES), 0).astype(jnp.int16)
+        one, zero = jnp.bfloat16(1.0), jnp.bfloat16(0.0)
+
         def add(index, carry):
             hots = []
-            count = counts[...]
+            count = jnp.zeros((columns, LANES), jnp.bfloat16)
             for offset in range(group):
                 marks = labels[pl.ds(index * group + offset, 1), :]
-                hot = (iota((columns, LANES), 0) == marks).astype(jnp.float32)
+                hot = jnp.where(ids == marks.astype(jnp.int16), one, zero)
                 count = count + hot
-                hots.append(hot.astype(jnp.bfloat16))
-            counts[...] = count
+                hots.append(hot)
+            counts[...] += count.astype(jnp.float32)
             rows = jnp.concatenate(
                 [rows_ref[index * group + offset, :LANES, :] for offset in range(group)], axis=0
             )
@@ -166,7 +168,7 @@
             fine = fine_ref[part, :]
             over_c = 1.0 / (count_c + prior_weight)
             over_f = 1.0 / (count_f + prior_weight)
-            for step in range(PASSES):
+            for _ in range(PASSES):
                 coarse = (sum_c + prior_weight * coarse) * over_c
                 fine = (sum_f - count_f * coarse + prior_weight * fine) * over_f
             coarse_out[slot : slot + 1, :] = coarse
@@ -186,7 +188,7 @@
         blocks = rows_ref.shape[0]
         pieces = out_ref.shape[0]
         quarter = per_cluster // pieces
-        group, pair = 4, 2
+        group, pair = 16, 2
 
         def one(index, carry):
             for first in range(0, group, pair):
@@ -317,14 +319,14 @@
     i16 = jnp.int16
     groups = tokens // LANES
     owner = owner_of.reshape(1, tokens)
-    label = (slot_in_owner * per_cluster + fine_in_cluster).reshape(1, tokens)
+    slot, part = slot_in_owner.reshape(1, tokens), fine_in_cluster.reshape(1, tokens)
     squares = jnp.sum(jnp.square(vectors.astype(f32)), axis=1).reshape(1, tokens)
     target, meta = call(
-        rank_body(owners, capacity, stride, per_cluster),
+        rank_body(owners, capacity, stride),
         (shape((1, tokens), i32), shape((5, owners, capacity), f32)),
-        [VMEM] * 3,
+        [VMEM] * 4,
         flops=400_000_000,
-    )(owner, label, squares)
+    )(owner, slot, part, squares)
     send_rows = call(
         pack_body(capacity, stride, 16),
         shape((owners * stride, width), bf16),
@@ -364,45 +366,45 @@
         mem=32 << 20,
     )(rows, coarse_init[mine], fine_init.reshape(columns, width))
 
-    with jax.named_scope("centres"):
-        gathered = coarse_mine
-        for bit in bits:
-            other = lax.ppermute(gathered, "dp", [(i, i ^ bit) for i in range(owners)])
-            gathered = jnp.concatenate([gathered, other], axis=0)
-
-    with jax.named_scope("measure"):
-        partial = call(
-            distance_body(slots, per_cluster),
-            shape((pieces, owners * quarter + owners, capacity), i16),
-            [VMEM] * 5,
-            flops=2 * total * columns * width,
-            scratch=[pltpu.VMEM((owners, LANES), f32)],
-            mem=32 << 20,
-        )(rows, held, square, cand, norms)
+    gathered = coarse_mine
+    for bit in bits:
+        other = lax.ppermute(gathered, "dp", [(i, i ^ bit) for i in range(owners)])
+        gathered = jnp.concatenate([gathered, other], axis=0)
+
+    partial = call(
+        distance_body(slots, per_cluster),
+        shape((pieces, owners * quarter + owners, capacity), i16),
+        [VMEM] * 5,
+        flops=2 * total * columns * width,
+        scratch=[pltpu.VMEM((owners, LANES), f32)],
+        mem=32 << 20,
+    )(rows, held, square, cand, norms)
+    arrived = exchanged(partial, "grp")
     share = call(
         total_body(),
         shape((owners, quarter, capacity), f32),
         [VMEM],
-        flops=10_000_000,
+        flops=2_000_000_000,
         scratch=[pltpu.VMEM((pieces, owners, LANES), f32)],
-    )(exchanged(partial, "grp"))
+    )(arrived)
     returned = exchanged(share, "dp")
     spread = call(
         pick_body(stride, features),
         shape((pieces, groups * quarter + groups, LANES), i16),
         [VMEM] * 3,
-        flops=100_000_000,
+        flops=4_000_000_000,
         scratch=[pltpu.VMEM((groups, LANES), f32)],
     )(returned, owner, target)
-    distances = call(
-        spread_body(quarter), shape((per_cluster, tokens), f32), [VMEM], flops=10_000_000
-    )(exchanged(spread, "grp"))
+    codes = exchanged(spread, "grp")
     coarse_out = call(
         arrange_body(),
         shape((owners * slots, width), f32),
         [SMEM, VMEM],
-        flops=10_000_000,
+        flops=2_000_000_000,
     )(cluster_at, gathered)
+    distances = call(
+        spread_body(quarter), shape((per_cluster, tokens), f32), [VMEM], flops=10_000_000
+    )(codes)
     return (coarse_out, fine.reshape(slots, per_cluster, width), distances)
 
 

time: 230 us -> 223 us (0.970)
  Pallas kernels: 53.2 us -> 46.1 us
    pallas_call x1, Pallas kernels: 14.6 us -> 10.1 us  [shards(): call(sums_body(slots, per_cluster), (shape((slots, width), f32), shape((c...]
    pallas_call x1, Pallas kernels: 11.9 us -> 9.25 us  [shards(): call(distance_body(slots, per_cluster), shape((pieces, owners * quarter +...]
    unnamed x21 -> x25, local copies, waits for them, and re-layouts: 6.03 us -> 7.47 us
where the time goes in v3:
time: 223 us; the launch traced here: 222 us
  waiting for transfers between devices  128 us (57%)
  Pallas kernels  46.1 us (21%)
  starting transfers between devices  35.8 us (16%)
  local copies, waits for them, and re-layouts  9.57 us (4%)
  other arithmetic  2.47 us (1%)
    all_to_all x4, waiting for transfers between devices, exchanged(): return lax.all_to_all(array, axis, split_axis=0, concat_axis=0, tiled=True)  109 us
    all_to_all x4, starting transfers between devices, exchanged(): return lax.all_to_all(array, axis, split_axis=0, concat_axis=0, tiled=True)  27.5 us
    ppermute x6, waiting for transfers between devices, shards(): other = lax.ppermute(gathered, 'dp', [(i, i ^ bit) for i in range(owners)])  18.9 us
    pallas_call x1, Pallas kernels, shards(): call(sums_body(slots, per_cluster), (shape((slots, width), f32), shape((c...  10.1 us
    pallas_call x1, Pallas kernels, shards(): call(distance_body(slots, per_cluster), shape((pieces, owners * quarter +...  9.25 us
    pallas_call x1, Pallas kernels, shards(): call(pick_body(stride, features), shape((pieces, groups * quarter + group...  8.58 us
    ppermute x6, starting transfers between devices, shards(): other = lax.ppermute(gathered, 'dp', [(i, i ^ bit) for i in range(owners)])  8.26 us
    pallas_call x1, Pallas kernels, shards(): call(pack_body(capacity, stride, 16), shape((owners * stride, width), bf1...  7.93 us
  transfers between devices with their start and end apart: 10, of which 7 were waited for; matrix products, arithmetic and copies ran while one was open for 2% of the time, Pallas kernels for 7%

profile of v3, /device:TPU:1, one launch (start us, length us, event | category | flops | bytes accessed | tf_op | source)
XLA Modules:
  0.0 222.4 jit_solution(3605082655008686943)
XLA Ops:
  0.6 0.0 copy-start
  0.6 0.0 copy-start.2
  0.7 2.4 %multiply_reduce_fusion = f32[4096]{0:T(1024)S(1)} fusion(bf16[4096,256]{1,0:T(8,128)(2,1)} %rows_ref.1), kind=kLoop, calls=%fused_computation.2 | loop fusion | flops 3141632 | bytes 2113536 | tf_op jit(solution)/shard_map/reduce_sum | solution.py:323
  3.0 0.0 copy-start.4
  3.0 0.7 copy-done.4
  3.7 0.7 copy-done.5
  4.5 0.7 copy-done.6
  5.2 2.5 %shard_map.103 = (s32[1,4096]{1,0:T(1,128)S(1)}, f32[5,64,128]{2,1,0:T(8,128)S(1)}) custom-call(s32[1,4096]{1,0:T(1,128)S(1)} %bitcast.14, s32[1,4096]{1,0:T(1,128)S(1)} %bitcast.12, s32[1,4096]{1,0:T(1,128)S(1)} %bitcast.13, f32[1,4096]{1,0:T(1,128)S(1)} %bitcast.10), custom_call_target="tpu_custom_call" | custom-call | flops 400000000 | bytes 4194304 | tf_op jit(solution)/shard_map/pallas_call | solution.py:324
  7.7 7.9 %shard_map.104 = bf16[8704,256]{1,0:T(8,128)(2,1)S(1)} custom-call(s32[4096]{0:T(1024)S(1)} %bitcast.9, bf16[4096,256]{1,0:T(8,128)(2,1)S(1)} %copy-done.2, f32[5,64,128]{2,1,0:T(8,128)S(1)} %get-tuple-element.12.meta_ref), custom_call_target="tpu_custom_call" | custom-call | flops 200000000 | bytes 4194304 | tf_op jit(solution)/shard_map/pallas_call | solution.py:330
  15.6 2.1 copy-done.1
  17.7 13.4 %all-to-all-start = ((bf16[64,136,256]{2,1,0:T(8,128)(2,1)}), bf16[64,136,256]{2,1,0:T(8,128)(2,1)}, u32[]{:S(2)}, u32[]{:S(2)}) async-start(bf16[64,136,256]{2,1,0:T(8,128)(2,1)} %bitcast.8), calls=%async_computation | async-start | bytes 8912896 | tf_op jit(solution)/shard_map/all_to_all | solution.py:32
  31.2 0.1 compare_select_fusion
  31.3 0.6 gather_fusion.1
  31.9 100.8 %all-to-all-done.rows_ref = bf16[64,136,256]{2,1,0:T(8,128)(2,1)} async-done(((bf16[64,136,256]{2,1,0:T(8,128)(2,1)}), bf16[64,136,256]{2,1,0:T(8,128)(2,1)}, u32[]{:S(2)}, u32[]{:S(2)}) %all-to-all-start) | async-done | bytes 4456480 | tf_op jit(solution)/shard_map/all_to_all | solution.py:32
  132.7 10.1 %shard_map.105 = (f32[16,256]{1,0:T(8,128)S(1)}, f32[1024,256]{1,0:T(8,128)}, bf16[1024,256]{1,0:T(8,128)(2,1)S(1)}, f32[1024,128]{1,0:T(8,128)S(1)}, s32[64,128]{1,0:T(8,128)S(1)}, /*index=5*/f32[64,128]{1,0:T(8,128)S(1)}) custom-call(bf16[64,136,256]{2,1,0:T(8,128)(2,1)} %all-to-all-done.rows_ref, f32[16,256]{1,0:T(8,128)S(1)} %gather_fusion.1, ...), custom_call_target="tpu_custom_call" | custom-call | flops 4294967296 | bytes 4194304 | tf_op jit(solution)/shard_map/pallas_call | solution.py:349
  142.8 9.2 %shard_map.107 = s16[4,1088,128]{2,1,0:T(8,128)(2,1)} custom-call(bf16[64,136,256]{2,1,0:T(8,128)(2,1)} %all-to-all-done.rows_ref, s32[64,128]{1,0:T(8,128)S(1)} %get-tuple-element.15.held_ref, f32[64,128]{1,0:T(8,128)S(1)} %get-tuple-element.16.square_ref, bf16[1024,256]{1,0:T(8,128)(2,1)S(1)} %get-tuple-element.17.cand_ref, ...), custom_call_target="tpu_custom_call" | custom-call | flops 4294967296 | bytes 4194304 | tf_op jit(solution)/shard_map/pallas_call | solution.py:374
  152.1 4.0 %all-to-all-start.1 = ((s16[4,1088,128]{2,1,0:T(8,128)(2,1)}), s16[4,1088,128]{2,1,0:T(8,128)(2,1)S(1)}, u32[]{:S(2)}, u32[]{:S(2)}) async-start(s16[4,1088,128]{2,1,0:T(8,128)(2,1)} %shard_map.107), calls=%async_computation.1 | async-start | bytes 2228224 | tf_op jit(solution)/shard_map/all_to_all | solution.py:32
  156.0 2.1 collective-permute-start
  158.1 0.6 constant_dynamic-update-slice_fusion.10
  158.7 3.8 %collective-permute-done = f32[16,256]{1,0:T(8,128)S(1)} collective-permute-done((f32[16,256]{1,0:T(8,128)S(1)}, f32[16,256]{1,0:T(8,128)S(1)}, u32[]{:S(2)}, u32[]{:S(2)}) %collective-permute-start) | collective-permute-done | bytes 16416 | tf_op jit(solution)/shard_map/ppermute | solution.py:371
  162.5 0.0 collective-permute-start.1
  162.5 0.6 constant_dynamic-update-slice_fusion.9
  163.2 3.4 %collective-permute-done.1 = f32[32,256]{1,0:T(8,128)S(1)} collective-permute-done((f32[32,256]{1,0:T(8,128)S(1)}, f32[32,256]{1,0:T(8,128)S(1)}, u32[]{:S(2)}, u32[]{:S(2)}) %collective-permute-start.1) | collective-permute-done | bytes 32800 | tf_op jit(solution)/shard_map/ppermute | solution.py:371
  166.5 0.0 copy-start.7
  166.5 0.7 collective-permute-start.2
  167.2 4.1 %all-to-all-done.1.got_ref = s16[4,1088,128]{2,1,0:T(8,128)(2,1)S(1)} async-done(((s16[4,1088,128]{2,1,0:T(8,128)(2,1)}), s16[4,1088,128]{2,1,0:T(8,128)(2,1)S(1)}, u32[]{:S(2)}, u32[]{:S(2)}) %all-to-all-start.1) | async-done | bytes 1114144 | tf_op jit(solution)/shard_map/all_to_all | solution.py:32
  171.3 1.3 shard_map.108
  172.6 6.6 %all-to-all-start.2 = ((f32[64,16,128]{2,1,0:T(8,128)}), f32[64,16,128]{2,1,0:T(8,128)S(1)}, u32[]{:S(2)}, u32[]{:S(2)}) async-start(f32[64,16,128]{2,1,0:T(8,128)} %shard_map.108), calls=%async_computation.2 | async-start | bytes 1048576 | tf_op jit(solution)/shard_map/all_to_all | solution.py:32
  179.2 0.0 collective-permute-done.2
  179.3 3.0 %collective-permute-start.3 = (f32[128,256]{1,0:T(8,128)S(1)}, f32[128,256]{1,0:T(8,128)S(1)}, u32[]{:S(2)}, u32[]{:S(2)}) collective-permute-start(f32[128,256]{1,0:T(8,128)S(1)} %pad_maximum_fusion), channel_id=1, source_target_pairs={{0,128},{4,132},{8,136},{12,140},{16,144},{20,148},{24,152},{28,15... | collective-permute-start | bytes 393224 | tf_op jit(solution)/shard_map/ppermute | solution.py:371
  182.3 0.6 constant_dynamic-update-slice_fusion.8
  182.9 0.7 constant_dynamic-update-slice_fusion.7
  183.6 3.3 %collective-permute-done.3 = f32[128,256]{1,0:T(8,128)S(1)} collective-permute-done((f32[128,256]{1,0:T(8,128)S(1)}, f32[128,256]{1,0:T(8,128)S(1)}, u32[]{:S(2)}, u32[]{:S(2)}) %collective-permute-start.3) | collective-permute-done | bytes 131104 | tf_op jit(solution)/shard_map/ppermute | solution.py:371
  186.9 0.7 constant_dynamic-update-slice_fusion.6
  187.6 0.8 collective-permute-start.4
  188.4 8.4 %collective-permute-done.4 = f32[256,256]{1,0:T(8,128)S(1)} collective-permute-done((f32[256,256]{1,0:T(8,128)}, f32[256,256]{1,0:T(8,128)S(1)}, u32[]{:S(2)}, u32[]{:S(2)}) %collective-permute-start.4) | collective-permute-done | bytes 262176 | tf_op jit(solution)/shard_map/ppermute | solution.py:371
  196.8 0.7 constant_dynamic-update-slice_fusion.5
  197.6 1.7 collective-permute-start.5
  199.2 0.1 reshape.36
  199.3 0.0 all-to-all-done.2.got_ref
  199.3 8.6 %shard_map.109 = s16[4,544,128]{2,1,0:T(8,128)(2,1)} custom-call(f32[64,16,128]{2,1,0:T(8,128)S(1)} %all-to-all-done.2.got_ref, s32[1,4096]{1,0:T(1,128)S(1)} %bitcast.15, s32[1,4096]{1,0:T(1,128)S(1)} %get-tuple-element.11.target_ref), custom_call_target="tpu_custom_call" | custom-call | flops 4000000000 | bytes 4194304 | tf_op jit(solution)/shard_map/pallas_call | solution.py:391
  207.9 3.5 %all-to-all-start.3 = ((s16[4,544,128]{2,1,0:T(8,128)(2,1)}), s16[4,544,128]{2,1,0:T(8,128)(2,1)S(1)}, u32[]{:S(2)}, u32[]{:S(2)}) async-start(s16[4,544,128]{2,1,0:T(8,128)(2,1)} %shard_map.109), calls=%async_computation.3 | async-start | bytes 1114112 | tf_op jit(solution)/shard_map/all_to_all | solution.py:32
  211.4 0.6 gather_fusion
  212.0 0.1 reshape.37.cluster_ref
  212.1 0.0 collective-permute-done.5
  212.1 5.3 %shard_map.106 = f32[1024,256]{1,0:T(8,128)} custom-call(s32[1024]{0:T(1024)S(1)} %reshape.37.cluster_ref, f32[1024,256]{1,0:T(8,128)S(1)} %constant_dynamic-update-slice_fusion.11.rows_ref), custom_call_target="tpu_custom_call" | custom-call | flops 2000000000 | bytes 4194304 | tf_op jit(solution)/shard_map/pallas_call | solution.py:399
  217.4 3.9 %all-to-all-done.3.got_ref = s16[4,544,128]{2,1,0:T(8,128)(2,1)S(1)} async-done(((s16[4,544,128]{2,1,0:T(8,128)(2,1)}), s16[4,544,128]{2,1,0:T(8,128)(2,1)S(1)}, u32[]{:S(2)}, u32[]{:S(2)}) %all-to-all-start.3) | async-done | bytes 557088 | tf_op jit(solution)/shard_map/all_to_all | solution.py:32
  221.3 1.1 shard_map.110
  (19 shorter events, 0.1 us)
Async XLA Ops:
  0.6 30.7 %copy-start = (f32[1024,256]{1,0:T(8,128)S(1)}, f32[1024,256]{1,0:T(8,128)}, u32[]{:S(2)}) copy-start(f32[1024,256]{1,0:T(8,128)} %param.9) | copy-start | bytes 3145732
  0.6 7.0 %copy-start.2 = (bf16[4096,256]{1,0:T(8,128)(2,1)S(1)}, bf16[4096,256]{1,0:T(8,128)(2,1)}, u32[]{:S(2)}) copy-start(bf16[4096,256]{1,0:T(8,128)(2,1)} %rows_ref.1) | copy-start | bytes 6291460
  3.0 0.7 copy-start.4
  3.7 0.7 copy-start.5
  4.5 0.7 copy-start.6
  15.6 2.1 copy-start.1
  17.7 13.5 %copy-start.8 = (s32[1024]{0:T(1024)S(1)}, s32[1024]{0:T(1024)}, u32[]{:S(2)}) copy-start(s32[1024]{0:T(1024)} %param.14) | copy-start | bytes 12292
  17.7 115.0 %copy-start.3 = (f32[16,64,256]{2,1,0:T(8,128)S(1)}, f32[16,64,256]{2,1,0:T(8,128)}, u32[]{:S(2)}) copy-start(f32[16,64,256]{2,1,0:T(8,128)} %param.10) | copy-start | bytes 3145732
  17.7 115.0 %all-to-all-start = ((bf16[64,136,256]{2,1,0:T(8,128)(2,1)}), bf16[64,136,256]{2,1,0:T(8,128)(2,1)}, u32[]{:S(2)}, u32[]{:S(2)}) async-start(bf16[64,136,256]{2,1,0:T(8,128)(2,1)} %bitcast.8), calls=%async_computation | async-start | bytes 8912896 | tf_op jit(solution)/shard_map/all_to_all | solution.py:32
  152.1 19.3 %all-to-all-start.1 = ((s16[4,1088,128]{2,1,0:T(8,128)(2,1)}), s16[4,1088,128]{2,1,0:T(8,128)(2,1)S(1)}, u32[]{:S(2)}, u32[]{:S(2)}) async-start(s16[4,1088,128]{2,1,0:T(8,128)(2,1)} %shard_map.107), calls=%async_computation.1 | async-start | bytes 2228224 | tf_op jit(solution)/shard_map/all_to_all | solution.py:32
  156.0 6.5 %collective-permute-start = (f32[16,256]{1,0:T(8,128)S(1)}, f32[16,256]{1,0:T(8,128)S(1)}, u32[]{:S(2)}, u32[]{:S(2)}) collective-permute-start(f32[16,256]{1,0:T(8,128)S(1)} %get-tuple-element.13), channel_id=1, source_target_pairs={{0,32},{4,36},{8,40},{12,44},{16,48},{20,52},{24,56},{28,60},{32,0... | collective-permute-start | bytes 49160 | tf_op jit(solution)/shard_map/ppermute | solution.py:371
  162.5 4.0 %collective-permute-start.1 = (f32[32,256]{1,0:T(8,128)S(1)}, f32[32,256]{1,0:T(8,128)S(1)}, u32[]{:S(2)}, u32[]{:S(2)}) collective-permute-start(f32[32,256]{1,0:T(8,128)S(1)} %pad_maximum_fusion.2), channel_id=1, source_target_pairs={{0,16},{4,20},{8,24},{12,28},{16,0},{20,4},{24,8},{28,12},{32,48},... | collective-permute-start | bytes 98312 | tf_op jit(solution)/shard_map/ppermute | solution.py:371
  166.5 32.7 %copy-start.9 = (s32[64]{0:T(128)S(1)}, s32[64]{0:T(128)}, u32[]{:S(2)}) copy-start(s32[64]{0:T(128)} %constant.7.clone) | copy-start | bytes 772
  166.5 32.8 %copy-start.7 = (s32[4096,1]{0,1:T(1,128)S(1)}, s32[4096,1]{0,1:T(1,128)}, u32[]{:S(2)}) copy-start(s32[4096,1]{0,1:T(1,128)} %param.11) | copy-start | bytes 49156
  166.5 12.7 %collective-permute-start.2 = (f32[64,256]{1,0:T(8,128)S(1)}, f32[64,256]{1,0:T(8,128)S(1)}, u32[]{:S(2)}, u32[]{:S(2)}) collective-permute-start(f32[64,256]{1,0:T(8,128)S(1)} %pad_maximum_fusion.1), channel_id=1, source_target_pairs={{0,8},{4,12},{8,0},{12,4},{16,24},{20,28},{24,16},{28,20},{32,40},... | collective-permute-start | bytes 196616 | tf_op jit(solution)/shard_map/ppermute | solution.py:371
  172.6 26.7 %all-to-all-start.2 = ((f32[64,16,128]{2,1,0:T(8,128)}), f32[64,16,128]{2,1,0:T(8,128)S(1)}, u32[]{:S(2)}, u32[]{:S(2)}) async-start(f32[64,16,128]{2,1,0:T(8,128)} %shard_map.108), calls=%async_computation.2 | async-start | bytes 1048576 | tf_op jit(solution)/shard_map/all_to_all | solution.py:32
  179.3 7.6 %collective-permute-start.3 = (f32[128,256]{1,0:T(8,128)S(1)}, f32[128,256]{1,0:T(8,128)S(1)}, u32[]{:S(2)}, u32[]{:S(2)}) collective-permute-start(f32[128,256]{1,0:T(8,128)S(1)} %pad_maximum_fusion), channel_id=1, source_target_pairs={{0,128},{4,132},{8,136},{12,140},{16,144},{20,148},{24,152},{28,15... | collective-permute-start | bytes 393224 | tf_op jit(solution)/shard_map/ppermute | solution.py:371
  187.6 9.2 %collective-permute-start.4 = (f32[256,256]{1,0:T(8,128)}, f32[256,256]{1,0:T(8,128)S(1)}, u32[]{:S(2)}, u32[]{:S(2)}) collective-permute-start(f32[256,256]{1,0:T(8,128)} %get-tuple-element.23), channel_id=1, source_target_pairs={{0,64},{4,68},{8,72},{12,76},{16,80},{20,84},{24,88},{28,92},{32,9... | collective-permute-start | bytes 786440 | tf_op jit(solution)/shard_map/ppermute | solution.py:371
  197.6 14.5 %collective-permute-start.5 = (f32[512,256]{1,0:T(8,128)}, f32[512,256]{1,0:T(8,128)S(1)}, u32[]{:S(2)}, u32[]{:S(2)}) collective-permute-start(f32[512,256]{1,0:T(8,128)} %get-tuple-element.19), channel_id=1, source_target_pairs={{0,4},{4,0},{8,12},{12,8},{16,20},{20,16},{24,28},{28,24},{32,36},... | collective-permute-start | bytes 1572872 | tf_op jit(solution)/shard_map/ppermute | solution.py:371
  207.9 13.4 %all-to-all-start.3 = ((s16[4,544,128]{2,1,0:T(8,128)(2,1)}), s16[4,544,128]{2,1,0:T(8,128)(2,1)S(1)}, u32[]{:S(2)}, u32[]{:S(2)}) async-start(s16[4,544,128]{2,1,0:T(8,128)(2,1)} %shard_map.109), calls=%async_computation.3 | async-start | bytes 1114112 | tf_op jit(solution)/shard_map/all_to_all | solution.py:32

commit v4 on v3

--- a/solution.py
+++ b/solution.py
@@ -8,20 +8,22 @@
 
 PASSES = 2
 LANES = 128
+CHUNKS = 4
 
 
 prior_weight = 2.0
 
 VMEM = pl.BlockSpec(memory_space=pltpu.VMEM)
 SMEM = pl.BlockSpec(memory_space=pltpu.SMEM)
-
-
-def call(body, out_shape, ins, flops, scratch=(), mem=16 << 20):
+HBM = pl.BlockSpec(memory_space=pl.ANY)
+
+
+def call(body, out_shape, ins, flops, scratch=(), mem=16 << 20, outs=None):
     return pl.pallas_call(
         body,
         out_shape=out_shape,
         in_specs=ins,
-        out_specs=jax.tree.map(lambda _: VMEM, out_shape),
+        out_specs=outs or jax.tree.map(lambda _: VMEM, out_shape),
         scratch_shapes=list(scratch),
         compiler_params=pltpu.CompilerParams(vmem_limit_bytes=mem),
         cost_estimate=pl.CostEstimate(flops=flops, bytes_accessed=4 << 20, transcendentals=0),
@@ -58,71 +60,102 @@
     return jnp.exp2(power.astype(jnp.int32).astype(jnp.float32) - 16.0)
 
 
-def rank_body(owners, capacity, stride):
-    def body(owner_ref, slot_ref, fine_ref, square_ref, target_ref, meta_ref):
-        tokens = owner_ref.shape[1]
+def send_body(capacity, stride, chunks, unroll):
+    def body(owner_ref, slot_ref, fine_ref, rows_hbm, target_ref, packed_hbm,
+             rows, source, wide, packed, targets, done):
+        tokens = rows.shape[0]
+        total = packed.shape[0]
+        owners = total // stride
         step = 256
+        load = pltpu.make_async_copy(rows_hbm, rows, done.at[0])
+        load.start()
         upper = (iota((step, step), 0) < iota((step, step), 1)).astype(jnp.bfloat16)
         carry = jnp.zeros((owners, 1), jnp.float32)
-        table = jnp.zeros((5 * owners, capacity), jnp.float32)
         for start in range(0, tokens, step):
             owner = owner_ref[:, start : start + step]
             hot = (iota((owners, step), 0) == owner).astype(jnp.float32)
-            hot16 = hot.astype(jnp.bfloat16)
-            before = jnp.dot(hot16, upper, preferred_element_type=jnp.float32) + carry
+            before = carry + jnp.dot(
+                hot.astype(jnp.bfloat16), upper, preferred_element_type=jnp.float32
+            )
             place = jnp.sum(hot * before, axis=0, keepdims=True).astype(jnp.int32)
             carry = carry + jnp.sum(hot, axis=1, keepdims=True)
             target_ref[:, start : start + step] = owner * stride + place
+        wide[...] = jnp.zeros_like(wide)
+        move = pltpu.make_async_copy(target_ref, targets, done.at[1])
+        move.start()
+        load.wait()
+        table = jnp.zeros((5 * owners, capacity), jnp.float32)
+        for start in range(0, tokens, step):
+            square = jnp.zeros((LANES, step), jnp.float32)
+            for half in range(2):
+                value = rows[
+                    start : start + step, half * LANES : (half + 1) * LANES
+                ].astype(jnp.float32)
+                source[pl.ds(2 * start + half, step, stride=2), :] = value
+                square = square + (value * value).T
+            owner = owner_ref[:, start : start + step]
+            place = target_ref[:, start : start + step] - owner * stride
+            hot = (iota((owners, step), 0) == owner).astype(jnp.float32)
             at_place = (iota((capacity, step), 0) == place).astype(jnp.bfloat16)
             slot = slot_ref[:, start : start + step].astype(jnp.float32)
             fine = fine_ref[:, start : start + step].astype(jnp.float32)
-            first, second, third = digits(square_ref[:, start : start + step])
+            squares = digits(jnp.sum(square, axis=0, keepdims=True))
             parts = jnp.concatenate(
-                [hot * value for value in (slot + 1.0, fine, first, second, third)], axis=0
+                [hot * value for value in (slot + 1.0, fine, *squares)], axis=0
             ).astype(jnp.bfloat16)
             table = table + lax.dot_general(
                 parts, at_place, (((1,), (1,)), ((), ())), preferred_element_type=jnp.float32
             )
         for part in range(5):
-            meta_ref[part] = table[part * owners : (part + 1) * owners]
-
-    return body
-
-
-def pack_body(capacity, stride, unroll):
-    def body(target_ref, rows_ref, meta_ref, packed_ref, source, wide):
-        tokens = rows_ref.shape[0]
-        total = packed_ref.shape[0]
-        wide[...] = jnp.zeros_like(wide)
-        for part in range(5):
-            wide[pl.ds(2 * capacity + part, meta_ref.shape[1], stride=2 * stride), :] = meta_ref[part]
-        for half in range(2):
-            source[pl.ds(half, tokens, stride=2), :] = rows_ref[
-                :, half * LANES : (half + 1) * LANES
-            ].astype(jnp.float32)
-
-        def move(index, carry):
+            wide[pl.ds(2 * capacity + part, owners, stride=2 * stride), :] = table[
+                part * owners : (part + 1) * owners
+            ]
+        move.wait()
+
+        def place_rows(index, carry):
             for offset in range(unroll):
                 token = index * unroll + offset
-                target = target_ref[token]
-                wide[pl.ds(2 * target, 2), :] = source[pl.ds(2 * token, 2), :]
-            return carry
-
-        lax.fori_loop(0, tokens // unroll, move, 0)
-        for half in range(2):
-            packed_ref[:, half * LANES : (half + 1) * LANES] = wide[
-                pl.ds(half, total, stride=2), :
-            ].astype(jnp.bfloat16)
-
-    return body
+                wide[pl.ds(2 * targets[0, token], 2), :] = source[pl.ds(2 * token, 2), :]
+            return carry
+
+        lax.fori_loop(0, tokens // unroll, place_rows, 0)
+        length = total // chunks
+        copies = []
+        for chunk in range(chunks):
+            part = pl.ds(chunk * length, length)
+            for half in range(2):
+                packed[part, half * LANES : (half + 1) * LANES] = wide[
+                    pl.ds(2 * chunk * length + half, length, stride=2), :
+                ].astype(jnp.bfloat16)
+            copies.append(
+                pltpu.make_async_copy(packed.at[part], packed_hbm.at[part], done.at[2 + chunk])
+            )
+            if chunk:
+                copies[-2].start()
+        copies[-1].start()
+        for copy in copies:
+            copy.wait()
+
+    return body
+
+
+def fetches(rows_hbm, rows, done, group):
+    copies = []
+    for chunk in range(rows.shape[0] // group):
+        part = pl.ds(chunk * group, group)
+        copies.append(pltpu.make_async_copy(rows_hbm.at[part], rows.at[part], done.at[chunk]))
+    return copies
 
 
 def sums_body(slots, per_cluster):
-    def body(rows_ref, coarse_ref, fine_ref, coarse_out, fine_out, cand_out, norm_out,
-             held_out, square_out, totals, counts, labels):
+    def body(rows_hbm, coarse_ref, fine_ref, coarse_out, fine_out, cand_out, norm_out,
+             held_out, square_out, totals, counts, labels, rows_ref, done):
         columns = slots * per_cluster
         blocks, stride, _ = rows_ref.shape
-        group = 16
+        group = blocks // CHUNKS
+        copies = fetches(rows_hbm, rows_ref, done, group)
+        for copy in copies:
+            copy.start()
         totals[...] = jnp.zeros_like(totals)
         counts[...] = jnp.zeros_like(counts)
 
@@ -134,8 +167,6 @@
             held_out[here, :] = slot.astype(jnp.int32) - 1
             square_out[here, :] = (meta[1:2, :LANES] + meta[1:2, LANES:]) + meta[2:3, :LANES]
             return carry
-
-        lax.fori_loop(0, blocks, read, 0, unroll=4)
 
         ids = iota((columns, LANES), 0).astype(jnp.int16)
         one, zero = jnp.bfloat16(1.0), jnp.bfloat16(0.0)
@@ -157,7 +188,10 @@
             )
             return carry
 
-        lax.fori_loop(0, blocks // group, add, 0)
+        for chunk, copy in enumerate(copies):
+            copy.wait()
+            lax.fori_loop(chunk * group, (chunk + 1) * group, read, 0, unroll=True)
+            add(chunk, 0)
         for slot in range(slots):
             part = pl.ds(slot * per_cluster, per_cluster)
             sum_f = totals[part, :]
@@ -184,11 +218,14 @@
 
 
 def distance_body(slots, per_cluster):
-    def body(rows_ref, held_ref, square_ref, cand_ref, norm_ref, out_ref, powers):
+    def body(rows_hbm, held_ref, square_ref, cand_ref, norm_ref, out_ref, powers, rows_ref, done):
         blocks = rows_ref.shape[0]
         pieces = out_ref.shape[0]
         quarter = per_cluster // pieces
-        group, pair = 16, 2
+        group, pair = blocks // CHUNKS, 2
+        copies = fetches(rows_hbm, rows_ref, done, group)
+        for copy in copies:
+            copy.start()
 
         def one(index, carry):
             for first in range(0, group, pair):
@@ -217,7 +254,9 @@
                         )
             return carry
 
-        lax.fori_loop(0, blocks // group, one, 0)
+        for chunk, copy in enumerate(copies):
+            copy.wait()
+            one(chunk, 0)
         for piece in range(pieces):
             out_ref[piece, blocks * quarter :, :] = powers[...].astype(jnp.int32).astype(jnp.int16)
 
@@ -258,7 +297,7 @@
             owner = jnp.broadcast_to(owner, (quarter, LANES))
             value = jnp.zeros((quarter, LANES), jnp.float32)
             for number in range(owners):
-                found = jnp.take_along_axis(got_ref[number], place, axis=1)
+                found = jnp.take_along_axis(got_ref[number], place, axis=1, mode="promise_in_bounds")
                 value = jnp.where(owner == number, found, value)
             code, power = coded(value * (1.0 / features))
             powers[pl.ds(index, 1), :] = power
@@ -266,7 +305,7 @@
                 out_ref[copy, pl.ds(pl.multiple_of(index * quarter, quarter), quarter), :] = code
             return carry
 
-        lax.fori_loop(0, groups, one, 0)
+        lax.fori_loop(0, groups, one, 0, unroll=2)
         for copy in range(copies):
             out_ref[copy, groups * quarter :, :] = powers[...].astype(jnp.int32).astype(jnp.int16)
 
@@ -320,24 +359,22 @@
     groups = tokens // LANES
     owner = owner_of.reshape(1, tokens)
     slot, part = slot_in_owner.reshape(1, tokens), fine_in_cluster.reshape(1, tokens)
-    squares = jnp.sum(jnp.square(vectors.astype(f32)), axis=1).reshape(1, tokens)
-    target, meta = call(
-        rank_body(owners, capacity, stride),
-        (shape((1, tokens), i32), shape((5, owners, capacity), f32)),
-        [VMEM] * 4,
+    target, send_rows = call(
+        send_body(capacity, stride, 4, 32),
+        (shape((1, tokens), i32), shape((owners * stride, width), bf16)),
+        [VMEM, VMEM, VMEM, HBM],
         flops=400_000_000,
-    )(owner, slot, part, squares)
-    send_rows = call(
-        pack_body(capacity, stride, 16),
-        shape((owners * stride, width), bf16),
-        [SMEM, VMEM, VMEM],
-        flops=200_000_000,
         scratch=[
+            pltpu.VMEM((tokens, width), bf16),
             pltpu.VMEM((2 * tokens, LANES), f32),
             pltpu.VMEM((2 * owners * stride, LANES), f32),
+            pltpu.VMEM((owners * stride, width), bf16),
+            pltpu.SMEM((1, tokens), i32),
+            pltpu.SemaphoreType.DMA((6,)),
         ],
-        mem=32 << 20,
-    )(target.reshape(tokens), vectors, meta)
+        mem=56 << 20,
+        outs=(VMEM, HBM),
+    )(owner, slot, part, vectors)
     rows = exchanged(send_rows.reshape(owners, stride, width), "dp")
     bits = [bit for bit in (8, 4, 2, 32, 16, 1) if bit < owners]
     masks = [
@@ -356,12 +393,14 @@
             shape((owners, LANES), i32),
             shape((owners, LANES), f32),
         ),
-        [VMEM] * 3,
+        [HBM, VMEM, VMEM],
         flops=2 * total * columns * width,
         scratch=[
             pltpu.VMEM((columns, width), f32),
             pltpu.VMEM((columns, LANES), f32),
             pltpu.VMEM((owners, LANES), i32),
+            pltpu.VMEM((owners, stride, width), bf16),
+            pltpu.SemaphoreType.DMA((CHUNKS,)),
         ],
         mem=32 << 20,
     )(rows, coarse_init[mine], fine_init.reshape(columns, width))
@@ -374,9 +413,13 @@
     partial = call(
         distance_body(slots, per_cluster),
         shape((pieces, owners * quarter + owners, capacity), i16),
-        [VMEM] * 5,
+        [HBM, VMEM, VMEM, VMEM, VMEM],
         flops=2 * total * columns * width,
-        scratch=[pltpu.VMEM((owners, LANES), f32)],
+        scratch=[
+            pltpu.VMEM((owners, LANES), f32),
+            pltpu.VMEM((owners, stride, width), bf16),
+            pltpu.SemaphoreType.DMA((CHUNKS,)),
+        ],
         mem=32 << 20,
     )(rows, held, square, cand, norms)
     arrived = exchanged(partial, "grp")

time: 223 us -> 217 us (0.973)
  local copies, waits for them, and re-layouts: 9.57 us -> 5.35 us
  other arithmetic: 2.47 us -> 0.12 us
    unnamed x25 -> x17, local copies, waits for them, and re-layouts: 7.47 us -> 3.25 us
    reduce_sum x1 -> x0, other arithmetic: 2.36 us -> none  [shards(): jnp.sum(jnp.square(vectors.astype(f32)), axis=1).reshape(1, tokens)]
    pallas_call x2 -> x1, Pallas kernels: 10.4 us -> 11.8 us  [shards(): call(send_body(capacity, stride, 4, 32), (shape((1, tokens), i32), shape(...]
  transfers between devices with their start and end apart: 10 -> 10, of which waited for: 7 -> 7; matrix products, arithmetic and copies ran while one was open for 2% -> 3% of each run, Pallas kernels for 7% -> 6%
where the time goes in v4:
time: 217 us
  waiting for transfers between devices  128 us (59%)
  Pallas kernels  46.8 us (22%)
  starting transfers between devices  35.9 us (17%)
  local copies, waits for them, and re-layouts  5.35 us (2%)
    all_to_all x4, waiting for transfers between devices, exchanged(): return lax.all_to_all(array, axis, split_axis=0, concat_axis=0, tiled=True)  109 us
    all_to_all x4, starting transfers between devices, exchanged(): return lax.all_to_all(array, axis, split_axis=0, concat_axis=0, tiled=True)  27.6 us
    ppermute x6, waiting for transfers between devices, shards(): other = lax.ppermute(gathered, 'dp', [(i, i ^ bit) for i in range(owners)])  18.9 us
    pallas_call x1, Pallas kernels, shards(): call(sums_body(slots, per_cluster), (shape((slots, width), f32), shape((c...  12.2 us
    pallas_call x1, Pallas kernels, shards(): call(send_body(capacity, stride, 4, 32), (shape((1, tokens), i32), shape(...  11.8 us
    ppermute x6, starting transfers between devices, shards(): other = lax.ppermute(gathered, 'dp', [(i, i ^ bit) for i in range(owners)])  8.3 us
    pallas_call x1, Pallas kernels, shards(): call(distance_body(slots, per_cluster), shape((pieces, owners * quarter +...  8.19 us
    pallas_call x1, Pallas kernels, shards(): call(pick_body(stride, features), shape((pieces, groups * quarter + group...  6.9 us
  transfers between devices with their start and end apart: 10, of which 7 were waited for; matrix products, arithmetic and copies ran while one was open for 3% of the time, Pallas kernels for 6%

profile of v4, /device:TPU:1, one launch (start us, length us, event | category | flops | bytes accessed | tf_op | source)
XLA Modules:
  0.0 216.7 jit_solution(14758773293489214047)
XLA Ops:
  0.6 0.0 copy-start
  0.6 11.8 %shard_map.103 = (s32[1,4096]{1,0:T(1,128)}, bf16[8704,256]{1,0:T(8,128)(2,1)}) custom-call(s32[1,4096]{1,0:T(1,128)} %bitcast.6, s32[1,4096]{1,0:T(1,128)} %bitcast.10, s32[1,4096]{1,0:T(1,128)} %bitcast.11, bf16[4096,256]{1,0:T(8,128)(2,1)} %rows_hbm.1), custom_call_target="tpu_custom_call" | custom-call | flops 400000000 | bytes 4194304 | tf_op jit(solution)/shard_map/pallas_call | solution.py:362
  12.5 0.0 copy-start.4
  12.5 0.0 copy-start.2
  12.5 13.5 %all-to-all-start = ((bf16[64,136,256]{2,1,0:T(8,128)(2,1)}), bf16[64,136,256]{2,1,0:T(8,128)(2,1)}, u32[]{:S(2)}, u32[]{:S(2)}) async-start(bf16[64,136,256]{2,1,0:T(8,128)(2,1)} %bitcast.9), calls=%async_computation | async-start | bytes 8912896 | tf_op jit(solution)/shard_map/all_to_all | solution.py:34
  26.0 0.0 copy-done.4
  26.0 0.1 compare_select_fusion
  26.1 0.0 copy-done
  26.1 0.6 gather_fusion.1
  26.6 100.8 %all-to-all-done.rows_hbm = bf16[64,136,256]{2,1,0:T(8,128)(2,1)} async-done(((bf16[64,136,256]{2,1,0:T(8,128)(2,1)}), bf16[64,136,256]{2,1,0:T(8,128)(2,1)}, u32[]{:S(2)}, u32[]{:S(2)}) %all-to-all-start) | async-done | bytes 4456480 | tf_op jit(solution)/shard_map/all_to_all | solution.py:34
  127.4 0.0 copy-done.2
  127.4 12.2 %shard_map.104 = (f32[16,256]{1,0:T(8,128)S(1)}, f32[1024,256]{1,0:T(8,128)}, bf16[1024,256]{1,0:T(8,128)(2,1)S(1)}, f32[1024,128]{1,0:T(8,128)S(1)}, s32[64,128]{1,0:T(8,128)S(1)}, /*index=5*/f32[64,128]{1,0:T(8,128)S(1)}) custom-call(bf16[64,136,256]{2,1,0:T(8,128)(2,1)} %all-to-all-done.rows_hbm, f32[16,256]{1,0:T(8,128)S(1)} %gather_fusion.1, ...), custom_call_target="tpu_custom_call" | custom-call | flops 4294967296 | bytes 4194304 | tf_op jit(solution)/shard_map/pallas_call | solution.py:386
  139.7 8.2 %shard_map.106 = s16[4,1088,128]{2,1,0:T(8,128)(2,1)} custom-call(bf16[64,136,256]{2,1,0:T(8,128)(2,1)} %all-to-all-done.rows_hbm, s32[64,128]{1,0:T(8,128)S(1)} %get-tuple-element.14.held_ref, f32[64,128]{1,0:T(8,128)S(1)} %get-tuple-element.15.square_ref, bf16[1024,256]{1,0:T(8,128)(2,1)S(1)} %get-tuple-element.16.cand_ref, ...), custom_call_target="tpu_custom_call" | custom-call | flops 4294967296 | bytes 4194304 | tf_op jit(solution)/shard_map/pallas_call | solution.py:413
  147.9 4.0 %all-to-all-start.1 = ((s16[4,1088,128]{2,1,0:T(8,128)(2,1)}), s16[4,1088,128]{2,1,0:T(8,128)(2,1)S(1)}, u32[]{:S(2)}, u32[]{:S(2)}) async-start(s16[4,1088,128]{2,1,0:T(8,128)(2,1)} %shard_map.106), calls=%async_computation.1 | async-start | bytes 2228224 | tf_op jit(solution)/shard_map/all_to_all | solution.py:34
  151.9 2.1 collective-permute-start
  154.0 0.6 constant_dynamic-update-slice_fusion.10
  154.6 3.8 %collective-permute-done = f32[16,256]{1,0:T(8,128)S(1)} collective-permute-done((f32[16,256]{1,0:T(8,128)S(1)}, f32[16,256]{1,0:T(8,128)S(1)}, u32[]{:S(2)}, u32[]{:S(2)}) %collective-permute-start) | collective-permute-done | bytes 16416 | tf_op jit(solution)/shard_map/ppermute | solution.py:410
  158.4 0.0 collective-permute-start.1
  158.4 0.6 constant_dynamic-update-slice_fusion.9
  159.0 3.3 %collective-permute-done.1 = f32[32,256]{1,0:T(8,128)S(1)} collective-permute-done((f32[32,256]{1,0:T(8,128)S(1)}, f32[32,256]{1,0:T(8,128)S(1)}, u32[]{:S(2)}, u32[]{:S(2)}) %collective-permute-start.1) | collective-permute-done | bytes 32800 | tf_op jit(solution)/shard_map/ppermute | solution.py:410
  162.4 0.7 collective-permute-start.2
  163.1 4.2 %all-to-all-done.1.got_ref = s16[4,1088,128]{2,1,0:T(8,128)(2,1)S(1)} async-done(((s16[4,1088,128]{2,1,0:T(8,128)(2,1)}), s16[4,1088,128]{2,1,0:T(8,128)(2,1)S(1)}, u32[]{:S(2)}, u32[]{:S(2)}) %all-to-all-start.1) | async-done | bytes 1114144 | tf_op jit(solution)/shard_map/all_to_all | solution.py:34
  167.3 1.3 shard_map.107
  168.5 0.0 copy-start.5
  168.5 6.7 %all-to-all-start.2 = ((f32[64,16,128]{2,1,0:T(8,128)}), f32[64,16,128]{2,1,0:T(8,128)S(1)}, u32[]{:S(2)}, u32[]{:S(2)}) async-start(f32[64,16,128]{2,1,0:T(8,128)} %shard_map.107), calls=%async_computation.2 | async-start | bytes 1048576 | tf_op jit(solution)/shard_map/all_to_all | solution.py:34
  175.2 0.0 collective-permute-done.2
  175.2 3.0 %collective-permute-start.3 = (f32[128,256]{1,0:T(8,128)S(1)}, f32[128,256]{1,0:T(8,128)S(1)}, u32[]{:S(2)}, u32[]{:S(2)}) collective-permute-start(f32[128,256]{1,0:T(8,128)S(1)} %pad_maximum_fusion), channel_id=1, source_target_pairs={{0,128},{4,132},{8,136},{12,140},{16,144},{20,148},{24,152},{28,15... | collective-permute-start | bytes 393224 | tf_op jit(solution)/shard_map/ppermute | solution.py:410
  178.3 0.6 constant_dynamic-update-slice_fusion.8
  178.9 0.7 constant_dynamic-update-slice_fusion.7
  179.6 3.3 %collective-permute-done.3 = f32[128,256]{1,0:T(8,128)S(1)} collective-permute-done((f32[128,256]{1,0:T(8,128)S(1)}, f32[128,256]{1,0:T(8,128)S(1)}, u32[]{:S(2)}, u32[]{:S(2)}) %collective-permute-start.3) | collective-permute-done | bytes 131104 | tf_op jit(solution)/shard_map/ppermute | solution.py:410
  182.8 0.7 constant_dynamic-update-slice_fusion.6
  183.6 0.8 collective-permute-start.4
  184.3 8.4 %collective-permute-done.4 = f32[256,256]{1,0:T(8,128)S(1)} collective-permute-done((f32[256,256]{1,0:T(8,128)}, f32[256,256]{1,0:T(8,128)S(1)}, u32[]{:S(2)}, u32[]{:S(2)}) %collective-permute-start.4) | collective-permute-done | bytes 262176 | tf_op jit(solution)/shard_map/ppermute | solution.py:410
  192.8 0.7 constant_dynamic-update-slice_fusion.5
  193.5 1.7 collective-permute-start.5
  195.2 0.0 copy-done.5
  195.2 0.1 reshape.30
  195.3 0.0 all-to-all-done.2.got_ref
  195.3 0.0 copy-done.1
  195.3 0.0 copy-done.3
  195.3 6.9 %shard_map.108 = s16[4,544,128]{2,1,0:T(8,128)(2,1)} custom-call(f32[64,16,128]{2,1,0:T(8,128)S(1)} %all-to-all-done.2.got_ref, s32[1,4096]{1,0:T(1,128)S(1)} %bitcast.7, s32[1,4096]{1,0:T(1,128)S(1)} %copy-done.3), custom_call_target="tpu_custom_call" | custom-call | flops 4000000000 | bytes 4194304 | tf_op jit(solution)/shard_map/pallas_call | solution.py:434
  202.2 3.5 %all-to-all-start.3 = ((s16[4,544,128]{2,1,0:T(8,128)(2,1)}), s16[4,544,128]{2,1,0:T(8,128)(2,1)S(1)}, u32[]{:S(2)}, u32[]{:S(2)}) async-start(s16[4,544,128]{2,1,0:T(8,128)(2,1)} %shard_map.108), calls=%async_computation.3 | async-start | bytes 1114112 | tf_op jit(solution)/shard_map/all_to_all | solution.py:34
  205.7 0.6 gather_fusion
  206.3 0.1 reshape.31.cluster_ref
  206.4 0.0 collective-permute-done.5
  206.4 5.3 %shard_map.105 = f32[1024,256]{1,0:T(8,128)} custom-call(s32[1024]{0:T(1024)S(1)} %reshape.31.cluster_ref, f32[1024,256]{1,0:T(8,128)S(1)} %constant_dynamic-update-slice_fusion.11.rows_ref), custom_call_target="tpu_custom_call" | custom-call | flops 2000000000 | bytes 4194304 | tf_op jit(solution)/shard_map/pallas_call | solution.py:442
  211.7 3.9 %all-to-all-done.3.got_ref = s16[4,544,128]{2,1,0:T(8,128)(2,1)S(1)} async-done(((s16[4,544,128]{2,1,0:T(8,128)(2,1)}), s16[4,544,128]{2,1,0:T(8,128)(2,1)S(1)}, u32[]{:S(2)}, u32[]{:S(2)}) %all-to-all-start.3) | async-done | bytes 557088 | tf_op jit(solution)/shard_map/all_to_all | solution.py:34
  215.5 1.1 shard_map.109
  (9 shorter events, 0.1 us)
Async XLA Ops:
  0.6 25.4 %copy-start = (f32[1024,256]{1,0:T(8,128)S(1)}, f32[1024,256]{1,0:T(8,128)}, u32[]{:S(2)}) copy-start(f32[1024,256]{1,0:T(8,128)} %param.9) | copy-start | bytes 3145732
  12.5 13.5 %copy-start.4 = (s32[1024]{0:T(1024)S(1)}, s32[1024]{0:T(1024)}, u32[]{:S(2)}) copy-start(s32[1024]{0:T(1024)} %param.14) | copy-start | bytes 12292
  12.5 115.0 %copy-start.2 = (f32[16,64,256]{2,1,0:T(8,128)S(1)}, f32[16,64,256]{2,1,0:T(8,128)}, u32[]{:S(2)}) copy-start(f32[16,64,256]{2,1,0:T(8,128)} %param.10) | copy-start | bytes 3145732
  12.5 115.0 %all-to-all-start = ((bf16[64,136,256]{2,1,0:T(8,128)(2,1)}), bf16[64,136,256]{2,1,0:T(8,128)(2,1)}, u32[]{:S(2)}, u32[]{:S(2)}) async-start(bf16[64,136,256]{2,1,0:T(8,128)(2,1)} %bitcast.9), calls=%async_computation | async-start | bytes 8912896 | tf_op jit(solution)/shard_map/all_to_all | solution.py:34
  147.9 19.4 %all-to-all-start.1 = ((s16[4,1088,128]{2,1,0:T(8,128)(2,1)}), s16[4,1088,128]{2,1,0:T(8,128)(2,1)S(1)}, u32[]{:S(2)}, u32[]{:S(2)}) async-start(s16[4,1088,128]{2,1,0:T(8,128)(2,1)} %shard_map.106), calls=%async_computation.1 | async-start | bytes 2228224 | tf_op jit(solution)/shard_map/all_to_all | solution.py:34
  151.9 6.5 %collective-permute-start = (f32[16,256]{1,0:T(8,128)S(1)}, f32[16,256]{1,0:T(8,128)S(1)}, u32[]{:S(2)}, u32[]{:S(2)}) collective-permute-start(f32[16,256]{1,0:T(8,128)S(1)} %get-tuple-element.12), channel_id=1, source_target_pairs={{0,32},{4,36},{8,40},{12,44},{16,48},{20,52},{24,56},{28,60},{32,0... | collective-permute-start | bytes 49160 | tf_op jit(solution)/shard_map/ppermute | solution.py:410
  158.4 4.0 %collective-permute-start.1 = (f32[32,256]{1,0:T(8,128)S(1)}, f32[32,256]{1,0:T(8,128)S(1)}, u32[]{:S(2)}, u32[]{:S(2)}) collective-permute-start(f32[32,256]{1,0:T(8,128)S(1)} %pad_maximum_fusion.2), channel_id=1, source_target_pairs={{0,16},{4,20},{8,24},{12,28},{16,0},{20,4},{24,8},{28,12},{32,48},... | collective-permute-start | bytes 98312 | tf_op jit(solution)/shard_map/ppermute | solution.py:410
  162.4 12.8 %collective-permute-start.2 = (f32[64,256]{1,0:T(8,128)S(1)}, f32[64,256]{1,0:T(8,128)S(1)}, u32[]{:S(2)}, u32[]{:S(2)}) collective-permute-start(f32[64,256]{1,0:T(8,128)S(1)} %pad_maximum_fusion.1), channel_id=1, source_target_pairs={{0,8},{4,12},{8,0},{12,4},{16,24},{20,28},{24,16},{28,20},{32,40},... | collective-permute-start | bytes 196616 | tf_op jit(solution)/shard_map/ppermute | solution.py:410
  168.5 26.7 %copy-start.5 = (s32[64]{0:T(128)S(1)}, s32[64]{0:T(128)}, u32[]{:S(2)}) copy-start(s32[64]{0:T(128)} %constant.6.clone) | copy-start | bytes 772
  168.5 26.7 %copy-start.1 = (s32[4096,1]{0,1:T(1,128)S(1)}, s32[4096,1]{0,1:T(1,128)}, u32[]{:S(2)}) copy-start(s32[4096,1]{0,1:T(1,128)} %param.11) | copy-start | bytes 49156
  168.5 26.8 %copy-start.3 = (s32[1,4096]{1,0:T(1,128)S(1)}, s32[1,4096]{1,0:T(1,128)}, u32[]{:S(2)}) copy-start(s32[1,4096]{1,0:T(1,128)} %get-tuple-element.18.target_ref) | copy-start | bytes 49156
  168.5 26.7 %all-to-all-start.2 = ((f32[64,16,128]{2,1,0:T(8,128)}), f32[64,16,128]{2,1,0:T(8,128)S(1)}, u32[]{:S(2)}, u32[]{:S(2)}) async-start(f32[64,16,128]{2,1,0:T(8,128)} %shard_map.107), calls=%async_computation.2 | async-start | bytes 1048576 | tf_op jit(solution)/shard_map/all_to_all | solution.py:34
  175.2 7.6 %collective-permute-start.3 = (f32[128,256]{1,0:T(8,128)S(1)}, f32[128,256]{1,0:T(8,128)S(1)}, u32[]{:S(2)}, u32[]{:S(2)}) collective-permute-start(f32[128,256]{1,0:T(8,128)S(1)} %pad_maximum_fusion), channel_id=1, source_target_pairs={{0,128},{4,132},{8,136},{12,140},{16,144},{20,148},{24,152},{28,15... | collective-permute-start | bytes 393224 | tf_op jit(solution)/shard_map/ppermute | solution.py:410
  183.6 9.2 %collective-permute-start.4 = (f32[256,256]{1,0:T(8,128)}, f32[256,256]{1,0:T(8,128)S(1)}, u32[]{:S(2)}, u32[]{:S(2)}) collective-permute-start(f32[256,256]{1,0:T(8,128)} %get-tuple-element.23), channel_id=1, source_target_pairs={{0,64},{4,68},{8,72},{12,76},{16,80},{20,84},{24,88},{28,92},{32,9... | collective-permute-start | bytes 786440 | tf_op jit(solution)/shard_map/ppermute | solution.py:410
  193.5 12.8 %collective-permute-start.5 = (f32[512,256]{1,0:T(8,128)}, f32[512,256]{1,0:T(8,128)S(1)}, u32[]{:S(2)}, u32[]{:S(2)}) collective-permute-start(f32[512,256]{1,0:T(8,128)} %get-tuple-element.19), channel_id=1, source_target_pairs={{0,4},{4,0},{8,12},{12,8},{16,20},{20,16},{24,28},{28,24},{32,36},... | collective-permute-start | bytes 1572872 | tf_op jit(solution)/shard_map/ppermute | solution.py:410
  202.2 13.4 %all-to-all-start.3 = ((s16[4,544,128]{2,1,0:T(8,128)(2,1)}), s16[4,544,128]{2,1,0:T(8,128)(2,1)S(1)}, u32[]{:S(2)}, u32[]{:S(2)}) async-start(s16[4,544,128]{2,1,0:T(8,128)(2,1)} %shard_map.108), calls=%async_computation.3 | async-start | bytes 1114112 | tf_op jit(solution)/shard_map/all_to_all | solution.py:34

commit v5 on v4

--- a/solution.py
+++ b/solution.py
@@ -58,6 +58,21 @@
 
 def scale_of(power):
     return jnp.exp2(power.astype(jnp.int32).astype(jnp.float32) - 16.0)
+
+
+def floated(value):
+    power = jnp.floor(jnp.log2(jnp.maximum(value, 2.0**-21)))
+    power = jnp.clip(power, -21.0, 9.0)
+    code = 2048.0 * (power + 21.0) + jnp.round(value * jnp.exp2(-power) * 2048.0)
+    code = jnp.minimum(code, 65535.0).astype(jnp.int32)
+    half = value.shape[0] // 2
+    return code[:half] | (code[half:] << 16)
+
+
+def unfloated(code):
+    octave = jnp.maximum((code >> 11) - 1, 0)
+    mantissa = (code - (octave << 11)).astype(jnp.float32)
+    return mantissa * jnp.exp2(octave.astype(jnp.float32) - 32.0)
 
 
 def send_body(capacity, stride, chunks, unroll):
@@ -148,14 +163,11 @@
 
 
 def sums_body(slots, per_cluster):
-    def body(rows_hbm, coarse_ref, fine_ref, coarse_out, fine_out, cand_out, norm_out,
-             held_out, square_out, totals, counts, labels, rows_ref, done):
+    def body(rows_ref, coarse_ref, fine_ref, coarse_out, fine_out, cand_out, norm_out,
+             held_out, square_out, totals, counts, labels):
         columns = slots * per_cluster
         blocks, stride, _ = rows_ref.shape
-        group = blocks // CHUNKS
-        copies = fetches(rows_hbm, rows_ref, done, group)
-        for copy in copies:
-            copy.start()
+        group = 16
         totals[...] = jnp.zeros_like(totals)
         counts[...] = jnp.zeros_like(counts)
 
@@ -167,6 +179,8 @@
             held_out[here, :] = slot.astype(jnp.int32) - 1
             square_out[here, :] = (meta[1:2, :LANES] + meta[1:2, LANES:]) + meta[2:3, :LANES]
             return carry
+
+        lax.fori_loop(0, blocks, read, 0, unroll=4)
 
         ids = iota((columns, LANES), 0).astype(jnp.int16)
         one, zero = jnp.bfloat16(1.0), jnp.bfloat16(0.0)
@@ -188,10 +202,7 @@
             )
             return carry
 
-        for chunk, copy in enumerate(copies):
-            copy.wait()
-            lax.fori_loop(chunk * group, (chunk + 1) * group, read, 0, unroll=True)
-            add(chunk, 0)
+        lax.fori_loop(0, blocks // group, add, 0)
         for slot in range(slots):
             part = pl.ds(slot * per_cluster, per_cluster)
             sum_f = totals[part, :]
@@ -263,10 +274,11 @@
     return body
 
 
-def total_body():
+def total_body(features):
     def body(got_ref, out_ref, scales):
-        blocks, quarter, _ = out_ref.shape
+        blocks, half, _ = out_ref.shape
         pieces = got_ref.shape[0]
+        quarter = 2 * half
         for piece in range(pieces):
             scales[piece] = scale_of(got_ref[piece, blocks * quarter :, :])
 
@@ -275,17 +287,17 @@
             value = decoded(got_ref[0, here, :], scales[0, pl.ds(block, 1), :])
             for piece in range(1, pieces):
                 value = value + decoded(got_ref[piece, here, :], scales[piece, pl.ds(block, 1), :])
-            out_ref[block] = value
-            return carry
-
-        lax.fori_loop(0, blocks, one, 0, unroll=4)
-
-    return body
-
-
-def pick_body(stride, features):
-    def body(got_ref, owner_ref, target_ref, out_ref, powers):
-        owners, quarter, _ = got_ref.shape
+            out_ref[block] = floated(value * (1.0 / features))
+            return carry
+
+        lax.fori_loop(0, blocks, one, 0, unroll=8)
+
+    return body
+
+
+def pick_body(stride):
+    def body(got_ref, owner_ref, target_ref, out_ref):
+        owners, half, _ = got_ref.shape
         copies = out_ref.shape[0]
         groups = owner_ref.shape[1] // LANES
 
@@ -293,37 +305,31 @@
             here = pl.ds(pl.multiple_of(index * LANES, LANES), LANES)
             owner = owner_ref[:, here]
             place = target_ref[:, here] - owner * stride
-            place = jnp.broadcast_to(place, (quarter, LANES))
-            owner = jnp.broadcast_to(owner, (quarter, LANES))
-            value = jnp.zeros((quarter, LANES), jnp.float32)
+            place = jnp.broadcast_to(place, (half, LANES))
+            owner = jnp.broadcast_to(owner, (half, LANES))
+            value = jnp.zeros((half, LANES), jnp.int32)
             for number in range(owners):
-                found = jnp.take_along_axis(got_ref[number], place, axis=1, mode="promise_in_bounds")
+                found = jnp.take_along_axis(
+                    got_ref[number], place, axis=1, mode="promise_in_bounds"
+                )
                 value = jnp.where(owner == number, found, value)
-            code, power = coded(value * (1.0 / features))
-            powers[pl.ds(index, 1), :] = power
             for copy in range(copies):
-                out_ref[copy, pl.ds(pl.multiple_of(index * quarter, quarter), quarter), :] = code
-            return carry
-
-        lax.fori_loop(0, groups, one, 0, unroll=2)
-        for copy in range(copies):
-            out_ref[copy, groups * quarter :, :] = powers[...].astype(jnp.int32).astype(jnp.int16)
-
-    return body
-
-
-def spread_body(quarter):
+                out_ref[copy, :, here] = value
+            return carry
+
+        lax.fori_loop(0, groups, one, 0, unroll=4)
+
+    return body
+
+
+def spread_body():
     def body(got_ref, out_ref):
-        groups = out_ref.shape[1] // LANES
-        for piece in range(got_ref.shape[0]):
-            scales = scale_of(got_ref[piece, groups * quarter :, :])
-            for group in range(groups):
-                out_ref[piece * quarter : (piece + 1) * quarter, group * LANES : (group + 1) * LANES] = (
-                    decoded(
-                        got_ref[piece, group * quarter : (group + 1) * quarter, :],
-                        scales[group : group + 1],
-                    )
-                )
+        pieces, half, _ = got_ref.shape
+        for piece in range(pieces):
+            code = got_ref[piece]
+            for part, value in enumerate((code & 65535, lax.shift_right_logical(code, 16))):
+                start = (2 * piece + part) * half
+                out_ref[start : start + half, :] = unfloated(value)
 
     return body
 
@@ -356,7 +362,6 @@
     shape = jax.ShapeDtypeStruct
 
     i16 = jnp.int16
-    groups = tokens // LANES
     owner = owner_of.reshape(1, tokens)
     slot, part = slot_in_owner.reshape(1, tokens), fine_in_cluster.reshape(1, tokens)
     target, send_rows = call(
@@ -393,14 +398,12 @@
             shape((owners, LANES), i32),
             shape((owners, LANES), f32),
         ),
-        [HBM, VMEM, VMEM],
+        [VMEM] * 3,
         flops=2 * total * columns * width,
         scratch=[
             pltpu.VMEM((columns, width), f32),
             pltpu.VMEM((columns, LANES), f32),
             pltpu.VMEM((owners, LANES), i32),
-            pltpu.VMEM((owners, stride, width), bf16),
-            pltpu.SemaphoreType.DMA((CHUNKS,)),
         ],
         mem=32 << 20,
     )(rows, coarse_init[mine], fine_init.reshape(columns, width))
@@ -424,19 +427,18 @@
     )(rows, held, square, cand, norms)
     arrived = exchanged(partial, "grp")
     share = call(
-        total_body(),
-        shape((owners, quarter, capacity), f32),
+        total_body(features),
+        shape((owners, quarter // 2, capacity), i32),
         [VMEM],
         flops=2_000_000_000,
         scratch=[pltpu.VMEM((pieces, owners, LANES), f32)],
     )(arrived)
     returned = exchanged(share, "dp")
     spread = call(
-        pick_body(stride, features),
-        shape((pieces, groups * quarter + groups, LANES), i16),
+        pick_body(stride),
+        shape((pieces, quarter // 2, tokens), i32),
         [VMEM] * 3,
         flops=4_000_000_000,
-        scratch=[pltpu.VMEM((groups, LANES), f32)],
     )(returned, owner, target)
     codes = exchanged(spread, "grp")
     coarse_out = call(
@@ -446,7 +448,7 @@
         flops=2_000_000_000,
     )(cluster_at, gathered)
     distances = call(
-        spread_body(quarter), shape((per_cluster, tokens), f32), [VMEM], flops=10_000_000
+        spread_body(), shape((per_cluster, tokens), f32), [VMEM], flops=10_000_000
     )(codes)
     return (coarse_out, fine.reshape(slots, per_cluster, width), distances)
 

time: 217 us -> 211 us (0.972)
  waiting for transfers between devices: 128 us -> 121 us
  Pallas kernels: 46.8 us -> 42.2 us
  starting transfers between devices: 35.9 us -> 39.2 us
    ppermute x6, waiting for transfers between devices: 18.9 us -> 7.75 us  [shards(): other = lax.ppermute(gathered, 'dp', [(i, i ^ bit) for i in range(owners)])]
    all_to_all x4, starting transfers between devices: 27.6 us -> 33.6 us  [exchanged(): return lax.all_to_all(array, axis, split_axis=0, concat_axis=0, tiled=True)]
    all_to_all x4, waiting for transfers between devices: 109 us -> 113 us  [exchanged(): return lax.all_to_all(array, axis, split_axis=0, concat_axis=0, tiled=True)]
    pallas_call x3, Pallas kernels: 9.3 us -> 6.56 us  [the longest x1 3.66 us: shards(): call(pick_body(stride), shape((pieces, quarter // 2, tokens), i32), [VMEM...]
    ppermute x6, starting transfers between devices: 8.3 us -> 5.64 us  [shards(): other = lax.ppermute(gathered, 'dp', [(i, i ^ bit) for i in range(owners)])]
  transfers between devices with their start and end apart: 10 -> 10, of which waited for: 7 -> 6; matrix products, arithmetic and copies ran while one was open for 3% -> 3% of each run, Pallas kernels for 6% -> 9%
where the time goes in v5:
time: 211 us; the launch traced here: 210 us
  waiting for transfers between devices  121 us (57%)
  Pallas kernels  42.2 us (20%)
  starting transfers between devices  39.2 us (19%)
  local copies, waits for them, and re-layouts  7.13 us (3%)
    all_to_all x4, waiting for transfers between devices, exchanged(): return lax.all_to_all(array, axis, split_axis=0, concat_axis=0, tiled=True)  113 us
    all_to_all x4, starting transfers between devices, exchanged(): return lax.all_to_all(array, axis, split_axis=0, concat_axis=0, tiled=True)  33.6 us
    pallas_call x1, Pallas kernels, shards(): call(send_body(capacity, stride, 4, 32), (shape((1, tokens), i32), shape(...  11.8 us
    pallas_call x1, Pallas kernels, shards(): call(sums_body(slots, per_cluster), (shape((slots, width), f32), shape((c...  10.1 us
    pallas_call x1, Pallas kernels, shards(): call(distance_body(slots, per_cluster), shape((pieces, owners * quarter +...  8.45 us
    ppermute x6, waiting for transfers between devices, shards(): other = lax.ppermute(gathered, 'dp', [(i, i ^ bit) for i in range(owners)])  7.75 us
    ppermute x6, starting transfers between devices, shards(): other = lax.ppermute(gathered, 'dp', [(i, i ^ bit) for i in range(owners)])  5.64 us
    pallas_call x1, Pallas kernels, shards(): call(arrange_body(), shape((owners * slots, width), f32), [SMEM, VMEM], f...  5.27 us
  transfers between devices with their start and end apart: 10, of which 6 were waited for; matrix products, arithmetic and copies ran while one was open for 3% of the time, Pallas kernels for 9%

profile of v5, /device:TPU:1, one launch (start us, length us, event | category | flops | bytes accessed | tf_op | source)
XLA Modules:
  0.0 210.5 jit_solution(11567603286037840827)
XLA Ops:
  0.6 0.0 copy-start
  0.6 11.8 %shard_map.103 = (s32[1,4096]{1,0:T(1,128)}, bf16[8704,256]{1,0:T(8,128)(2,1)}) custom-call(s32[1,4096]{1,0:T(1,128)} %bitcast.6, s32[1,4096]{1,0:T(1,128)} %bitcast.10, s32[1,4096]{1,0:T(1,128)} %bitcast.11, bf16[4096,256]{1,0:T(8,128)(2,1)} %rows_hbm.1), custom_call_target="tpu_custom_call" | custom-call | flops 400000000 | bytes 4194304 | tf_op jit(solution)/shard_map/pallas_call | solution.py:367
  12.5 0.0 copy-start.4
  12.5 0.0 copy-start.2
  12.5 13.5 %all-to-all-start = ((bf16[64,136,256]{2,1,0:T(8,128)(2,1)}), bf16[64,136,256]{2,1,0:T(8,128)(2,1)}, u32[]{:S(2)}, u32[]{:S(2)}) async-start(bf16[64,136,256]{2,1,0:T(8,128)(2,1)} %bitcast.9), calls=%async_computation | async-start | bytes 8912896 | tf_op jit(solution)/shard_map/all_to_all | solution.py:34
  25.9 0.0 copy-done.4
  26.0 0.1 compare_select_fusion
  26.0 0.0 copy-done
  26.0 0.6 gather_fusion.1
  26.6 100.8 %all-to-all-done.rows_ref.rows_hbm = bf16[64,136,256]{2,1,0:T(8,128)(2,1)} async-done(((bf16[64,136,256]{2,1,0:T(8,128)(2,1)}), bf16[64,136,256]{2,1,0:T(8,128)(2,1)}, u32[]{:S(2)}, u32[]{:S(2)}) %all-to-all-start) | async-done | bytes 4456480 | tf_op jit(solution)/shard_map/all_to_all | solution.py:34
  127.4 0.0 copy-done.2
  127.4 10.1 %shard_map.104 = (f32[16,256]{1,0:T(8,128)S(1)}, f32[1024,256]{1,0:T(8,128)}, bf16[1024,256]{1,0:T(8,128)(2,1)S(1)}, f32[1024,128]{1,0:T(8,128)S(1)}, s32[64,128]{1,0:T(8,128)S(1)}, /*index=5*/f32[64,128]{1,0:T(8,128)S(1)}) custom-call(bf16[64,136,256]{2,1,0:T(8,128)(2,1)} %all-to-all-done.rows_ref.rows_hbm, f32[16,256]{1,0:T(8,128)S(1)} %gather_fusion.1, ...), custom_call_target="tpu_custom_call" | custom-call | flops 4294967296 | bytes 4194304 | tf_op jit(solution)/shard_map/pallas_call | solution.py:391
  137.6 2.1 collective-permute-start
  139.7 8.5 %shard_map.106 = s16[4,1088,128]{2,1,0:T(8,128)(2,1)} custom-call(bf16[64,136,256]{2,1,0:T(8,128)(2,1)} %all-to-all-done.rows_ref.rows_hbm, s32[64,128]{1,0:T(8,128)S(1)} %get-tuple-element.14.held_ref, f32[64,128]{1,0:T(8,128)S(1)} %get-tuple-element.15.square_ref, bf16[1024,256]{1,0:T(8,128)(2,1)S(1)} %get-tuple-element.16.cand_ref, ...), custom_call_target="tpu_custom_call" | custom-call | flops 4294967296 | bytes 4194304 | tf_op jit(solution)/shard_map/pallas_call | solution.py:416
  148.1 4.0 %all-to-all-start.1 = ((s16[4,1088,128]{2,1,0:T(8,128)(2,1)}), s16[4,1088,128]{2,1,0:T(8,128)(2,1)S(1)}, u32[]{:S(2)}, u32[]{:S(2)}) async-start(s16[4,1088,128]{2,1,0:T(8,128)(2,1)} %shard_map.106), calls=%async_computation.1 | async-start | bytes 2228224 | tf_op jit(solution)/shard_map/all_to_all | solution.py:34
  152.2 0.0 collective-permute-done
  152.2 1.3 collective-permute-start.1
  153.4 0.6 constant_dynamic-update-slice_fusion.10
  154.0 2.2 %collective-permute-done.1 = f32[32,256]{1,0:T(8,128)S(1)} collective-permute-done((f32[32,256]{1,0:T(8,128)S(1)}, f32[32,256]{1,0:T(8,128)S(1)}, u32[]{:S(2)}, u32[]{:S(2)}) %collective-permute-start.1) | collective-permute-done | bytes 32800 | tf_op jit(solution)/shard_map/ppermute | solution.py:413
  156.3 0.1 collective-permute-start.2
  156.4 0.6 constant_dynamic-update-slice_fusion.9
  157.0 2.7 %collective-permute-done.2 = f32[64,256]{1,0:T(8,128)S(1)} collective-permute-done((f32[64,256]{1,0:T(8,128)S(1)}, f32[64,256]{1,0:T(8,128)S(1)}, u32[]{:S(2)}, u32[]{:S(2)}) %collective-permute-start.2) | collective-permute-done | bytes 65568 | tf_op jit(solution)/shard_map/ppermute | solution.py:413
  159.7 1.6 collective-permute-start.3
  161.3 0.6 constant_dynamic-update-slice_fusion.8
  161.9 0.6 constant_dynamic-update-slice_fusion.7
  162.6 2.8 %collective-permute-done.3 = f32[128,256]{1,0:T(8,128)S(1)} collective-permute-done((f32[128,256]{1,0:T(8,128)S(1)}, f32[128,256]{1,0:T(8,128)S(1)}, u32[]{:S(2)}, u32[]{:S(2)}) %collective-permute-start.3) | collective-permute-done | bytes 131104 | tf_op jit(solution)/shard_map/ppermute | solution.py:413
  165.4 0.7 constant_dynamic-update-slice_fusion.6
  166.1 0.8 copy-done.5
  166.9 0.1 collective-permute-start.4
  167.0 0.0 all-to-all-done.1.got_ref
  167.0 1.5 shard_map.107
  168.5 11.8 %all-to-all-start.2 = ((s32[64,8,128]{2,1,0:T(8,128)}), s32[64,8,128]{2,1,0:T(8,128)S(1)}, u32[]{:S(2)}, u32[]{:S(2)}) async-start(s32[64,8,128]{2,1,0:T(8,128)} %shard_map.107), calls=%async_computation.2 | async-start | bytes 524288 | tf_op jit(solution)/shard_map/all_to_all | solution.py:34
  180.4 0.0 collective-permute-done.4
  180.4 0.7 constant_dynamic-update-slice_fusion.5
  181.1 0.5 collective-permute-start.5
  181.6 0.0 copy-done.6
  181.6 0.1 reshape.30
  181.7 10.7 %all-to-all-done.2.got_ref = s32[64,8,128]{2,1,0:T(8,128)S(1)} async-done(((s32[64,8,128]{2,1,0:T(8,128)}), s32[64,8,128]{2,1,0:T(8,128)S(1)}, u32[]{:S(2)}, u32[]{:S(2)}) %all-to-all-start.2) | async-done | bytes 262176 | tf_op jit(solution)/shard_map/all_to_all | solution.py:34
  192.3 0.0 copy-done.1
  192.3 3.7 %shard_map.108 = s32[4,8,4096]{2,1,0:T(8,128)} custom-call(s32[64,8,128]{2,1,0:T(8,128)S(1)} %all-to-all-done.2.got_ref, s32[1,4096]{1,0:T(1,128)S(1)} %bitcast.7, s32[1,4096]{1,0:T(1,128)S(1)} %copy-done.3), custom_call_target="tpu_custom_call" | custom-call | flops 4000000000 | bytes 4194304 | tf_op jit(solution)/shard_map/pallas_call | solution.py:437
  196.0 4.3 %all-to-all-start.3 = ((s32[4,8,4096]{2,1,0:T(8,128)}), s32[4,8,4096]{2,1,0:T(8,128)S(1)}, u32[]{:S(2)}, u32[]{:S(2)}) async-start(s32[4,8,4096]{2,1,0:T(8,128)} %shard_map.108), calls=%async_computation.3 | async-start | bytes 1048576 | tf_op jit(solution)/shard_map/all_to_all | solution.py:34
  200.3 0.6 gather_fusion
  200.9 0.1 reshape.31.cluster_ref
  200.9 0.0 collective-permute-done.5
  201.0 1.1 constant_dynamic-update-slice_fusion.11.rows_ref
  202.0 5.3 %shard_map.105 = f32[1024,256]{1,0:T(8,128)} custom-call(s32[1024]{0:T(1024)S(1)} %reshape.31.cluster_ref, f32[1024,256]{1,0:T(8,128)S(1)} %constant_dynamic-update-slice_fusion.11.rows_ref), custom_call_target="tpu_custom_call" | custom-call | flops 2000000000 | bytes 4194304 | tf_op jit(solution)/shard_map/pallas_call | solution.py:444
  207.3 1.8 all-to-all-done.3.got_ref
  209.1 1.4 shard_map.109
  (11 shorter events, 0.0 us)
Async XLA Ops:
  0.6 25.4 %copy-start = (f32[1024,256]{1,0:T(8,128)S(1)}, f32[1024,256]{1,0:T(8,128)}, u32[]{:S(2)}) copy-start(f32[1024,256]{1,0:T(8,128)} %param.9) | copy-start | bytes 3145732
  12.5 13.5 %copy-start.4 = (s32[1024]{0:T(1024)S(1)}, s32[1024]{0:T(1024)}, u32[]{:S(2)}) copy-start(s32[1024]{0:T(1024)} %param.14) | copy-start | bytes 12292
  12.5 115.0 %copy-start.2 = (f32[16,64,256]{2,1,0:T(8,128)S(1)}, f32[16,64,256]{2,1,0:T(8,128)}, u32[]{:S(2)}) copy-start(f32[16,64,256]{2,1,0:T(8,128)} %param.10) | copy-start | bytes 3145732
  12.5 115.0 %all-to-all-start = ((bf16[64,136,256]{2,1,0:T(8,128)(2,1)}), bf16[64,136,256]{2,1,0:T(8,128)(2,1)}, u32[]{:S(2)}, u32[]{:S(2)}) async-start(bf16[64,136,256]{2,1,0:T(8,128)(2,1)} %bitcast.9), calls=%async_computation | async-start | bytes 8912896 | tf_op jit(solution)/shard_map/all_to_all | solution.py:34
  137.6 14.6 %collective-permute-start = (f32[16,256]{1,0:T(8,128)S(1)}, f32[16,256]{1,0:T(8,128)S(1)}, u32[]{:S(2)}, u32[]{:S(2)}) collective-permute-start(f32[16,256]{1,0:T(8,128)S(1)} %get-tuple-element.12), channel_id=1, source_target_pairs={{0,32},{4,36},{8,40},{12,44},{16,48},{20,52},{24,56},{28,60},{32,0... | collective-permute-start | bytes 49160 | tf_op jit(solution)/shard_map/ppermute | solution.py:413
  148.1 18.9 %all-to-all-start.1 = ((s16[4,1088,128]{2,1,0:T(8,128)(2,1)}), s16[4,1088,128]{2,1,0:T(8,128)(2,1)S(1)}, u32[]{:S(2)}, u32[]{:S(2)}) async-start(s16[4,1088,128]{2,1,0:T(8,128)(2,1)} %shard_map.106), calls=%async_computation.1 | async-start | bytes 2228224 | tf_op jit(solution)/shard_map/all_to_all | solution.py:34
  152.2 4.1 %collective-permute-start.1 = (f32[32,256]{1,0:T(8,128)S(1)}, f32[32,256]{1,0:T(8,128)S(1)}, u32[]{:S(2)}, u32[]{:S(2)}) collective-permute-start(f32[32,256]{1,0:T(8,128)S(1)} %pad_maximum_fusion.2), channel_id=1, source_target_pairs={{0,16},{4,20},{8,24},{12,28},{16,0},{20,4},{24,8},{28,12},{32,48},... | collective-permute-start | bytes 98312 | tf_op jit(solution)/shard_map/ppermute | solution.py:413
  156.3 3.4 %collective-permute-start.2 = (f32[64,256]{1,0:T(8,128)S(1)}, f32[64,256]{1,0:T(8,128)S(1)}, u32[]{:S(2)}, u32[]{:S(2)}) collective-permute-start(f32[64,256]{1,0:T(8,128)S(1)} %pad_maximum_fusion.1), channel_id=1, source_target_pairs={{0,8},{4,12},{8,0},{12,4},{16,24},{20,28},{24,16},{28,20},{32,40},... | collective-permute-start | bytes 196616 | tf_op jit(solution)/shard_map/ppermute | solution.py:413
  159.7 5.7 %collective-permute-start.3 = (f32[128,256]{1,0:T(8,128)S(1)}, f32[128,256]{1,0:T(8,128)S(1)}, u32[]{:S(2)}, u32[]{:S(2)}) collective-permute-start(f32[128,256]{1,0:T(8,128)S(1)} %pad_maximum_fusion), channel_id=1, source_target_pairs={{0,128},{4,132},{8,136},{12,140},{16,144},{20,148},{24,152},{28,15... | collective-permute-start | bytes 393224 | tf_op jit(solution)/shard_map/ppermute | solution.py:413
  166.1 0.8 copy-start.5
  166.9 14.7 %copy-start.6 = (s32[64]{0:T(128)S(1)}, s32[64]{0:T(128)}, u32[]{:S(2)}) copy-start(s32[64]{0:T(128)} %constant.6.clone) | copy-start | bytes 772
  166.9 25.4 %copy-start.1 = (s32[4096,1]{0,1:T(1,128)S(1)}, s32[4096,1]{0,1:T(1,128)}, u32[]{:S(2)}) copy-start(s32[4096,1]{0,1:T(1,128)} %param.11) | copy-start | bytes 49156
  166.9 25.4 %copy-start.3 = (s32[1,4096]{1,0:T(1,128)S(1)}, s32[1,4096]{1,0:T(1,128)}, u32[]{:S(2)}) copy-start(s32[1,4096]{1,0:T(1,128)} %get-tuple-element.18.target_ref) | copy-start | bytes 49156
  166.9 13.5 %collective-permute-start.4 = (f32[256,256]{1,0:T(8,128)}, f32[256,256]{1,0:T(8,128)S(1)}, u32[]{:S(2)}, u32[]{:S(2)}) collective-permute-start(f32[256,256]{1,0:T(8,128)} %get-tuple-element.23), channel_id=1, source_target_pairs={{0,64},{4,68},{8,72},{12,76},{16,80},{20,84},{24,88},{28,92},{32,9... | collective-permute-start | bytes 786440 | tf_op jit(solution)/shard_map/ppermute | solution.py:413
  168.5 23.8 %all-to-all-start.2 = ((s32[64,8,128]{2,1,0:T(8,128)}), s32[64,8,128]{2,1,0:T(8,128)S(1)}, u32[]{:S(2)}, u32[]{:S(2)}) async-start(s32[64,8,128]{2,1,0:T(8,128)} %shard_map.107), calls=%async_computation.2 | async-start | bytes 524288 | tf_op jit(solution)/shard_map/all_to_all | solution.py:34
  181.1 19.8 %collective-permute-start.5 = (f32[512,256]{1,0:T(8,128)}, f32[512,256]{1,0:T(8,128)}, u32[]{:S(2)}, u32[]{:S(2)}) collective-permute-start(f32[512,256]{1,0:T(8,128)} %get-tuple-element.19), channel_id=1, source_target_pairs={{0,4},{4,0},{8,12},{12,8},{16,20},{20,16},{24,28},{28,24},{32,36},... | collective-permute-start | bytes 1572872 | tf_op jit(solution)/shard_map/ppermute | solution.py:413
  196.0 13.1 %all-to-all-start.3 = ((s32[4,8,4096]{2,1,0:T(8,128)}), s32[4,8,4096]{2,1,0:T(8,128)S(1)}, u32[]{:S(2)}, u32[]{:S(2)}) async-start(s32[4,8,4096]{2,1,0:T(8,128)} %shard_map.108), calls=%async_computation.3 | async-start | bytes 1048576 | tf_op jit(solution)/shard_map/all_to_all | solution.py:34

commit v6 on v5

--- a/solution.py
+++ b/solution.py
@@ -154,14 +154,6 @@
     return body
 
 
-def fetches(rows_hbm, rows, done, group):
-    copies = []
-    for chunk in range(rows.shape[0] // group):
-        part = pl.ds(chunk * group, group)
-        copies.append(pltpu.make_async_copy(rows_hbm.at[part], rows.at[part], done.at[chunk]))
-    return copies
-
-
 def sums_body(slots, per_cluster):
     def body(rows_ref, coarse_ref, fine_ref, coarse_out, fine_out, cand_out, norm_out,
              held_out, square_out, totals, counts, labels):
@@ -229,14 +221,11 @@
 
 
 def distance_body(slots, per_cluster):
-    def body(rows_hbm, held_ref, square_ref, cand_ref, norm_ref, out_ref, powers, rows_ref, done):
+    def body(rows_ref, held_ref, square_ref, cand_ref, norm_ref, out_ref, powers):
         blocks = rows_ref.shape[0]
         pieces = out_ref.shape[0]
         quarter = per_cluster // pieces
         group, pair = blocks // CHUNKS, 2
-        copies = fetches(rows_hbm, rows_ref, done, group)
-        for copy in copies:
-            copy.start()
 
         def one(index, carry):
             for first in range(0, group, pair):
@@ -265,11 +254,23 @@
                         )
             return carry
 
-        for chunk, copy in enumerate(copies):
-            copy.wait()
+        for chunk in range(CHUNKS):
             one(chunk, 0)
         for piece in range(pieces):
             out_ref[piece, blocks * quarter :, :] = powers[...].astype(jnp.int32).astype(jnp.int16)
+
+    return body
+
+
+def update_body(slots, per_cluster):
+    sums = sums_body(slots, per_cluster)
+    distances = distance_body(slots, per_cluster)
+
+    def body(rows_ref, coarse_ref, fine_ref, coarse_out, fine_out, out_ref,
+             totals, counts, labels, cand, norm, held, square, powers):
+        sums(rows_ref, coarse_ref, fine_ref, coarse_out, fine_out, cand, norm, held, square,
+             totals, counts, labels)
+        distances(rows_ref, held, square, cand, norm, out_ref, powers)
 
     return body
 
@@ -388,24 +389,26 @@
     order = jnp.bitwise_xor(jnp.array(masks, i32), lax.axis_index("dp"))
     cluster_at = slot_cluster.reshape(owners, slots)[order].reshape(owners * slots)
     mine = lax.dynamic_slice_in_dim(slot_cluster, lax.axis_index("dp") * slots, slots, 0)
-    coarse_mine, fine, cand, norms, held, square = call(
-        sums_body(slots, per_cluster),
+    coarse_mine, fine, partial = call(
+        update_body(slots, per_cluster),
         (
             shape((slots, width), f32),
             shape((columns, width), f32),
-            shape((columns, width), bf16),
-            shape((columns, LANES), f32),
-            shape((owners, LANES), i32),
-            shape((owners, LANES), f32),
+            shape((pieces, owners * quarter + owners, capacity), i16),
         ),
         [VMEM] * 3,
-        flops=2 * total * columns * width,
+        flops=4 * total * columns * width,
         scratch=[
             pltpu.VMEM((columns, width), f32),
             pltpu.VMEM((columns, LANES), f32),
             pltpu.VMEM((owners, LANES), i32),
+            pltpu.VMEM((columns, width), bf16),
+            pltpu.VMEM((columns, LANES), f32),
+            pltpu.VMEM((owners, LANES), i32),
+            pltpu.VMEM((owners, LANES), f32),
+            pltpu.VMEM((owners, LANES), f32),
         ],
-        mem=32 << 20,
+        mem=40 << 20,
     )(rows, coarse_init[mine], fine_init.reshape(columns, width))
 
     gathered = coarse_mine
@@ -413,18 +416,6 @@
         other = lax.ppermute(gathered, "dp", [(i, i ^ bit) for i in range(owners)])
         gathered = jnp.concatenate([gathered, other], axis=0)
 
-    partial = call(
-        distance_body(slots, per_cluster),
-        shape((pieces, owners * quarter + owners, capacity), i16),
-        [HBM, VMEM, VMEM, VMEM, VMEM],
-        flops=2 * total * columns * width,
-        scratch=[
-            pltpu.VMEM((owners, LANES), f32),
-            pltpu.VMEM((owners, stride, width), bf16),
-            pltpu.SemaphoreType.DMA((CHUNKS,)),
-        ],
-        mem=32 << 20,
-    )(rows, held, square, cand, norms)
     arrived = exchanged(partial, "grp")
     share = call(
         total_body(features),

time: 211 us -> 207 us (0.981)
  Pallas kernels: 42.2 us -> 38.7 us
    pallas_call x2 -> x1, Pallas kernels: 18.6 us -> 15 us  [shards(): call(update_body(slots, per_cluster), (shape((slots, width), f32), shape(...]
    ppermute x6, starting transfers between devices: 5.64 us -> 9.1 us  [shards(): other = lax.ppermute(gathered, 'dp', [(i, i ^ bit) for i in range(owners)])]
  transfers between devices with their start and end apart: 10 -> 10, of which waited for: 6 -> 7; matrix products, arithmetic and copies ran while one was open for 3% -> 3% of each run, Pallas kernels for 9% -> 5%
where the time goes in v6:
time: 207 us
  waiting for transfers between devices  119 us (57%)
  starting transfers between devices  40.9 us (20%)
  Pallas kernels  38.7 us (19%)
  local copies, waits for them, and re-layouts  7.13 us (3%)
    all_to_all x4, waiting for transfers between devices, exchanged(): return lax.all_to_all(array, axis, split_axis=0, concat_axis=0, tiled=True)  113 us
    all_to_all x4, starting transfers between devices, exchanged(): return lax.all_to_all(array, axis, split_axis=0, concat_axis=0, tiled=True)  31.8 us
    pallas_call x1, Pallas kernels, shards(): call(update_body(slots, per_cluster), (shape((slots, width), f32), shape(...  15 us
    pallas_call x1, Pallas kernels, shards(): call(send_body(capacity, stride, 4, 32), (shape((1, tokens), i32), shape(...  11.8 us
    ppermute x6, starting transfers between devices, shards(): other = lax.ppermute(gathered, 'dp', [(i, i ^ bit) for i in range(owners)])  9.1 us
    ppermute x6, waiting for transfers between devices, shards(): other = lax.ppermute(gathered, 'dp', [(i, i ^ bit) for i in range(owners)])  6.11 us
    pallas_call x1, Pallas kernels, shards(): call(arrange_body(), shape((owners * slots, width), f32), [SMEM, VMEM], f...  5.27 us
  transfers between devices with their start and end apart: 10, of which 7 were waited for; matrix products, arithmetic and copies ran while one was open for 3% of the time, Pallas kernels for 5%

profile of v6, /device:TPU:1, one launch (start us, length us, event | category | flops | bytes accessed | tf_op | source)
XLA Modules:
  0.0 206.9 jit_solution(3792838422055278790)
XLA Ops:
  0.6 0.0 copy-start
  0.6 11.8 %shard_map.103 = (s32[1,4096]{1,0:T(1,128)}, bf16[8704,256]{1,0:T(8,128)(2,1)}) custom-call(s32[1,4096]{1,0:T(1,128)} %bitcast.6, s32[1,4096]{1,0:T(1,128)} %bitcast.10, s32[1,4096]{1,0:T(1,128)} %bitcast.11, bf16[4096,256]{1,0:T(8,128)(2,1)} %rows_hbm.1), custom_call_target="tpu_custom_call" | custom-call | flops 400000000 | bytes 4194304 | tf_op jit(solution)/shard_map/pallas_call | solution.py:368
  12.5 0.0 copy-start.4
  12.5 0.0 copy-start.2
  12.5 13.5 %all-to-all-start = ((bf16[64,136,256]{2,1,0:T(8,128)(2,1)}), bf16[64,136,256]{2,1,0:T(8,128)(2,1)}, u32[]{:S(2)}, u32[]{:S(2)}) async-start(bf16[64,136,256]{2,1,0:T(8,128)(2,1)} %bitcast.9), calls=%async_computation | async-start | bytes 8912896 | tf_op jit(solution)/shard_map/all_to_all | solution.py:34
  25.9 0.0 copy-done.4
  26.0 0.1 compare_select_fusion
  26.0 0.0 copy-done
  26.0 0.6 gather_fusion.1
  26.6 100.8 %all-to-all-done.rows_ref = bf16[64,136,256]{2,1,0:T(8,128)(2,1)} async-done(((bf16[64,136,256]{2,1,0:T(8,128)(2,1)}), bf16[64,136,256]{2,1,0:T(8,128)(2,1)}, u32[]{:S(2)}, u32[]{:S(2)}) %all-to-all-start) | async-done | bytes 4456480 | tf_op jit(solution)/shard_map/all_to_all | solution.py:34
  127.4 0.0 copy-done.2
  127.4 15.0 %shard_map.104 = (f32[16,256]{1,0:T(8,128)S(1)}, f32[1024,256]{1,0:T(8,128)}, s16[4,1088,128]{2,1,0:T(8,128)(2,1)}) custom-call(bf16[64,136,256]{2,1,0:T(8,128)(2,1)} %all-to-all-done.rows_ref, f32[16,256]{1,0:T(8,128)S(1)} %gather_fusion.1, f32[1024,256]{1,0:T(8,128)S(1)} %bitcast.8), custom_call_target="tpu_custom_call" | custom-call | flops 8589934592 | bytes 4194304 | tf_op jit(solution)/shard_map/pallas_call | solution.py:392
  142.5 2.1 %collective-permute-start = (f32[16,256]{1,0:T(8,128)S(1)}, f32[16,256]{1,0:T(8,128)S(1)}, u32[]{:S(2)}, u32[]{:S(2)}) collective-permute-start(f32[16,256]{1,0:T(8,128)S(1)} %get-tuple-element.9), channel_id=1, source_target_pairs={{0,32},{4,36},{8,40},{12,44},{16,48},{20,52},{24,56},{28,60},{32,0... | collective-permute-start | bytes 49160 | tf_op jit(solution)/shard_map/ppermute | solution.py:416
  144.6 4.0 %all-to-all-start.1 = ((s16[4,1088,128]{2,1,0:T(8,128)(2,1)}), s16[4,1088,128]{2,1,0:T(8,128)(2,1)S(1)}, u32[]{:S(2)}, u32[]{:S(2)}) async-start(s16[4,1088,128]{2,1,0:T(8,128)(2,1)} %get-tuple-element.11), calls=%async_computation.1 | async-start | bytes 2228224 | tf_op jit(solution)/shard_map/all_to_all | solution.py:34
  148.6 0.4 collective-permute-done
  149.0 0.9 collective-permute-start.1
  149.9 0.6 constant_dynamic-update-slice_fusion.10
  150.5 2.2 %collective-permute-done.1 = f32[32,256]{1,0:T(8,128)S(1)} collective-permute-done((f32[32,256]{1,0:T(8,128)S(1)}, f32[32,256]{1,0:T(8,128)S(1)}, u32[]{:S(2)}, u32[]{:S(2)}) %collective-permute-start.1) | collective-permute-done | bytes 32800 | tf_op jit(solution)/shard_map/ppermute | solution.py:416
  152.7 0.6 collective-permute-start.2
  153.3 0.6 constant_dynamic-update-slice_fusion.9
  153.9 2.2 %collective-permute-done.2 = f32[64,256]{1,0:T(8,128)S(1)} collective-permute-done((f32[64,256]{1,0:T(8,128)S(1)}, f32[64,256]{1,0:T(8,128)S(1)}, u32[]{:S(2)}, u32[]{:S(2)}) %collective-permute-start.2) | collective-permute-done | bytes 65568 | tf_op jit(solution)/shard_map/ppermute | solution.py:416
  156.1 3.8 %collective-permute-start.3 = (f32[128,256]{1,0:T(8,128)S(1)}, f32[128,256]{1,0:T(8,128)S(1)}, u32[]{:S(2)}, u32[]{:S(2)}) collective-permute-start(f32[128,256]{1,0:T(8,128)S(1)} %pad_maximum_fusion), channel_id=1, source_target_pairs={{0,128},{4,132},{8,136},{12,140},{16,144},{20,148},{24,152},{28,15... | collective-permute-start | bytes 393224 | tf_op jit(solution)/shard_map/ppermute | solution.py:416
  159.9 0.6 constant_dynamic-update-slice_fusion.8
  160.5 0.6 constant_dynamic-update-slice_fusion.7
  161.1 1.4 collective-permute-done.3
  162.5 0.7 constant_dynamic-update-slice_fusion.6
  163.2 0.8 copy-done.5
  164.0 1.2 collective-permute-start.4
  165.2 0.0 all-to-all-done.1.got_ref
  165.3 1.5 shard_map.106
  166.8 10.3 %all-to-all-start.2 = ((s32[64,8,128]{2,1,0:T(8,128)}), s32[64,8,128]{2,1,0:T(8,128)S(1)}, u32[]{:S(2)}, u32[]{:S(2)}) async-start(s32[64,8,128]{2,1,0:T(8,128)} %shard_map.106), calls=%async_computation.2 | async-start | bytes 524288 | tf_op jit(solution)/shard_map/all_to_all | solution.py:34
  177.1 0.0 collective-permute-done.4
  177.1 0.7 constant_dynamic-update-slice_fusion.5
  177.9 0.5 collective-permute-start.5
  178.3 0.0 copy-done.6
  178.3 0.1 reshape.30
  178.4 10.7 %all-to-all-done.2.got_ref = s32[64,8,128]{2,1,0:T(8,128)S(1)} async-done(((s32[64,8,128]{2,1,0:T(8,128)}), s32[64,8,128]{2,1,0:T(8,128)S(1)}, u32[]{:S(2)}, u32[]{:S(2)}) %all-to-all-start.2) | async-done | bytes 262176 | tf_op jit(solution)/shard_map/all_to_all | solution.py:34
  189.1 0.0 copy-done.1
  189.1 0.0 copy-done.3
  189.1 3.7 %shard_map.107 = s32[4,8,4096]{2,1,0:T(8,128)} custom-call(s32[64,8,128]{2,1,0:T(8,128)S(1)} %all-to-all-done.2.got_ref, s32[1,4096]{1,0:T(1,128)S(1)} %bitcast.7, s32[1,4096]{1,0:T(1,128)S(1)} %copy-done.3), custom_call_target="tpu_custom_call" | custom-call | flops 4000000000 | bytes 4194304 | tf_op jit(solution)/shard_map/pallas_call | solution.py:428
  192.7 4.0 %all-to-all-start.3 = ((s32[4,8,4096]{2,1,0:T(8,128)}), s32[4,8,4096]{2,1,0:T(8,128)S(1)}, u32[]{:S(2)}, u32[]{:S(2)}) async-start(s32[4,8,4096]{2,1,0:T(8,128)} %shard_map.107), calls=%async_computation.3 | async-start | bytes 1048576 | tf_op jit(solution)/shard_map/all_to_all | solution.py:34
  196.7 0.6 gather_fusion
  197.3 0.1 reshape.31.cluster_ref
  197.4 0.0 collective-permute-done.5
  197.4 1.1 constant_dynamic-update-slice_fusion.11.rows_ref
  198.5 5.3 %shard_map.105 = f32[1024,256]{1,0:T(8,128)} custom-call(s32[1024]{0:T(1024)S(1)} %reshape.31.cluster_ref, f32[1024,256]{1,0:T(8,128)S(1)} %constant_dynamic-update-slice_fusion.11.rows_ref), custom_call_target="tpu_custom_call" | custom-call | flops 2000000000 | bytes 4194304 | tf_op jit(solution)/shard_map/pallas_call | solution.py:435
  203.8 1.8 all-to-all-done.3.got_ref
  205.6 1.4 shard_map.108
  (10 shorter events, 0.0 us)
Async XLA Ops:
  0.6 25.4 %copy-start = (f32[1024,256]{1,0:T(8,128)S(1)}, f32[1024,256]{1,0:T(8,128)}, u32[]{:S(2)}) copy-start(f32[1024,256]{1,0:T(8,128)} %param.9) | copy-start | bytes 3145732
  12.5 13.5 %copy-start.4 = (s32[1024]{0:T(1024)S(1)}, s32[1024]{0:T(1024)}, u32[]{:S(2)}) copy-start(s32[1024]{0:T(1024)} %param.14) | copy-start | bytes 12292
  12.5 115.0 %copy-start.2 = (f32[16,64,256]{2,1,0:T(8,128)S(1)}, f32[16,64,256]{2,1,0:T(8,128)}, u32[]{:S(2)}) copy-start(f32[16,64,256]{2,1,0:T(8,128)} %param.10) | copy-start | bytes 3145732
  12.5 115.0 %all-to-all-start = ((bf16[64,136,256]{2,1,0:T(8,128)(2,1)}), bf16[64,136,256]{2,1,0:T(8,128)(2,1)}, u32[]{:S(2)}, u32[]{:S(2)}) async-start(bf16[64,136,256]{2,1,0:T(8,128)(2,1)} %bitcast.9), calls=%async_computation | async-start | bytes 8912896 | tf_op jit(solution)/shard_map/all_to_all | solution.py:34
  142.5 6.5 %collective-permute-start = (f32[16,256]{1,0:T(8,128)S(1)}, f32[16,256]{1,0:T(8,128)S(1)}, u32[]{:S(2)}, u32[]{:S(2)}) collective-permute-start(f32[16,256]{1,0:T(8,128)S(1)} %get-tuple-element.9), channel_id=1, source_target_pairs={{0,32},{4,36},{8,40},{12,44},{16,48},{20,52},{24,56},{28,60},{32,0... | collective-permute-start | bytes 49160 | tf_op jit(solution)/shard_map/ppermute | solution.py:416
  144.6 20.7 %all-to-all-start.1 = ((s16[4,1088,128]{2,1,0:T(8,128)(2,1)}), s16[4,1088,128]{2,1,0:T(8,128)(2,1)S(1)}, u32[]{:S(2)}, u32[]{:S(2)}) async-start(s16[4,1088,128]{2,1,0:T(8,128)(2,1)} %get-tuple-element.11), calls=%async_computation.1 | async-start | bytes 2228224 | tf_op jit(solution)/shard_map/all_to_all | solution.py:34
  149.0 3.7 %collective-permute-start.1 = (f32[32,256]{1,0:T(8,128)S(1)}, f32[32,256]{1,0:T(8,128)S(1)}, u32[]{:S(2)}, u32[]{:S(2)}) collective-permute-start(f32[32,256]{1,0:T(8,128)S(1)} %pad_maximum_fusion.2), channel_id=1, source_target_pairs={{0,16},{4,20},{8,24},{12,28},{16,0},{20,4},{24,8},{28,12},{32,48},... | collective-permute-start | bytes 98312 | tf_op jit(solution)/shard_map/ppermute | solution.py:416
  152.7 3.4 %collective-permute-start.2 = (f32[64,256]{1,0:T(8,128)S(1)}, f32[64,256]{1,0:T(8,128)S(1)}, u32[]{:S(2)}, u32[]{:S(2)}) collective-permute-start(f32[64,256]{1,0:T(8,128)S(1)} %pad_maximum_fusion.1), channel_id=1, source_target_pairs={{0,8},{4,12},{8,0},{12,4},{16,24},{20,28},{24,16},{28,20},{32,40},... | collective-permute-start | bytes 196616 | tf_op jit(solution)/shard_map/ppermute | solution.py:416
  156.1 6.5 %collective-permute-start.3 = (f32[128,256]{1,0:T(8,128)S(1)}, f32[128,256]{1,0:T(8,128)S(1)}, u32[]{:S(2)}, u32[]{:S(2)}) collective-permute-start(f32[128,256]{1,0:T(8,128)S(1)} %pad_maximum_fusion), channel_id=1, source_target_pairs={{0,128},{4,132},{8,136},{12,140},{16,144},{20,148},{24,152},{28,15... | collective-permute-start | bytes 393224 | tf_op jit(solution)/shard_map/ppermute | solution.py:416
  163.2 0.8 copy-start.5
  164.0 14.3 %copy-start.6 = (s32[64]{0:T(128)S(1)}, s32[64]{0:T(128)}, u32[]{:S(2)}) copy-start(s32[64]{0:T(128)} %constant.6.clone) | copy-start | bytes 772
  164.0 25.1 %copy-start.1 = (s32[4096,1]{0,1:T(1,128)S(1)}, s32[4096,1]{0,1:T(1,128)}, u32[]{:S(2)}) copy-start(s32[4096,1]{0,1:T(1,128)} %param.11) | copy-start | bytes 49156
  164.0 25.1 %copy-start.3 = (s32[1,4096]{1,0:T(1,128)S(1)}, s32[1,4096]{1,0:T(1,128)}, u32[]{:S(2)}) copy-start(s32[1,4096]{1,0:T(1,128)} %get-tuple-element.12.target_ref) | copy-start | bytes 49156
  164.0 13.1 %collective-permute-start.4 = (f32[256,256]{1,0:T(8,128)}, f32[256,256]{1,0:T(8,128)S(1)}, u32[]{:S(2)}, u32[]{:S(2)}) collective-permute-start(f32[256,256]{1,0:T(8,128)} %get-tuple-element.17), channel_id=1, source_target_pairs={{0,64},{4,68},{8,72},{12,76},{16,80},{20,84},{24,88},{28,92},{32,9... | collective-permute-start | bytes 786440 | tf_op jit(solution)/shard_map/ppermute | solution.py:416
  166.8 22.3 %all-to-all-start.2 = ((s32[64,8,128]{2,1,0:T(8,128)}), s32[64,8,128]{2,1,0:T(8,128)S(1)}, u32[]{:S(2)}, u32[]{:S(2)}) async-start(s32[64,8,128]{2,1,0:T(8,128)} %shard_map.106), calls=%async_computation.2 | async-start | bytes 524288 | tf_op jit(solution)/shard_map/all_to_all | solution.py:34
  177.9 19.6 %collective-permute-start.5 = (f32[512,256]{1,0:T(8,128)}, f32[512,256]{1,0:T(8,128)}, u32[]{:S(2)}, u32[]{:S(2)}) collective-permute-start(f32[512,256]{1,0:T(8,128)} %get-tuple-element.13), channel_id=1, source_target_pairs={{0,4},{4,0},{8,12},{12,8},{16,20},{20,16},{24,28},{28,24},{32,36},... | collective-permute-start | bytes 1572872 | tf_op jit(solution)/shard_map/ppermute | solution.py:416
  192.7 12.8 %all-to-all-start.3 = ((s32[4,8,4096]{2,1,0:T(8,128)}), s32[4,8,4096]{2,1,0:T(8,128)S(1)}, u32[]{:S(2)}, u32[]{:S(2)}) async-start(s32[4,8,4096]{2,1,0:T(8,128)} %shard_map.107), calls=%async_computation.3 | async-start | bytes 1048576 | tf_op jit(solution)/shard_map/all_to_all | solution.py:34

commit v7 on v6

--- a/solution.py
+++ b/solution.py
@@ -336,14 +336,17 @@
 
 
 def arrange_body():
-    def body(cluster_ref, rows_ref, out_ref):
+    def body(cluster_ref, first_ref, second_ref, out_ref):
+        rows = first_ref.shape[0]
+
         def move(index, carry):
             for offset in range(8):
                 row = index * 8 + offset
-                out_ref[pl.ds(cluster_ref[row], 1), :] = rows_ref[pl.ds(row, 1), :]
-            return carry
-
-        lax.fori_loop(0, rows_ref.shape[0] // 8, move, 0)
+                out_ref[pl.ds(cluster_ref[row], 1), :] = first_ref[pl.ds(row, 1), :]
+                out_ref[pl.ds(cluster_ref[row + rows], 1), :] = second_ref[pl.ds(row, 1), :]
+            return carry
+
+        lax.fori_loop(0, rows // 8, move, 0)
 
     return body
 
@@ -411,10 +414,11 @@
         mem=40 << 20,
     )(rows, coarse_init[mine], fine_init.reshape(columns, width))
 
-    gathered = coarse_mine
-    for bit in bits:
+    gathered = other = coarse_mine
+    for hop, bit in enumerate(bits):
+        if hop:
+            gathered = lax.optimization_barrier(jnp.concatenate([gathered, other], axis=0))
         other = lax.ppermute(gathered, "dp", [(i, i ^ bit) for i in range(owners)])
-        gathered = jnp.concatenate([gathered, other], axis=0)
 
     arrived = exchanged(partial, "grp")
     share = call(
@@ -435,9 +439,9 @@
     coarse_out = call(
         arrange_body(),
         shape((owners * slots, width), f32),
-        [SMEM, VMEM],
+        [SMEM, VMEM, VMEM],
         flops=2_000_000_000,
-    )(cluster_at, gathered)
+    )(cluster_at, gathered, other)
     distances = call(
         spread_body(), shape((per_cluster, tokens), f32), [VMEM], flops=10_000_000
     )(codes)

time: 207 us -> 205 us (level)
  waiting for transfers between devices: 119 us -> 126 us
  local copies, waits for them, and re-layouts: 7.13 us -> 1.36 us
  starting transfers between devices: 40.9 us -> 38.3 us
    ppermute x6, waiting for transfers between devices: 6.11 us -> 21 us  [shards(): other = lax.ppermute(gathered, 'dp', [(i, i ^ bit) for i in range(owners)])]
    all_to_all x4, waiting for transfers between devices: 113 us -> 105 us  [exchanged(): return lax.all_to_all(array, axis, split_axis=0, concat_axis=0, tiled=True)]
    unnamed x19 -> x12, local copies, waits for them, and re-layouts: 3.99 us -> 0.03 us
  transfers between devices with their start and end apart: 10 -> 10, of which waited for: 7 -> 7; matrix products, arithmetic and copies ran while one was open for 3% -> 1% of each run, Pallas kernels for 5% -> 5%
where the time goes in v7:
time: 205 us; the launch traced here: 204 us
  waiting for transfers between devices  126 us (61%)
  starting transfers between devices  38.3 us (19%)
  Pallas kernels  37.9 us (18%)
    all_to_all x4, waiting for transfers between devices, exchanged(): return lax.all_to_all(array, axis, split_axis=0, concat_axis=0, tiled=True)  105 us
    all_to_all x4, starting transfers between devices, exchanged(): return lax.all_to_all(array, axis, split_axis=0, concat_axis=0, tiled=True)  30.8 us
    ppermute x6, waiting for transfers between devices, shards(): other = lax.ppermute(gathered, 'dp', [(i, i ^ bit) for i in range(owners)])  21 us
    pallas_call x1, Pallas kernels, shards(): call(update_body(slots, per_cluster), (shape((slots, width), f32), shape(...  15 us
    pallas_call x1, Pallas kernels, shards(): call(send_body(capacity, stride, 4, 32), (shape((1, tokens), i32), shape(...  11.8 us
    ppermute x6, starting transfers between devices, shards(): other = lax.ppermute(gathered, 'dp', [(i, i ^ bit) for i in range(owners)])  7.55 us
    pallas_call x1, Pallas kernels, shards(): call(arrange_body(), shape((owners * slots, width), f32), [SMEM, VMEM, VM...  4.47 us
  transfers between devices with their start and end apart: 10, of which 7 were waited for; matrix products, arithmetic and copies ran while one was open for 1% of the time, Pallas kernels for 5%

profile of v7, /device:TPU:1, one launch (start us, length us, event | category | flops | bytes accessed | tf_op | source)
XLA Modules:
  0.0 204.3 jit_solution(15864347880439669852)
XLA Ops:
  0.6 0.0 copy-start
  0.6 11.8 %shard_map.103 = (s32[1,4096]{1,0:T(1,128)}, bf16[8704,256]{1,0:T(8,128)(2,1)}) custom-call(s32[1,4096]{1,0:T(1,128)} %bitcast.6, s32[1,4096]{1,0:T(1,128)} %bitcast.10, s32[1,4096]{1,0:T(1,128)} %bitcast.11, bf16[4096,256]{1,0:T(8,128)(2,1)} %rows_hbm.1), custom_call_target="tpu_custom_call" | custom-call | flops 400000000 | bytes 4194304 | tf_op jit(solution)/shard_map/pallas_call | solution.py:371
  12.5 0.0 copy-start.4
  12.5 0.0 copy-start.2
  12.5 13.5 %all-to-all-start = ((bf16[64,136,256]{2,1,0:T(8,128)(2,1)}), bf16[64,136,256]{2,1,0:T(8,128)(2,1)}, u32[]{:S(2)}, u32[]{:S(2)}) async-start(bf16[64,136,256]{2,1,0:T(8,128)(2,1)} %bitcast.9), calls=%async_computation | async-start | bytes 8912896 | tf_op jit(solution)/shard_map/all_to_all | solution.py:34
  26.0 0.0 copy-done.4
  26.0 0.1 compare_select_fusion
  26.1 0.0 copy-done
  26.1 0.6 gather_fusion.1
  26.7 100.8 %all-to-all-done.rows_ref = bf16[64,136,256]{2,1,0:T(8,128)(2,1)} async-done(((bf16[64,136,256]{2,1,0:T(8,128)(2,1)}), bf16[64,136,256]{2,1,0:T(8,128)(2,1)}, u32[]{:S(2)}, u32[]{:S(2)}) %all-to-all-start) | async-done | bytes 4456480 | tf_op jit(solution)/shard_map/all_to_all | solution.py:34
  127.5 0.0 copy-done.2
  127.5 15.0 %shard_map.104 = (f32[16,256]{1,0:T(8,128)S(1)}, f32[1024,256]{1,0:T(8,128)}, s16[4,1088,128]{2,1,0:T(8,128)(2,1)}) custom-call(bf16[64,136,256]{2,1,0:T(8,128)(2,1)} %all-to-all-done.rows_ref, f32[16,256]{1,0:T(8,128)S(1)} %gather_fusion.1, f32[1024,256]{1,0:T(8,128)S(1)} %bitcast.8), custom_call_target="tpu_custom_call" | custom-call | flops 8589934592 | bytes 4194304 | tf_op jit(solution)/shard_map/pallas_call | solution.py:395
  142.5 4.0 %all-to-all-start.1 = ((s16[4,1088,128]{2,1,0:T(8,128)(2,1)}), s16[4,1088,128]{2,1,0:T(8,128)(2,1)S(1)}, u32[]{:S(2)}, u32[]{:S(2)}) async-start(s16[4,1088,128]{2,1,0:T(8,128)(2,1)} %get-tuple-element.11), calls=%async_computation.1 | async-start | bytes 2228224 | tf_op jit(solution)/shard_map/all_to_all | solution.py:34
  146.5 2.1 %collective-permute-start = (f32[16,256]{1,0:T(8,128)S(1)}, f32[16,256]{1,0:T(8,128)S(1)}, u32[]{:S(2)}, u32[]{:S(2)}) collective-permute-start(f32[16,256]{1,0:T(8,128)S(1)} %get-tuple-element.9), channel_id=1, source_target_pairs={{0,32},{4,36},{8,40},{12,44},{16,48},{20,52},{24,56},{28,60},{32,0... | collective-permute-start | bytes 49160 | tf_op jit(solution)/shard_map/ppermute | solution.py:421
  148.6 4.4 %collective-permute-done = f32[16,256]{1,0:T(8,128)S(1)} collective-permute-done((f32[16,256]{1,0:T(8,128)S(1)}, f32[16,256]{1,0:T(8,128)S(1)}, u32[]{:S(2)}, u32[]{:S(2)}) %collective-permute-start) | collective-permute-done | bytes 16416 | tf_op jit(solution)/shard_map/ppermute | solution.py:421
  153.0 0.0 collective-permute-start.1
  153.0 4.3 %collective-permute-done.1 = f32[32,256]{1,0:T(8,128)S(1)} collective-permute-done((f32[32,256]{1,0:T(8,128)S(1)}, f32[32,256]{1,0:T(8,128)S(1)}, u32[]{:S(2)}, u32[]{:S(2)}) %collective-permute-start.1) | collective-permute-done | bytes 32800 | tf_op jit(solution)/shard_map/ppermute | solution.py:421
  157.3 0.0 collective-permute-start.2
  157.3 3.4 %collective-permute-done.2 = f32[64,256]{1,0:T(8,128)S(1)} collective-permute-done((f32[64,256]{1,0:T(8,128)S(1)}, f32[64,256]{1,0:T(8,128)S(1)}, u32[]{:S(2)}, u32[]{:S(2)}) %collective-permute-start.2) | collective-permute-done | bytes 65568 | tf_op jit(solution)/shard_map/ppermute | solution.py:421
  160.8 2.9 %collective-permute-start.3 = (f32[128,256]{1,0:T(8,128)S(1)}, f32[128,256]{1,0:T(8,128)S(1)}, u32[]{:S(2)}, u32[]{:S(2)}) collective-permute-start(f32[128,256]{1,0:T(8,128)S(1)} %pad_maximum_fusion.2), channel_id=1, source_target_pairs={{0,128},{4,132},{8,136},{12,140},{16,144},{20,148},{24,152},{28,15... | collective-permute-start | bytes 393224 | tf_op jit(solution)/shard_map/ppermute | solution.py:421
  163.6 0.0 all-to-all-done.1.got_ref
  163.7 1.5 shard_map.106
  165.2 0.0 copy-start.1
  165.2 0.0 copy-start.3
  165.2 8.7 %all-to-all-start.2 = ((s32[64,8,128]{2,1,0:T(8,128)}), s32[64,8,128]{2,1,0:T(8,128)S(1)}, u32[]{:S(2)}, u32[]{:S(2)}) async-start(s32[64,8,128]{2,1,0:T(8,128)} %shard_map.106), calls=%async_computation.2 | async-start | bytes 524288 | tf_op jit(solution)/shard_map/all_to_all | solution.py:34
  173.9 0.0 collective-permute-done.3
  173.9 1.4 collective-permute-start.4
  175.4 8.9 %collective-permute-done.4 = f32[256,256]{1,0:T(8,128)S(1)} collective-permute-done((f32[256,256]{1,0:T(8,128)S(1)}, f32[256,256]{1,0:T(8,128)S(1)}, u32[]{:S(2)}, u32[]{:S(2)}) %collective-permute-start.4) | collective-permute-done | bytes 262176 | tf_op jit(solution)/shard_map/ppermute | solution.py:421
  184.3 1.1 collective-permute-start.5
  185.4 0.4 all-to-all-done.2.got_ref
  185.8 0.0 copy-done.1
  185.8 0.0 copy-done.3
  185.8 0.0 copy-start.5
  185.8 3.6 %shard_map.107 = s32[4,8,4096]{2,1,0:T(8,128)} custom-call(s32[64,8,128]{2,1,0:T(8,128)S(1)} %all-to-all-done.2.got_ref, s32[1,4096]{1,0:T(1,128)S(1)} %bitcast.7, s32[1,4096]{1,0:T(1,128)S(1)} %copy-done.3), custom_call_target="tpu_custom_call" | custom-call | flops 4000000000 | bytes 4194304 | tf_op jit(solution)/shard_map/pallas_call | solution.py:432
  189.5 4.6 %all-to-all-start.3 = ((s32[4,8,4096]{2,1,0:T(8,128)}), s32[4,8,4096]{2,1,0:T(8,128)S(1)}, u32[]{:S(2)}, u32[]{:S(2)}) async-start(s32[4,8,4096]{2,1,0:T(8,128)} %shard_map.107), calls=%async_computation.3 | async-start | bytes 1048576 | tf_op jit(solution)/shard_map/all_to_all | solution.py:34
  194.1 0.0 copy-done.5
  194.1 0.1 reshape.30
  194.2 0.6 gather_fusion
  194.8 0.1 reshape.31.cluster_ref
  194.8 0.0 collective-permute-done.5.second_ref
  194.8 4.5 %shard_map.105 = f32[1024,256]{1,0:T(8,128)} custom-call(s32[1024]{0:T(1024)S(1)} %reshape.31.cluster_ref, f32[512,256]{1,0:T(8,128)S(1)} %pad_maximum_fusion.first_ref, f32[512,256]{1,0:T(8,128)S(1)} %collective-permute-done.5.second_ref), custom_call_target="tpu_custom_call" | custom-call | flops 2000000000 | bytes 4194304 | tf_op jit(solution)/shard_map/pallas_call | solution.py:439
  199.3 3.6 %all-to-all-done.3.got_ref = s32[4,8,4096]{2,1,0:T(8,128)S(1)} async-done(((s32[4,8,4096]{2,1,0:T(8,128)}), s32[4,8,4096]{2,1,0:T(8,128)S(1)}, u32[]{:S(2)}, u32[]{:S(2)}) %all-to-all-start.3) | async-done | bytes 524320 | tf_op jit(solution)/shard_map/all_to_all | solution.py:34
  202.9 1.4 shard_map.108
  (8 shorter events, 0.1 us)
Async XLA Ops:
  0.6 25.5 %copy-start = (f32[1024,256]{1,0:T(8,128)S(1)}, f32[1024,256]{1,0:T(8,128)}, u32[]{:S(2)}) copy-start(f32[1024,256]{1,0:T(8,128)} %param.9) | copy-start | bytes 3145732
  12.5 13.5 %copy-start.4 = (s32[1024]{0:T(1024)S(1)}, s32[1024]{0:T(1024)}, u32[]{:S(2)}) copy-start(s32[1024]{0:T(1024)} %param.14) | copy-start | bytes 12292
  12.5 115.0 %copy-start.2 = (f32[16,64,256]{2,1,0:T(8,128)S(1)}, f32[16,64,256]{2,1,0:T(8,128)}, u32[]{:S(2)}) copy-start(f32[16,64,256]{2,1,0:T(8,128)} %param.10) | copy-start | bytes 3145732
  12.5 115.0 %all-to-all-start = ((bf16[64,136,256]{2,1,0:T(8,128)(2,1)}), bf16[64,136,256]{2,1,0:T(8,128)(2,1)}, u32[]{:S(2)}, u32[]{:S(2)}) async-start(bf16[64,136,256]{2,1,0:T(8,128)(2,1)} %bitcast.9), calls=%async_computation | async-start | bytes 8912896 | tf_op jit(solution)/shard_map/all_to_all | solution.py:34
  142.5 21.1 %all-to-all-start.1 = ((s16[4,1088,128]{2,1,0:T(8,128)(2,1)}), s16[4,1088,128]{2,1,0:T(8,128)(2,1)S(1)}, u32[]{:S(2)}, u32[]{:S(2)}) async-start(s16[4,1088,128]{2,1,0:T(8,128)(2,1)} %get-tuple-element.11), calls=%async_computation.1 | async-start | bytes 2228224 | tf_op jit(solution)/shard_map/all_to_all | solution.py:34
  146.5 6.5 %collective-permute-start = (f32[16,256]{1,0:T(8,128)S(1)}, f32[16,256]{1,0:T(8,128)S(1)}, u32[]{:S(2)}, u32[]{:S(2)}) collective-permute-start(f32[16,256]{1,0:T(8,128)S(1)} %get-tuple-element.9), channel_id=1, source_target_pairs={{0,32},{4,36},{8,40},{12,44},{16,48},{20,52},{24,56},{28,60},{32,0... | collective-permute-start | bytes 49160 | tf_op jit(solution)/shard_map/ppermute | solution.py:421
  153.0 4.3 %collective-permute-start.1 = (f32[32,256]{1,0:T(8,128)S(1)}, f32[32,256]{1,0:T(8,128)S(1)}, u32[]{:S(2)}, u32[]{:S(2)}) collective-permute-start(f32[32,256]{1,0:T(8,128)S(1)} %pad_maximum_fusion.4), channel_id=1, source_target_pairs={{0,16},{4,20},{8,24},{12,28},{16,0},{20,4},{24,8},{28,12},{32,48},... | collective-permute-start | bytes 98312 | tf_op jit(solution)/shard_map/ppermute | solution.py:421
  157.3 3.4 %collective-permute-start.2 = (f32[64,256]{1,0:T(8,128)S(1)}, f32[64,256]{1,0:T(8,128)S(1)}, u32[]{:S(2)}, u32[]{:S(2)}) collective-permute-start(f32[64,256]{1,0:T(8,128)S(1)} %pad_maximum_fusion.3), channel_id=1, source_target_pairs={{0,8},{4,12},{8,0},{12,4},{16,24},{20,28},{24,16},{28,20},{32,40},... | collective-permute-start | bytes 196616 | tf_op jit(solution)/shard_map/ppermute | solution.py:421
  160.8 13.1 %collective-permute-start.3 = (f32[128,256]{1,0:T(8,128)S(1)}, f32[128,256]{1,0:T(8,128)S(1)}, u32[]{:S(2)}, u32[]{:S(2)}) collective-permute-start(f32[128,256]{1,0:T(8,128)S(1)} %pad_maximum_fusion.2), channel_id=1, source_target_pairs={{0,128},{4,132},{8,136},{12,140},{16,144},{20,148},{24,152},{28,15... | collective-permute-start | bytes 393224 | tf_op jit(solution)/shard_map/ppermute | solution.py:421
  165.2 20.7 %copy-start.1 = (s32[4096,1]{0,1:T(1,128)S(1)}, s32[4096,1]{0,1:T(1,128)}, u32[]{:S(2)}) copy-start(s32[4096,1]{0,1:T(1,128)} %param.11) | copy-start | bytes 49156
  165.2 20.7 %copy-start.3 = (s32[1,4096]{1,0:T(1,128)S(1)}, s32[1,4096]{1,0:T(1,128)}, u32[]{:S(2)}) copy-start(s32[1,4096]{1,0:T(1,128)} %get-tuple-element.12.target_ref) | copy-start | bytes 49156
  165.2 20.7 %all-to-all-start.2 = ((s32[64,8,128]{2,1,0:T(8,128)}), s32[64,8,128]{2,1,0:T(8,128)S(1)}, u32[]{:S(2)}, u32[]{:S(2)}) async-start(s32[64,8,128]{2,1,0:T(8,128)} %shard_map.106), calls=%async_computation.2 | async-start | bytes 524288 | tf_op jit(solution)/shard_map/all_to_all | solution.py:34
  173.9 10.3 %collective-permute-start.4 = (f32[256,256]{1,0:T(8,128)S(1)}, f32[256,256]{1,0:T(8,128)S(1)}, u32[]{:S(2)}, u32[]{:S(2)}) collective-permute-start(f32[256,256]{1,0:T(8,128)S(1)} %pad_maximum_fusion.1), channel_id=1, source_target_pairs={{0,64},{4,68},{8,72},{12,76},{16,80},{20,84},{24,88},{28,92},{32,9... | collective-permute-start | bytes 786440 | tf_op jit(solution)/shard_map/ppermute | solution.py:421
  184.3 10.6 %collective-permute-start.5 = (f32[512,256]{1,0:T(8,128)S(1)}, f32[512,256]{1,0:T(8,128)S(1)}, u32[]{:S(2)}, u32[]{:S(2)}) collective-permute-start(f32[512,256]{1,0:T(8,128)S(1)} %pad_maximum_fusion.first_ref), channel_id=1, source_target_pairs={{0,4},{4,0},{8,12},{12,8},{16,20},{20,16},{24,28},{28,24},{32,36},... | collective-permute-start | bytes 1572872 | tf_op jit(solution)/shard_map/ppermute | solution.py:421
  185.8 8.2 %copy-start.5 = (s32[64]{0:T(128)S(1)}, s32[64]{0:T(128)}, u32[]{:S(2)}) copy-start(s32[64]{0:T(128)} %constant.6.clone) | copy-start | bytes 772
  189.5 13.4 %all-to-all-start.3 = ((s32[4,8,4096]{2,1,0:T(8,128)}), s32[4,8,4096]{2,1,0:T(8,128)S(1)}, u32[]{:S(2)}, u32[]{:S(2)}) async-start(s32[4,8,4096]{2,1,0:T(8,128)} %shard_map.107), calls=%async_computation.3 | async-start | bytes 1048576 | tf_op jit(solution)/shard_map/all_to_all | solution.py:34

commit v8 on v7

--- a/solution.py
+++ b/solution.py
@@ -172,7 +172,7 @@
             square_out[here, :] = (meta[1:2, :LANES] + meta[1:2, LANES:]) + meta[2:3, :LANES]
             return carry
 
-        lax.fori_loop(0, blocks, read, 0, unroll=4)
+        lax.fori_loop(0, blocks, read, 0, unroll=8)
 
         ids = iota((columns, LANES), 0).astype(jnp.int16)
         one, zero = jnp.bfloat16(1.0), jnp.bfloat16(0.0)
@@ -318,7 +318,7 @@
                 out_ref[copy, :, here] = value
             return carry
 
-        lax.fori_loop(0, groups, one, 0, unroll=4)
+        lax.fori_loop(0, groups, one, 0, unroll=8)
 
     return body
 
@@ -369,7 +369,7 @@
     owner = owner_of.reshape(1, tokens)
     slot, part = slot_in_owner.reshape(1, tokens), fine_in_cluster.reshape(1, tokens)
     target, send_rows = call(
-        send_body(capacity, stride, 4, 32),
+        send_body(capacity, stride, 4, 64),
         (shape((1, tokens), i32), shape((owners * stride, width), bf16)),
         [VMEM, VMEM, VMEM, HBM],
         flops=400_000_000,

time: 205 us -> 204 us (level)
  no operation moved by 1% of the time
where the time goes in v8:
time: 204 us
  waiting for transfers between devices  125 us (61%)
  starting transfers between devices  39.2 us (19%)
  Pallas kernels  37.4 us (18%)
    all_to_all x4, waiting for transfers between devices, exchanged(): return lax.all_to_all(array, axis, split_axis=0, concat_axis=0, tiled=True)  105 us
    all_to_all x4, starting transfers between devices, exchanged(): return lax.all_to_all(array, axis, split_axis=0, concat_axis=0, tiled=True)  30.7 us
    ppermute x6, waiting for transfers between devices, shards(): other = lax.ppermute(gathered, 'dp', [(i, i ^ bit) for i in range(owners)])  20.1 us
    pallas_call x1, Pallas kernels, shards(): call(update_body(slots, per_cluster), (shape((slots, width), f32), shape(...  15 us
    pallas_call x1, Pallas kernels, shards(): call(send_body(capacity, stride, 4, 64), (shape((1, tokens), i32), shape(...  11.7 us
    ppermute x6, starting transfers between devices, shards(): other = lax.ppermute(gathered, 'dp', [(i, i ^ bit) for i in range(owners)])  8.48 us
    pallas_call x1, Pallas kernels, shards(): call(arrange_body(), shape((owners * slots, width), f32), [SMEM, VMEM, VM...  4.47 us
  transfers between devices with their start and end apart: 10, of which 7 were waited for; matrix products, arithmetic and copies ran while one was open for 1% of the time, Pallas kernels for 5%

profile of v8, /device:TPU:1, one launch (start us, length us, event | category | flops | bytes accessed | tf_op | source)
XLA Modules:
  0.0 203.9 jit_solution(3986214324949717757)
XLA Ops:
  0.6 0.0 copy-start
  0.6 11.7 %shard_map.103 = (s32[1,4096]{1,0:T(1,128)}, bf16[8704,256]{1,0:T(8,128)(2,1)}) custom-call(s32[1,4096]{1,0:T(1,128)} %bitcast.6, s32[1,4096]{1,0:T(1,128)} %bitcast.10, s32[1,4096]{1,0:T(1,128)} %bitcast.11, bf16[4096,256]{1,0:T(8,128)(2,1)} %rows_hbm.1), custom_call_target="tpu_custom_call" | custom-call | flops 400000000 | bytes 4194304 | tf_op jit(solution)/shard_map/pallas_call | solution.py:371
  12.4 0.0 copy-start.4
  12.4 0.0 copy-start.2
  12.4 13.5 %all-to-all-start = ((bf16[64,136,256]{2,1,0:T(8,128)(2,1)}), bf16[64,136,256]{2,1,0:T(8,128)(2,1)}, u32[]{:S(2)}, u32[]{:S(2)}) async-start(bf16[64,136,256]{2,1,0:T(8,128)(2,1)} %bitcast.9), calls=%async_computation | async-start | bytes 8912896 | tf_op jit(solution)/shard_map/all_to_all | solution.py:34
  25.9 0.0 copy-done.4
  25.9 0.1 compare_select_fusion
  26.0 0.0 copy-done
  26.0 0.6 gather_fusion.1
  26.6 100.8 %all-to-all-done.rows_ref = bf16[64,136,256]{2,1,0:T(8,128)(2,1)} async-done(((bf16[64,136,256]{2,1,0:T(8,128)(2,1)}), bf16[64,136,256]{2,1,0:T(8,128)(2,1)}, u32[]{:S(2)}, u32[]{:S(2)}) %all-to-all-start) | async-done | bytes 4456480 | tf_op jit(solution)/shard_map/all_to_all | solution.py:34
  127.4 0.0 copy-done.2
  127.4 15.0 %shard_map.104 = (f32[16,256]{1,0:T(8,128)S(1)}, f32[1024,256]{1,0:T(8,128)}, s16[4,1088,128]{2,1,0:T(8,128)(2,1)}) custom-call(bf16[64,136,256]{2,1,0:T(8,128)(2,1)} %all-to-all-done.rows_ref, f32[16,256]{1,0:T(8,128)S(1)} %gather_fusion.1, f32[1024,256]{1,0:T(8,128)S(1)} %bitcast.8), custom_call_target="tpu_custom_call" | custom-call | flops 8589934592 | bytes 4194304 | tf_op jit(solution)/shard_map/pallas_call | solution.py:395
  142.4 4.0 %all-to-all-start.1 = ((s16[4,1088,128]{2,1,0:T(8,128)(2,1)}), s16[4,1088,128]{2,1,0:T(8,128)(2,1)S(1)}, u32[]{:S(2)}, u32[]{:S(2)}) async-start(s16[4,1088,128]{2,1,0:T(8,128)(2,1)} %get-tuple-element.11), calls=%async_computation.1 | async-start | bytes 2228224 | tf_op jit(solution)/shard_map/all_to_all | solution.py:34
  146.4 2.1 %collective-permute-start = (f32[16,256]{1,0:T(8,128)S(1)}, f32[16,256]{1,0:T(8,128)S(1)}, u32[]{:S(2)}, u32[]{:S(2)}) collective-permute-start(f32[16,256]{1,0:T(8,128)S(1)} %get-tuple-element.9), channel_id=1, source_target_pairs={{0,32},{4,36},{8,40},{12,44},{16,48},{20,52},{24,56},{28,60},{32,0... | collective-permute-start | bytes 49160 | tf_op jit(solution)/shard_map/ppermute | solution.py:421
  148.5 4.4 %collective-permute-done = f32[16,256]{1,0:T(8,128)S(1)} collective-permute-done((f32[16,256]{1,0:T(8,128)S(1)}, f32[16,256]{1,0:T(8,128)S(1)}, u32[]{:S(2)}, u32[]{:S(2)}) %collective-permute-start) | collective-permute-done | bytes 16416 | tf_op jit(solution)/shard_map/ppermute | solution.py:421
  152.9 0.0 collective-permute-start.1
  152.9 4.0 %collective-permute-done.1 = f32[32,256]{1,0:T(8,128)S(1)} collective-permute-done((f32[32,256]{1,0:T(8,128)S(1)}, f32[32,256]{1,0:T(8,128)S(1)}, u32[]{:S(2)}, u32[]{:S(2)}) %collective-permute-start.1) | collective-permute-done | bytes 32800 | tf_op jit(solution)/shard_map/ppermute | solution.py:421
  156.8 0.6 collective-permute-start.2
  157.4 2.8 %collective-permute-done.2 = f32[64,256]{1,0:T(8,128)S(1)} collective-permute-done((f32[64,256]{1,0:T(8,128)S(1)}, f32[64,256]{1,0:T(8,128)S(1)}, u32[]{:S(2)}, u32[]{:S(2)}) %collective-permute-start.2) | collective-permute-done | bytes 65568 | tf_op jit(solution)/shard_map/ppermute | solution.py:421
  160.3 3.2 %collective-permute-start.3 = (f32[128,256]{1,0:T(8,128)S(1)}, f32[128,256]{1,0:T(8,128)S(1)}, u32[]{:S(2)}, u32[]{:S(2)}) collective-permute-start(f32[128,256]{1,0:T(8,128)S(1)} %pad_maximum_fusion.2), channel_id=1, source_target_pairs={{0,128},{4,132},{8,136},{12,140},{16,144},{20,148},{24,152},{28,15... | collective-permute-start | bytes 393224 | tf_op jit(solution)/shard_map/ppermute | solution.py:421
  163.5 0.0 all-to-all-done.1.got_ref
  163.5 1.5 shard_map.106
  165.0 0.0 copy-start.1
  165.0 0.0 copy-start.3
  165.0 8.7 %all-to-all-start.2 = ((s32[64,8,128]{2,1,0:T(8,128)}), s32[64,8,128]{2,1,0:T(8,128)S(1)}, u32[]{:S(2)}, u32[]{:S(2)}) async-start(s32[64,8,128]{2,1,0:T(8,128)} %shard_map.106), calls=%async_computation.2 | async-start | bytes 524288 | tf_op jit(solution)/shard_map/all_to_all | solution.py:34
  173.7 0.0 collective-permute-done.3
  173.8 1.4 collective-permute-start.4
  175.2 8.9 %collective-permute-done.4 = f32[256,256]{1,0:T(8,128)S(1)} collective-permute-done((f32[256,256]{1,0:T(8,128)S(1)}, f32[256,256]{1,0:T(8,128)S(1)}, u32[]{:S(2)}, u32[]{:S(2)}) %collective-permute-start.4) | collective-permute-done | bytes 262176 | tf_op jit(solution)/shard_map/ppermute | solution.py:421
  184.1 1.1 collective-permute-start.5
  185.3 0.4 all-to-all-done.2.got_ref
  185.7 0.0 copy-done.1
  185.7 0.0 copy-done.3
  185.7 0.0 copy-start.5
  185.7 3.3 %shard_map.107 = s32[4,8,4096]{2,1,0:T(8,128)} custom-call(s32[64,8,128]{2,1,0:T(8,128)S(1)} %all-to-all-done.2.got_ref, s32[1,4096]{1,0:T(1,128)S(1)} %bitcast.7, s32[1,4096]{1,0:T(1,128)S(1)} %copy-done.3), custom_call_target="tpu_custom_call" | custom-call | flops 4000000000 | bytes 4194304 | tf_op jit(solution)/shard_map/pallas_call | solution.py:432
  189.0 4.6 %all-to-all-start.3 = ((s32[4,8,4096]{2,1,0:T(8,128)}), s32[4,8,4096]{2,1,0:T(8,128)S(1)}, u32[]{:S(2)}, u32[]{:S(2)}) async-start(s32[4,8,4096]{2,1,0:T(8,128)} %shard_map.107), calls=%async_computation.3 | async-start | bytes 1048576 | tf_op jit(solution)/shard_map/all_to_all | solution.py:34
  193.6 0.0 copy-done.5
  193.6 0.1 reshape.30
  193.7 0.6 gather_fusion
  194.3 0.1 reshape.31.cluster_ref
  194.4 0.0 collective-permute-done.5.second_ref
  194.4 4.5 %shard_map.105 = f32[1024,256]{1,0:T(8,128)} custom-call(s32[1024]{0:T(1024)S(1)} %reshape.31.cluster_ref, f32[512,256]{1,0:T(8,128)S(1)} %pad_maximum_fusion.first_ref, f32[512,256]{1,0:T(8,128)S(1)} %collective-permute-done.5.second_ref), custom_call_target="tpu_custom_call" | custom-call | flops 2000000000 | bytes 4194304 | tf_op jit(solution)/shard_map/pallas_call | solution.py:439
  198.9 3.6 %all-to-all-done.3.got_ref = s32[4,8,4096]{2,1,0:T(8,128)S(1)} async-done(((s32[4,8,4096]{2,1,0:T(8,128)}), s32[4,8,4096]{2,1,0:T(8,128)S(1)}, u32[]{:S(2)}, u32[]{:S(2)}) %all-to-all-start.3) | async-done | bytes 524320 | tf_op jit(solution)/shard_map/all_to_all | solution.py:34
  202.5 1.4 shard_map.108
  (8 shorter events, 0.1 us)
Async XLA Ops:
  0.6 25.4 %copy-start = (f32[1024,256]{1,0:T(8,128)S(1)}, f32[1024,256]{1,0:T(8,128)}, u32[]{:S(2)}) copy-start(f32[1024,256]{1,0:T(8,128)} %param.9) | copy-start | bytes 3145732
  12.4 13.5 %copy-start.4 = (s32[1024]{0:T(1024)S(1)}, s32[1024]{0:T(1024)}, u32[]{:S(2)}) copy-start(s32[1024]{0:T(1024)} %param.14) | copy-start | bytes 12292
  12.4 115.0 %copy-start.2 = (f32[16,64,256]{2,1,0:T(8,128)S(1)}, f32[16,64,256]{2,1,0:T(8,128)}, u32[]{:S(2)}) copy-start(f32[16,64,256]{2,1,0:T(8,128)} %param.10) | copy-start | bytes 3145732
  12.4 115.0 %all-to-all-start = ((bf16[64,136,256]{2,1,0:T(8,128)(2,1)}), bf16[64,136,256]{2,1,0:T(8,128)(2,1)}, u32[]{:S(2)}, u32[]{:S(2)}) async-start(bf16[64,136,256]{2,1,0:T(8,128)(2,1)} %bitcast.9), calls=%async_computation | async-start | bytes 8912896 | tf_op jit(solution)/shard_map/all_to_all | solution.py:34
  142.4 21.1 %all-to-all-start.1 = ((s16[4,1088,128]{2,1,0:T(8,128)(2,1)}), s16[4,1088,128]{2,1,0:T(8,128)(2,1)S(1)}, u32[]{:S(2)}, u32[]{:S(2)}) async-start(s16[4,1088,128]{2,1,0:T(8,128)(2,1)} %get-tuple-element.11), calls=%async_computation.1 | async-start | bytes 2228224 | tf_op jit(solution)/shard_map/all_to_all | solution.py:34
  146.4 6.5 %collective-permute-start = (f32[16,256]{1,0:T(8,128)S(1)}, f32[16,256]{1,0:T(8,128)S(1)}, u32[]{:S(2)}, u32[]{:S(2)}) collective-permute-start(f32[16,256]{1,0:T(8,128)S(1)} %get-tuple-element.9), channel_id=1, source_target_pairs={{0,32},{4,36},{8,40},{12,44},{16,48},{20,52},{24,56},{28,60},{32,0... | collective-permute-start | bytes 49160 | tf_op jit(solution)/shard_map/ppermute | solution.py:421
  152.9 4.0 %collective-permute-start.1 = (f32[32,256]{1,0:T(8,128)S(1)}, f32[32,256]{1,0:T(8,128)S(1)}, u32[]{:S(2)}, u32[]{:S(2)}) collective-permute-start(f32[32,256]{1,0:T(8,128)S(1)} %pad_maximum_fusion.4), channel_id=1, source_target_pairs={{0,16},{4,20},{8,24},{12,28},{16,0},{20,4},{24,8},{28,12},{32,48},... | collective-permute-start | bytes 98312 | tf_op jit(solution)/shard_map/ppermute | solution.py:421
  156.8 3.4 %collective-permute-start.2 = (f32[64,256]{1,0:T(8,128)S(1)}, f32[64,256]{1,0:T(8,128)S(1)}, u32[]{:S(2)}, u32[]{:S(2)}) collective-permute-start(f32[64,256]{1,0:T(8,128)S(1)} %pad_maximum_fusion.3), channel_id=1, source_target_pairs={{0,8},{4,12},{8,0},{12,4},{16,24},{20,28},{24,16},{28,20},{32,40},... | collective-permute-start | bytes 196616 | tf_op jit(solution)/shard_map/ppermute | solution.py:421
  160.3 13.5 %collective-permute-start.3 = (f32[128,256]{1,0:T(8,128)S(1)}, f32[128,256]{1,0:T(8,128)S(1)}, u32[]{:S(2)}, u32[]{:S(2)}) collective-permute-start(f32[128,256]{1,0:T(8,128)S(1)} %pad_maximum_fusion.2), channel_id=1, source_target_pairs={{0,128},{4,132},{8,136},{12,140},{16,144},{20,148},{24,152},{28,15... | collective-permute-start | bytes 393224 | tf_op jit(solution)/shard_map/ppermute | solution.py:421
  165.0 20.7 %copy-start.1 = (s32[4096,1]{0,1:T(1,128)S(1)}, s32[4096,1]{0,1:T(1,128)}, u32[]{:S(2)}) copy-start(s32[4096,1]{0,1:T(1,128)} %param.11) | copy-start | bytes 49156
  165.0 20.7 %copy-start.3 = (s32[1,4096]{1,0:T(1,128)S(1)}, s32[1,4096]{1,0:T(1,128)}, u32[]{:S(2)}) copy-start(s32[1,4096]{1,0:T(1,128)} %get-tuple-element.12.target_ref) | copy-start | bytes 49156
  165.0 20.7 %all-to-all-start.2 = ((s32[64,8,128]{2,1,0:T(8,128)}), s32[64,8,128]{2,1,0:T(8,128)S(1)}, u32[]{:S(2)}, u32[]{:S(2)}) async-start(s32[64,8,128]{2,1,0:T(8,128)} %shard_map.106), calls=%async_computation.2 | async-start | bytes 524288 | tf_op jit(solution)/shard_map/all_to_all | solution.py:34
  173.8 10.3 %collective-permute-start.4 = (f32[256,256]{1,0:T(8,128)S(1)}, f32[256,256]{1,0:T(8,128)S(1)}, u32[]{:S(2)}, u32[]{:S(2)}) collective-permute-start(f32[256,256]{1,0:T(8,128)S(1)} %pad_maximum_fusion.1), channel_id=1, source_target_pairs={{0,64},{4,68},{8,72},{12,76},{16,80},{20,84},{24,88},{28,92},{32,9... | collective-permute-start | bytes 786440 | tf_op jit(solution)/shard_map/ppermute | solution.py:421
  184.1 10.3 %collective-permute-start.5 = (f32[512,256]{1,0:T(8,128)S(1)}, f32[512,256]{1,0:T(8,128)S(1)}, u32[]{:S(2)}, u32[]{:S(2)}) collective-permute-start(f32[512,256]{1,0:T(8,128)S(1)} %pad_maximum_fusion.first_ref), channel_id=1, source_target_pairs={{0,4},{4,0},{8,12},{12,8},{16,20},{20,16},{24,28},{28,24},{32,36},... | collective-permute-start | bytes 1572872 | tf_op jit(solution)/shard_map/ppermute | solution.py:421
  185.7 7.9 %copy-start.5 = (s32[64]{0:T(128)S(1)}, s32[64]{0:T(128)}, u32[]{:S(2)}) copy-start(s32[64]{0:T(128)} %constant.6.clone) | copy-start | bytes 772
  189.0 13.4 %all-to-all-start.3 = ((s32[4,8,4096]{2,1,0:T(8,128)}), s32[4,8,4096]{2,1,0:T(8,128)S(1)}, u32[]{:S(2)}, u32[]{:S(2)}) async-start(s32[4,8,4096]{2,1,0:T(8,128)} %shard_map.107), calls=%async_computation.3 | async-start | bytes 1048576 | tf_op jit(solution)/shard_map/all_to_all | solution.py:34
